TPU v7x, 32 devices: a whole 2x2x4 slice. The times are simulated.
32 devices in a mesh: dp: 4 (over x, core), mp: 8 (over z, y).
Axes of the slice: x: 2, y: 2, z: 4, core: 2. Of those that a mesh axis runs over, the one named last changes fastest.
Arguments:
- tokens: bfloat16 [3072, 6144], P('dp'), may hold values from -60 to 60
- ln_gain: float32 [6144], replicated, may hold values from 0.1 to 1.9
- w_qkv: bfloat16 [6144, 3, 6144], P('dp', None, 'mp'), may hold values from -1 to 1
- q_gain: float32 [128], replicated, may hold values from 0.7 to 2
- k_gain: float32 [128], replicated, may hold values from 0.7 to 2
Outputs:
- context: bfloat16 [3072, 6144], P('dp', 'mp')
All inputs are finite; a program needn't handle non-finite values.
Results may differ from a plain program's by a relative error of at most 0.012.
The roundings to bfloat16 on the way count: a program that leaves them out, or rounds other values in their place, can miss the bound.
Values may be sent and summed in bfloat16 or wider, within the bound.
No kernel may reach another device: no remote copies, remote signals or barrier semaphores. Data moves between devices by JAX's collectives and lax.ppermute only.
A program may use at most 128 MiB of HBM per device.

v0:
```python
import jax
import jax.numpy as jnp
from jax import lax
from jax.sharding import PartitionSpec as P

HEADS = 48
HEAD_DIM = 128
PATCHES = 256
SPLITS = 4


norm_eps = 1e-06


def from_behind(shard, axis, by):
    length = lax.axis_size(axis)
    return lax.ppermute(shard, axis, [(i, (i + by) % length) for i in range(length)])


def layer_norm(values, gain_vector):
    centre = jnp.mean(values, axis=-1, keepdims=True)
    centred = values - centre
    spread = jnp.mean(centred * centred, axis=-1, keepdims=True)
    return centred * lax.rsqrt(spread + norm_eps) * gain_vector


def head_norm(pieces, gain_rows):
    values = pieces.astype(jnp.float32)
    centre = jnp.mean(values, axis=(0, 4), keepdims=True)
    centred = values - centre
    spread = jnp.mean(centred * centred, axis=(0, 4), keepdims=True)
    return centred * lax.rsqrt(spread + norm_eps) * gain_rows[:, None, None, None, :]


def ordered_gains(gain_vector, quarter_order):
    gain_table = gain_vector.reshape(SPLITS, -1)
    selector = (quarter_order[:, None] == jnp.arange(SPLITS, dtype=jnp.int32)[None, :]).astype(
        jnp.float32
    )
    return jnp.dot(selector, gain_table, precision=lax.Precision.HIGHEST)


def body(tokens, ln_gain, w_qkv, q_gain, k_gain):
    local_rows = tokens.shape[0]
    normed = layer_norm(tokens.astype(jnp.float32), ln_gain).astype(jnp.bfloat16)
    flat_weight = w_qkv.reshape(w_qkv.shape[0], -1)
    out_width = flat_weight.shape[1]
    row_piece = lax.all_gather(w_qkv, "dp", axis=0, tiled=True)
    partial_value = jnp.dot(
        normed, row_piece.reshape(row_piece.shape[0], out_width), preferred_element_type=jnp.float32
    )
    projected = partial_value.astype(jnp.bfloat16)
    groups = lax.axis_size("mp") // SPLITS
    head_count = HEADS // groups
    quarter_rows = PATCHES // SPLITS
    my_quarter = lax.axis_index("mp") // groups
    images = local_rows // PATCHES
    head_view = projected.reshape(images, PATCHES, 3, head_count, HEAD_DIM // SPLITS)
    queries = head_view[:, :, 0]
    keys_vals = head_view[:, :, 1:]
    counting = jnp.arange(SPLITS, dtype=jnp.int32)
    own_rows = lax.dynamic_slice_in_dim(queries, my_quarter * quarter_rows, quarter_rows, 1)
    query_list = [own_rows]
    pair_list = [keys_vals]
    for offset in range(1, SPLITS):
        outgoing = lax.dynamic_slice_in_dim(
            queries, (my_quarter + offset) % SPLITS * quarter_rows, quarter_rows, 1
        )
        got_query, got_pair = from_behind((outgoing, keys_vals), "mp", offset * groups)
        query_list.append(got_query)
        pair_list.append(got_pair)
    query_pieces = jnp.stack(query_list, 0)
    pair_pieces = jnp.stack(pair_list, 0)
    quarter_order = (my_quarter - counting) % SPLITS
    query_normed = (
        head_norm(query_pieces, ordered_gains(q_gain, quarter_order)) * HEAD_DIM ** (-0.5)
    ).astype(jnp.bfloat16)
    key_normed = head_norm(pair_pieces[:, :, :, 0], ordered_gains(k_gain, quarter_order)).astype(
        jnp.bfloat16
    )
    value_part = pair_pieces[:, :, :, 1]
    scores = jnp.einsum(
        "sirhe,sikhe->ihrk", query_normed, key_normed, preferred_element_type=jnp.float32
    )
    raised = jnp.exp(scores)
    weights = (raised / jnp.sum(raised, axis=-1, keepdims=True)).astype(jnp.bfloat16)
    context = jnp.einsum(
        "ihrk,sikhe->sirhe", weights, value_part, preferred_element_type=jnp.float32
    ).astype(jnp.bfloat16)
    rows_list = [context[0]]
    for offset in range(1, SPLITS):
        wanted = (my_quarter - offset) % SPLITS
        slot_index = jnp.sum(jnp.where(quarter_order == wanted, counting, 0))
        outgoing = lax.dynamic_index_in_dim(context, slot_index, 0, keepdims=False)
        rows_list.append(from_behind(outgoing, "mp", (SPLITS - offset) * groups))
    own_block = jnp.roll(jnp.concatenate(rows_list, 1), my_quarter * quarter_rows, axis=1)
    return own_block.reshape(local_rows, -1)


def solution(mesh):
    return jax.shard_map(
        body,
        mesh=mesh,
        in_specs=(P("dp", None), P(), P("dp", None, "mp"), P(), P()),
        out_specs=P("dp", "mp"),
        check_vma=False,
    )
```

profile of v0, /device:TPU:0, one launch (start us, length us, event | category | flops | bytes accessed | tf_op | source)
XLA Modules:
  0.0 591.0 jit_solution(13350601865086748374)
XLA Ops:
  6.5 10.3 %copy.28 = bf16[1536,3,768]{0,2,1:T(8,128)(2,1)} copy(bf16[1536,3,768]{2,0,1:T(8,128)(2,1)} %param.7) | data formatting | bytes 14155776 | tf_op args[2]
  16.9 5.2 convert_reduce_fusion
  22.0 1.2 copy-done
  23.2 2.6 fusion.2
  25.8 166.1 %all-gather.2.cloned.1.call-done = bf16[6144,3,768]{0,2,1:T(8,128)(2,1)} async-done(((bf16[1536,3,768]{0,2,1:T(8,128)(2,1)}), bf16[6144,3,768]{0,2,1:T(8,128)(2,1)}) %all-gather.2.cloned.1.call-update) | async-done | bytes 28311568 | tf_op jit(solution)/shard_map/all_gather | solution.py:48
  191.9 31.3 %fusion.18 = bf16[768,2304]{1,0:T(8,128)(2,1)} fusion(bf16[6144,2304]{0,1:T(8,128)(2,1)} %bitcast.100, bf16[768,6144]{1,0:T(8,128)(2,1)} %param.5, f32[6144]{0:T(1024)S(1)} %copy-done.4, f32[768]{0:T(1024)S(1)} %add_rsqrt_fusion.2, f32[768]{0:T(1024)S(1)} %broadcast_multiply_fusion.2), kind=kOutput, calls=%fused_computation.24 | convolution fusion | flops 21768634368 | bytes 41318400 | tf_op jit(solution)/shard_map/dot_general | solution.py:49
  223.2 5.8 copy.29
  228.9 8.7 %reshape.77 = bf16[3,256,3,24,32]{1,0,4,3,2:T(4,128)(2,1)} reshape(bf16[768,2304]{0,1:T(8,128)(2,1)} %copy.29) | data formatting | bytes 7077888 | tf_op jit(solution)/shard_map/reshape | solution.py:58
  237.7 4.0 slice.20
  241.7 1.9 copy.49
  243.6 3.3 collective-permute-start.2
  247.0 1.1 collective-permute-start
  248.1 1.4 slice-done
  249.5 3.2 constant_dynamic-slice_fusion.4
  252.6 0.9 copy.72
  253.6 2.7 collective-permute-start.5
  256.4 2.0 copy.73
  258.4 1.1 collective-permute-start.4
  259.6 2.1 copy.74
  261.6 151.2 %collective-permute-done.5 = bf16[3,64,24,32]{1,3,2,0:T(8,128)(2,1)} collective-permute-done((bf16[3,64,24,32]{1,3,2,0:T(8,128)(2,1)}, bf16[3,64,24,32]{1,3,2,0:T(8,128)(2,1)}, u32[]{:S(2)}, u32[]{:S(2)}) %collective-permute-start.5) | collective-permute-done | bytes 294944 | tf_op jit(solution)/shard_map/ppermute | solution.py:17
  412.8 76.3 %collective-permute-start.3 = (bf16[3,64,24,32]{1,3,2,0:T(8,128)(2,1)}, bf16[3,64,24,32]{1,3,2,0:T(8,128)(2,1)}, u32[]{:S(2)}, u32[]{:S(2)}) collective-permute-start(bf16[3,64,24,32]{1,3,2,0:T(8,128)(2,1)} %bitcast.90), channel_id=1, source_target_pairs={{0,2},{1,3},{2,4},{3,5},{4,6},{5,7},{6,0},{7,1},{8,10},{9,11},{10,... | collective-permute-start | bytes 884744 | tf_op jit(solution)/shard_map/ppermute | solution.py:17
  489.3 0.7 fusion.38
  492.5 0.7 fusion.40
  496.8 0.5 copy.77
  497.3 0.4 copy-done.1
  497.8 2.7 collective-permute-done.4
  500.5 0.4 collective-permute-done.3
  500.9 2.1 convert_reduce_fusion.2
  503.0 2.2 fusion.21
  505.2 4.2 pad_maximum_fusion
  509.4 1.4 convert_reduce_fusion.1
  510.8 2.1 fusion.8
  513.0 4.0 fusion.26
  517.1 0.7 fusion.28
  517.8 2.0 fusion.31
  519.8 0.5 copy.76
  520.3 1.3 dynamic-slice_bitcast_fusion.1
  521.6 3.2 collective-permute-start.6
  524.8 0.7 collective-permute-start.7
  525.5 0.9 dynamic-slice_bitcast_fusion
  526.4 0.5 collective-permute-start.8
  526.9 12.0 %collective-permute-done.6 = bf16[3,64,24,32]{1,3,2,0:T(8,128)(2,1)} collective-permute-done((bf16[3,64,24,32]{1,3,2,0:T(8,128)(2,1)}, bf16[3,64,24,32]{1,3,2,0:T(8,128)(2,1)}, u32[]{:S(2)}, u32[]{:S(2)}) %collective-permute-start.6) | collective-permute-done | bytes 294944 | tf_op jit(solution)/shard_map/ppermute | solution.py:17
  539.0 35.8 %collective-permute-done.7 = bf16[3,64,24,32]{1,3,2,0:T(8,128)(2,1)} collective-permute-done((bf16[3,64,24,32]{1,3,2,0:T(8,128)(2,1)}, bf16[3,64,24,32]{1,3,2,0:T(8,128)(2,1)}, u32[]{:S(2)}, u32[]{:S(2)}) %collective-permute-start.7) | collective-permute-done | bytes 294944 | tf_op jit(solution)/shard_map/ppermute | solution.py:17
  574.8 6.0 %concatenate.6 = bf16[3,512,24,32]{1,3,2,0:T(8,128)(2,1)S(1)} concatenate(bf16[3,64,24,32]{1,3,2,0:T(8,128)(2,1)S(1)} %slice_bitcast_fusion.4, bf16[3,64,24,32]{1,3,2,0:T(8,128)(2,1)} %collective-permute-done.6, bf16[3,64,24,32]{1,3,2,0:T(8,128)(2,1)} %collective-permute-done.7, bf16[3,64,24,32]{1,3,2,0:T(8,128)(2,1)} %collective-permute-done.8, ...), dimensions={1} | concatenate | bytes 4718592 | tf_op jit(solution)/shard_map/jit(_roll_dynamic)/concatenate | solution.py:96
  580.8 0.5 constant_dynamic-slice_fusion
  581.4 1.1 copy.42
  582.5 0.3 copy.50
  582.7 1.5 copy.43
  (29 shorter events, 0.8 us)
Async XLA Ops:
  6.5 185.4 %all-gather.2.cloned.1.call-start = ((), (), s32[]{:S(2)}) async-start(), calls=%async_computation | async-start | bytes 35389440 | tf_op jit(solution)/shard_map/all_gather | solution.py:48
  16.9 6.4 %copy-start = (bf16[768,6144]{1,0:T(8,128)(2,1)S(1)}, bf16[768,6144]{1,0:T(8,128)(2,1)}, u32[]{:S(2)}) copy-start(bf16[768,6144]{1,0:T(8,128)(2,1)} %param.5) | copy-start | bytes 28311556
  23.2 168.7 %copy-start.4 = (f32[6144]{0:T(1024)S(1)}, f32[6144]{0:T(1024)}, u32[]{:S(2)}) copy-start(f32[6144]{0:T(1024)} %param.6) | copy-start | bytes 73732
  243.6 261.6 %collective-permute-start.2 = (bf16[3,256,2,24,32]{1,4,3,0,2:T(8,128)(2,1)}, bf16[3,256,2,24,32]{1,4,3,0,2:T(8,128)(2,1)}, u32[]{:S(2)}, u32[]{:S(2)}) collective-permute-start(bf16[3,256,2,24,32]{1,4,3,0,2:T(8,128)(2,1)} %copy.49), channel_id=1, source_target_pairs={{0,6},{1,7},{2,0},{3,1},{4,2},{5,3},{6,4},{7,5},{8,14},{9,15},{10,... | collective-permute-start | bytes 7077896 | tf_op jit(solution)/shard_map/ppermute | solution.py:17
  246.9 258.3 %collective-permute-start.1 = (bf16[3,256,2,24,32]{1,4,3,0,2:T(8,128)(2,1)}, bf16[3,256,2,24,32]{1,4,3,0,2:T(8,128)(2,1)}, u32[]{:S(2)}, u32[]{:S(2)}) collective-permute-start(bf16[3,256,2,24,32]{1,4,3,0,2:T(8,128)(2,1)} %copy.49), channel_id=1, source_target_pairs={{0,4},{1,5},{2,6},{3,7},{4,0},{5,1},{6,2},{7,3},{8,12},{9,13},{10,... | collective-permute-start | bytes 7077896 | tf_op jit(solution)/shard_map/ppermute | solution.py:17
  247.0 258.3 %collective-permute-start = (bf16[3,256,2,24,32]{1,4,3,0,2:T(8,128)(2,1)}, bf16[3,256,2,24,32]{1,4,3,0,2:T(8,128)(2,1)}, u32[]{:S(2)}, u32[]{:S(2)}) collective-permute-start(bf16[3,256,2,24,32]{1,4,3,0,2:T(8,128)(2,1)} %copy.49), channel_id=1, source_target_pairs={{0,2},{1,3},{2,4},{3,5},{4,6},{5,7},{6,0},{7,1},{8,10},{9,11},{10,... | collective-permute-start | bytes 7077896 | tf_op jit(solution)/shard_map/ppermute | solution.py:17
  248.1 1.4 slice-start
  248.1 8.2 %copy-start.2 = (f32[128]{0:T(128)S(1)}, f32[128]{0:T(128)}, u32[]{:S(2)}) copy-start(f32[128]{0:T(128)} %param.9) | copy-start | bytes 1540
  249.5 245.1 %copy-start.3 = (f32[128]{0:T(128)S(1)}, f32[128]{0:T(128)}, u32[]{:S(2)}) copy-start(f32[128]{0:T(128)} %param.8) | copy-start | bytes 1540
  253.6 159.2 %collective-permute-start.5 = (bf16[3,64,24,32]{1,3,2,0:T(8,128)(2,1)}, bf16[3,64,24,32]{1,3,2,0:T(8,128)(2,1)}, u32[]{:S(2)}, u32[]{:S(2)}) collective-permute-start(bf16[3,64,24,32]{1,3,2,0:T(8,128)(2,1)} %bitcast.88), channel_id=1, source_target_pairs={{0,6},{1,7},{2,0},{3,1},{4,2},{5,3},{6,4},{7,5},{8,14},{9,15},{10,... | collective-permute-start | bytes 884744 | tf_op jit(solution)/shard_map/ppermute | solution.py:17
  258.4 242.1 %collective-permute-start.4 = (bf16[3,64,24,32]{1,3,2,0:T(8,128)(2,1)}, bf16[3,64,24,32]{1,3,2,0:T(8,128)(2,1)}, u32[]{:S(2)}, u32[]{:S(2)}) collective-permute-start(bf16[3,64,24,32]{1,3,2,0:T(8,128)(2,1)} %bitcast.89), channel_id=1, source_target_pairs={{0,4},{1,5},{2,6},{3,7},{4,0},{5,1},{6,2},{7,3},{8,12},{9,13},{10,... | collective-permute-start | bytes 884744 | tf_op jit(solution)/shard_map/ppermute | solution.py:17
  412.8 88.1 %collective-permute-start.3 = (bf16[3,64,24,32]{1,3,2,0:T(8,128)(2,1)}, bf16[3,64,24,32]{1,3,2,0:T(8,128)(2,1)}, u32[]{:S(2)}, u32[]{:S(2)}) collective-permute-start(bf16[3,64,24,32]{1,3,2,0:T(8,128)(2,1)} %bitcast.90), channel_id=1, source_target_pairs={{0,2},{1,3},{2,4},{3,5},{4,6},{5,7},{6,0},{7,1},{8,10},{9,11},{10,... | collective-permute-start | bytes 884744 | tf_op jit(solution)/shard_map/ppermute | solution.py:17
  496.6 1.1 copy-start.1
  521.6 17.4 %collective-permute-start.6 = (bf16[3,64,24,32]{1,3,2,0:T(8,128)(2,1)}, bf16[3,64,24,32]{1,3,2,0:T(8,128)(2,1)}, u32[]{:S(2)}, u32[]{:S(2)}) collective-permute-start(bf16[3,64,24,32]{1,3,2,0:T(8,128)(2,1)} %get-tuple-element.6), channel_id=1, source_target_pairs={{0,6},{1,7},{2,0},{3,1},{4,2},{5,3},{6,4},{7,5},{8,14},{9,15},{10,... | collective-permute-start | bytes 884744 | tf_op jit(solution)/shard_map/ppermute | solution.py:17
  524.8 50.0 %collective-permute-start.7 = (bf16[3,64,24,32]{1,3,2,0:T(8,128)(2,1)}, bf16[3,64,24,32]{1,3,2,0:T(8,128)(2,1)}, u32[]{:S(2)}, u32[]{:S(2)}) collective-permute-start(bf16[3,64,24,32]{1,3,2,0:T(8,128)(2,1)} %get-tuple-element.5), channel_id=1, source_target_pairs={{0,4},{1,5},{2,6},{3,7},{4,0},{5,1},{6,2},{7,3},{8,12},{9,13},{10,... | collective-permute-start | bytes 884744 | tf_op jit(solution)/shard_map/ppermute | solution.py:17
  526.4 48.4 %collective-permute-start.8 = (bf16[3,64,24,32]{1,3,2,0:T(8,128)(2,1)}, bf16[3,64,24,32]{1,3,2,0:T(8,128)(2,1)}, u32[]{:S(2)}, u32[]{:S(2)}) collective-permute-start(bf16[3,64,24,32]{1,3,2,0:T(8,128)(2,1)} %dynamic-slice_bitcast_fusion), channel_id=1, source_target_pairs={{0,2},{1,3},{2,4},{3,5},{4,6},{5,7},{6,0},{7,1},{8,10},{9,11},{10,... | collective-permute-start | bytes 884744 | tf_op jit(solution)/shard_map/ppermute | solution.py:17
Sparse Core Ops, SparseCore 0:
  17.0 174.8 all-gather.1
where the time goes:
time: 592 us; the launch traced here: 591 us
  waiting for transfers between devices  368 us (62%)
  starting transfers between devices  89 us (15%)
  local copies, waits for them, and re-layouts  54.8 us (9%)
  matrix products  37.7 us (6%)
  other arithmetic  21.9 us (4%)
  between operations  19.4 us (3%)
    ppermute x9, waiting for transfers between devices, from_behind(): lax.ppermute(shard, axis, [(i, (i + by) % length) for i in range(length)])  202 us
    all_gather x1, waiting for transfers between devices, body(): row_piece = lax.all_gather(w_qkv, 'dp', axis=0, tiled=True)  166 us
    ppermute x9, starting transfers between devices, from_behind(): lax.ppermute(shard, axis, [(i, (i + by) % length) for i in range(length)])  89 us
    dot_general x1, matrix products, body(): jnp.dot(normed, row_piece.reshape(row_piece.shape[0], out_width), preferr...  31.3 us
    unnamed x14, local copies, waits for them, and re-layouts  14.6 us
  transfers between devices with their start and end apart: 10, of which 6 were waited for; matrix products, arithmetic and copies ran while one was open for 4% of the time, Pallas kernels for 0%

commit v1 on v0

--- a/solution.py
+++ b/solution.py
@@ -1,12 +1,18 @@
+import functools
+
 import jax
 import jax.numpy as jnp
 from jax import lax
+from jax.experimental import pallas as pl
+from jax.experimental.pallas import tpu as pltpu
 from jax.sharding import PartitionSpec as P
+
 
 HEADS = 48
 HEAD_DIM = 128
 PATCHES = 256
 SPLITS = 4
+LANES = 128
 
 
 norm_eps = 1e-06
@@ -40,7 +46,7 @@
     return jnp.dot(selector, gain_table, precision=lax.Precision.HIGHEST)
 
 
-def body(tokens, ln_gain, w_qkv, q_gain, k_gain):
+def row_body(tokens, ln_gain, w_qkv, q_gain, k_gain):
     local_rows = tokens.shape[0]
     normed = layer_norm(tokens.astype(jnp.float32), ln_gain).astype(jnp.bfloat16)
     flat_weight = w_qkv.reshape(w_qkv.shape[0], -1)
@@ -97,6 +103,251 @@
     return own_block.reshape(local_rows, -1)
 
 
+def swap(value, axis, mask):
+    length = lax.axis_size(axis)
+    return lax.ppermute(value, axis, [(i, i ^ mask) for i in range(length)])
+
+
+def call(kernel, grid, in_specs, out_specs, out_shape, flops, bytes_accessed, scalars, scratch=()):
+    return pl.pallas_call(
+        kernel,
+        grid_spec=pltpu.PrefetchScalarGridSpec(
+            num_scalar_prefetch=scalars,
+            grid=grid,
+            in_specs=in_specs,
+            out_specs=out_specs,
+            scratch_shapes=list(scratch),
+        ),
+        out_shape=out_shape,
+        cost_estimate=pl.CostEstimate(
+            flops=flops, bytes_accessed=bytes_accessed, transcendentals=0
+        ),
+        compiler_params=pltpu.CompilerParams(
+            dimension_semantics=("arbitrary",) * len(grid), vmem_limit_bytes=48 * 2**20
+        ),
+    )
+
+
+def norm_kernel(parts, place, tokens, gain, out):
+    width = tokens.shape[1] // parts
+    values = tokens[...].astype(jnp.float32)
+    centre = jnp.mean(values, axis=-1, keepdims=True)
+    centred = values - centre
+    spread = jnp.mean(centred * centred, axis=-1, keepdims=True)
+    scale = lax.rsqrt(spread + norm_eps)
+    for rel in range(parts):
+        start = pl.multiple_of((place[0] ^ rel) * width, LANES)
+        piece = tokens[:, pl.ds(start, width)].astype(jnp.float32)
+        piece = (piece - centre) * scale * gain[:, pl.ds(start, width)]
+        out[:, rel * width : (rel + 1) * width] = piece.astype(jnp.bfloat16)
+
+
+def norm_tokens(place, tokens, gain, parts):
+    rows, width = tokens.shape
+    block = rows // 6
+    return call(
+        functools.partial(norm_kernel, parts),
+        (rows // block,),
+        [
+            pl.BlockSpec((block, width), lambda i, s: (i, 0)),
+            pl.BlockSpec((1, width), lambda i, s: (0, 0)),
+        ],
+        pl.BlockSpec((block, width), lambda i, s: (i, 0)),
+        jax.ShapeDtypeStruct((rows, width), jnp.bfloat16),
+        rows * width * 1200,
+        rows * width * 4,
+        1,
+    )(place, tokens, gain[None, :])
+
+
+def wide(weight):
+    return jnp.concatenate([weight[p] for p in range(weight.shape[0])], axis=1)
+
+
+def product(normed, first, second):
+    depth = first.shape[1]
+    total = jnp.dot(normed[:, :depth], wide(first), preferred_element_type=jnp.float32)
+    return total + jnp.dot(normed[:, depth:], wide(second), preferred_element_type=jnp.float32)
+
+
+def near_kernel(normed, first, second, out):
+    out[...] = product(normed, first, second)
+
+
+def near_product(normed, first, second, chunk):
+    rows, width = normed.shape
+    kinds, depth, _ = first.shape
+    cols = kinds * LANES
+    return call(
+        near_kernel,
+        (rows // PATCHES,),
+        [
+            pl.BlockSpec((PATCHES, width // 2), lambda i: (i, 0)),
+            pl.BlockSpec((kinds, depth, LANES), lambda i: (0, 0, chunk)),
+            pl.BlockSpec((kinds, depth, LANES), lambda i: (0, 0, chunk)),
+        ],
+        pl.BlockSpec((PATCHES, cols), lambda i: (i, 0)),
+        jax.ShapeDtypeStruct((rows, cols), jnp.float32),
+        rows * width * cols,
+        rows * width + 2 * cols * width // 2,
+        0,
+    )(normed, first, second)
+
+
+def far_kernel(quarter, total, normed, first, second, out0, out1, out2, out3, hold):
+    done = (total[...] + product(normed, first, second)).astype(jnp.bfloat16)
+    part = hold.shape[1] // SPLITS
+    for kind in range(hold.shape[0]):
+        hold[kind] = done[:, kind * LANES : (kind + 1) * LANES].T
+    for rel, out in enumerate((out0, out1, out2, out3)):
+        start = pl.multiple_of((quarter[0] ^ rel) * part, part)
+        out[...] = hold[:, pl.ds(start, part), :]
+
+
+def far_product(quarter, total, normed, first, second):
+    rows, width = normed.shape
+    kinds, depth, _ = first.shape
+    cols = kinds * LANES
+    part = LANES // SPLITS
+    return call(
+        far_kernel,
+        (rows // PATCHES,),
+        [
+            pl.BlockSpec((PATCHES, cols), lambda i, s: (i, 0)),
+            pl.BlockSpec((PATCHES, width // 2), lambda i, s: (i, 1)),
+            pl.BlockSpec((kinds, depth, LANES), lambda i, s: (0, 0, 0)),
+            pl.BlockSpec((kinds, depth, LANES), lambda i, s: (0, 0, 0)),
+        ],
+        [pl.BlockSpec((kinds, part, PATCHES), lambda i, s: (0, 0, i))] * SPLITS,
+        [jax.ShapeDtypeStruct((kinds, part, rows), jnp.bfloat16)] * SPLITS,
+        rows * width * cols,
+        rows * width + 2 * cols * width // 2,
+        1,
+        [pltpu.VMEM((kinds, LANES, PATCHES), jnp.bfloat16)],
+    )(quarter, total, normed, first, second)
+
+
+def head_layer_norm(values, gain_rows):
+    centre = jnp.mean(values, axis=0, keepdims=True)
+    centred = values - centre
+    spread = jnp.mean(centred * centred, axis=0, keepdims=True)
+    return centred * lax.rsqrt(spread + norm_eps) * gain_rows
+
+
+def attend_kernel(quarter, in0, in1, in2, in3, q_gain, k_gain, out0, out1, out2, out3):
+    pieces = (in0, in1, in2, in3)
+    part = in0.shape[1]
+
+    def gains(ref):
+        return jnp.concatenate(
+            [
+                ref[pl.ds(pl.multiple_of((quarter[0] ^ rel) * part, part), part), :]
+                for rel in range(SPLITS)
+            ],
+            axis=0,
+        )
+
+    def features(kind):
+        return jnp.concatenate([piece[kind] for piece in pieces], axis=0)
+
+    query = head_layer_norm(features(0).astype(jnp.float32), gains(q_gain))
+    query = (query * HEAD_DIM ** (-0.5)).astype(jnp.bfloat16)
+    key = head_layer_norm(features(1).astype(jnp.float32), gains(k_gain)).astype(jnp.bfloat16)
+    scores = lax.dot_general(
+        key, query, (((0,), (0,)), ((), ())), preferred_element_type=jnp.float32
+    )
+    raised = jnp.exp(scores)
+    weights = (raised / jnp.sum(raised, axis=0, keepdims=True)).astype(jnp.bfloat16)
+    attended = jnp.dot(features(2), weights, preferred_element_type=jnp.float32)
+    attended = attended.astype(jnp.bfloat16)
+    for rel, out in enumerate((out0, out1, out2, out3)):
+        out[...] = attended[rel * part : (rel + 1) * part]
+
+
+def attend(quarter, pieces, q_gain, k_gain):
+    kinds, part, rows = pieces[0].shape
+    gain_spec = pl.BlockSpec((HEAD_DIM, PATCHES), lambda i, s: (0, 0))
+    return call(
+        attend_kernel,
+        (rows // PATCHES,),
+        [pl.BlockSpec((kinds, part, PATCHES), lambda i, s: (0, 0, i))] * SPLITS
+        + [gain_spec, gain_spec],
+        [pl.BlockSpec((part, PATCHES), lambda i, s: (0, i))] * SPLITS,
+        [jax.ShapeDtypeStruct((part, rows), jnp.bfloat16)] * SPLITS,
+        rows * PATCHES * HEAD_DIM * 30,
+        rows * HEAD_DIM * 8,
+        1,
+    )(quarter, *pieces, q_gain, k_gain)
+
+
+def finish_kernel(quarter, *refs):
+    out, hold = refs[-2:]
+    pieces = refs[:-2]
+    part = pieces[0].shape[0]
+    for chunk in range(len(pieces) // SPLITS):
+        for rel in range(SPLITS):
+            start = pl.multiple_of((quarter[0] ^ rel) * part, part)
+            hold[pl.ds(start, part), :] = pieces[chunk * SPLITS + rel][...]
+        out[:, chunk * LANES : (chunk + 1) * LANES] = hold[...].T
+
+
+def finish(quarter, pieces):
+    part, rows = pieces[0].shape
+    width = part * len(pieces)
+    return call(
+        finish_kernel,
+        (1,),
+        [pl.BlockSpec((part, rows), lambda i, s: (0, 0))] * len(pieces),
+        pl.BlockSpec((rows, width), lambda i, s: (0, 0)),
+        jax.ShapeDtypeStruct((rows, width), jnp.bfloat16),
+        rows * width * 100,
+        rows * width * 4,
+        1,
+        [pltpu.VMEM((LANES, rows), jnp.bfloat16)],
+    )(quarter, *pieces)
+
+
+def after(value, *others):
+    return lax.optimization_barrier((value, *others))[0]
+
+
+def chunked_body(tokens, ln_gain, w_qkv, q_gain, k_gain):
+    parts = lax.axis_size("dp")
+    groups = lax.axis_size("mp") // SPLITS
+    place = lax.axis_index("dp").astype(jnp.int32)[None]
+    quarter = (lax.axis_index("mp") // groups).astype(jnp.int32)[None]
+    weight = jnp.transpose(w_qkv, (1, 0, 2))
+    chunks = weight.shape[2] // LANES
+    slices = [weight[:, :, :LANES]]
+    rest = after(weight, slices[0])
+    slices += [rest[:, :, c * LANES : (c + 1) * LANES] for c in range(1, chunks)]
+    beside = [swap(slices[c], "dp", 2) for c in range(chunks)]
+    paired = swap(after(weight, slices[1]), "dp", 1)
+    normed = norm_tokens(place, tokens, ln_gain, parts)
+    wide_q = jnp.broadcast_to(q_gain[:, None], (HEAD_DIM, PATCHES))
+    wide_k = jnp.broadcast_to(k_gain[:, None], (HEAD_DIM, PATCHES))
+    returned = []
+    for c in range(chunks):
+        total = near_product(normed, weight, paired, c)
+        across = swap(beside[c], "dp", 1)
+        pieces = far_product(quarter, total, normed, beside[c], across)
+        moved = [pieces[0]] + [swap(pieces[rel], "mp", rel * groups) for rel in range(1, SPLITS)]
+        results = attend(quarter, moved, wide_q, wide_k)
+        returned += [results[0]] + [
+            swap(results[rel], "mp", rel * groups)
+            for rel in range(1, SPLITS)
+        ]
+    return finish(quarter, returned)
+
+
+def body(tokens, ln_gain, w_qkv, q_gain, k_gain):
+    pairs = lax.axis_size("dp") == 4
+    whole = w_qkv.shape[2] % LANES == 0 and HEAD_DIM // SPLITS * SPLITS == LANES
+    if pairs and whole:
+        return chunked_body(tokens, ln_gain, w_qkv, q_gain, k_gain)
+    return row_body(tokens, ln_gain, w_qkv, q_gain, k_gain)
+
+
 def solution(mesh):
     return jax.shard_map(
         body,

time: 592 us -> 309 us (0.52)
  waiting for transfers between devices: 368 us -> 128 us
  Pallas kernels: 0 us -> 91 us
  local copies, waits for them, and re-layouts: 54.8 us -> 7.96 us
  matrix products: 37.7 us -> 0 us
  other arithmetic: 21.9 us -> 0 us
  between operations: 19.4 us -> 0.35 us
  starting transfers between devices: 89 us -> 81 us
    all_gather x1 -> x0, waiting for transfers between devices: 166 us -> none  [body(): row_piece = lax.all_gather(w_qkv, 'dp', axis=0, tiled=True)]
    pallas_call x0 -> x20, Pallas kernels: none -> 91 us  [the longest x6 33 us: near_product(): call(near_kernel, (rows // PATCHES,), [pl.BlockSpec((PATCHES, width // 2)...]
    ppermute x9 -> x49, waiting for transfers between devices: 202 us -> 128 us  [swap(): return lax.ppermute(value, axis, [(i, i ^ mask) for i in range(length)])]
    dot_general x5 -> x0, matrix products: 37.7 us -> none  [the longest x1 31.3 us: body(): jnp.dot(normed, row_piece.reshape(row_piece.shape[0], out_width), preferr...]
    reduce_sum x9 -> x0, other arithmetic: 17.7 us -> none  [the longest x1 5.17 us: layer_norm(): centre = jnp.mean(values, axis=-1, keepdims=True)]
    unnamed x14 -> x6, local copies, waits for them, and re-layouts: 14.6 us -> 0.75 us
    reshape x4 -> x0, local copies, waits for them, and re-layouts: 10.3 us -> none  [the longest x1 8.73 us: body(): projected.reshape(images, PATCHES, 3, head_count, HEAD_DIM // SPLITS)]
    dynamic_slice x7 -> x0, local copies, waits for them, and re-layouts: 9.9 us -> none  [the longest x3 5.02 us: body(): lax.dynamic_slice_in_dim(queries, (my_quarter + offset) % SPLITS * quarte...]
  transfers between devices with their start and end apart: 10 -> 49, of which waited for: 6 -> 12; matrix products, arithmetic and copies ran while one was open for 4% -> 0% of each run, Pallas kernels for 0% -> 29%
where the time goes in v1:
time: 309 us; the launch traced here: 308 us
  waiting for transfers between devices  128 us (41%)
  Pallas kernels  91 us (29%)
  starting transfers between devices  81 us (26%)
  local copies, waits for them, and re-layouts  7.96 us (3%)
    ppermute x49, waiting for transfers between devices, swap(): return lax.ppermute(value, axis, [(i, i ^ mask) for i in range(length)])  128 us
    ppermute x49, starting transfers between devices, swap(): return lax.ppermute(value, axis, [(i, i ^ mask) for i in range(length)])  81 us
    pallas_call x6, Pallas kernels, near_product(): call(near_kernel, (rows // PATCHES,), [pl.BlockSpec((PATCHES, width // 2)...  33 us
    pallas_call x6, Pallas kernels, far_product(): call(far_kernel, (rows // PATCHES,), [pl.BlockSpec((PATCHES, cols), lambd...  33 us
    pallas_call x1, Pallas kernels, norm_tokens(): call(functools.partial(norm_kernel, parts), (rows // block,), [pl.BlockSp...  13.7 us
    pallas_call x6, Pallas kernels, attend(): call(attend_kernel, (rows // PATCHES,), [pl.BlockSpec((kinds, part, PATCH...  9.92 us
  transfers between devices with their start and end apart: 49, of which 12 were waited for; matrix products, arithmetic and copies ran while one was open for 0% of the time, Pallas kernels for 29%

profile of v1, /device:TPU:0, one launch (start us, length us, event | category | flops | bytes accessed | tf_op | source)
XLA Modules:
  0.0 308.3 jit_solution(18152440466028174477)
XLA Ops:
  0.0 2.4 slice.24
  2.4 4.7 %fusion = (bf16[3,1536,128]{2,1,0:T(8,128)(2,1)S(1)}, bf16[3,1536,128]{2,1,0:T(8,128)(2,1)S(1)}, bf16[3,1536,128]{2,1,0:T(8,128)(2,1)S(1)}, bf16[3,1536,128]{2,1,0:T(8,128)(2,1)}, bf16[3,1536,128]{2,1,0:T(8,128)(2,1)}) fusion(bf16[3,1536,768]{2,1,0:T(8,128)(2,1)} %bitcast.3.first), kind=kLoop, calls=%fused_computation | loop fusion | bytes 11796480 | tf_op jit(solution)/shard_map/slice | solution.py:323
  7.6 2.5 collective-permute-start.41
  10.1 2.0 collective-permute-start.25
  12.1 24.8 %collective-permute-done.41.first = bf16[3,1536,128]{2,1,0:T(8,128)(2,1)} collective-permute-done((bf16[3,1536,128]{2,1,0:T(8,128)(2,1)S(1)}, bf16[3,1536,128]{2,1,0:T(8,128)(2,1)}, u32[]{:S(2)}, u32[]{:S(2)}) %collective-permute-start.41) | collective-permute-done | bytes 1179680 | tf_op jit(solution)/shard_map/ppermute | solution.py:108
  37.0 2.0 collective-permute-start.9
  39.0 23.3 %collective-permute-done.33.first = bf16[3,1536,128]{2,1,0:T(8,128)(2,1)} collective-permute-done((bf16[3,1536,128]{2,1,0:T(8,128)(2,1)S(1)}, bf16[3,1536,128]{2,1,0:T(8,128)(2,1)}, u32[]{:S(2)}, u32[]{:S(2)}) %collective-permute-start.33) | collective-permute-done | bytes 1179680 | tf_op jit(solution)/shard_map/ppermute | solution.py:108
  62.2 2.0 collective-permute-start.1
  64.3 23.3 %collective-permute-done.25.first = bf16[3,1536,128]{2,1,0:T(8,128)(2,1)} collective-permute-done((bf16[3,1536,128]{2,1,0:T(8,128)(2,1)S(1)}, bf16[3,1536,128]{2,1,0:T(8,128)(2,1)}, u32[]{:S(2)}, u32[]{:S(2)}) %collective-permute-start.25) | collective-permute-done | bytes 1179680 | tf_op jit(solution)/shard_map/ppermute | solution.py:108
  88.3 13.7 %shard_map.55.normed = bf16[768,6144]{1,0:T(8,128)(2,1)} custom-call(s32[1]{0:T(128)} %bitcast.1.place, bf16[768,6144]{1,0:T(8,128)(2,1)} %tokens.1, f32[1,6144]{1,0:T(1,128)S(1)} %bitcast.4), custom_call_target="tpu_custom_call" | custom-call | flops 5662310400 | bytes 18874368 | tf_op jit(solution)/shard_map/pallas_call | solution.py:148
  102.5 5.5 %shard_map.71.total = f32[768,384]{1,0:T(8,128)S(1)} custom-call(bf16[768,6144]{1,0:T(8,128)(2,1)} %shard_map.55.normed, bf16[3,1536,768]{2,1,0:T(8,128)(2,1)} %bitcast.3.first, bf16[3,1536,768]{2,1,0:T(8,128)(2,1)} %collective-permute-done.second), custom_call_target="tpu_custom_call" | custom-call | flops 1811939328 | bytes 7077888 | tf_op jit(solution)/shard_map/pallas_call | solution.py:181
  108.0 4.7 %collective-permute-done.17.first = bf16[3,1536,128]{2,1,0:T(8,128)(2,1)S(1)} collective-permute-done((bf16[3,1536,128]{2,1,0:T(8,128)(2,1)}, bf16[3,1536,128]{2,1,0:T(8,128)(2,1)S(1)}, u32[]{:S(2)}, u32[]{:S(2)}) %collective-permute-start.17) | collective-permute-done | bytes 1179680 | tf_op jit(solution)/shard_map/ppermute | solution.py:108
  112.7 5.5 %shard_map.68.total = f32[768,384]{1,0:T(8,128)S(1)} custom-call(bf16[768,6144]{1,0:T(8,128)(2,1)} %shard_map.55.normed, bf16[3,1536,768]{2,1,0:T(8,128)(2,1)} %bitcast.3.first, bf16[3,1536,768]{2,1,0:T(8,128)(2,1)} %collective-permute-done.second), custom_call_target="tpu_custom_call" | custom-call | flops 1811939328 | bytes 7077888 | tf_op jit(solution)/shard_map/pallas_call | solution.py:181
  118.2 19.8 %collective-permute-done.9.first = bf16[3,1536,128]{2,1,0:T(8,128)(2,1)S(1)} collective-permute-done((bf16[3,1536,128]{2,1,0:T(8,128)(2,1)}, bf16[3,1536,128]{2,1,0:T(8,128)(2,1)S(1)}, u32[]{:S(2)}, u32[]{:S(2)}) %collective-permute-start.9) | collective-permute-done | bytes 1179680 | tf_op jit(solution)/shard_map/ppermute | solution.py:108
  138.0 5.5 %shard_map.65.total = f32[768,384]{1,0:T(8,128)S(1)} custom-call(bf16[768,6144]{1,0:T(8,128)(2,1)} %shard_map.55.normed, bf16[3,1536,768]{2,1,0:T(8,128)(2,1)} %bitcast.3.first, bf16[3,1536,768]{2,1,0:T(8,128)(2,1)} %collective-permute-done.second), custom_call_target="tpu_custom_call" | custom-call | flops 1811939328 | bytes 7077888 | tf_op jit(solution)/shard_map/pallas_call | solution.py:181
  143.5 19.6 %collective-permute-done.1.first = bf16[3,1536,128]{2,1,0:T(8,128)(2,1)S(1)} collective-permute-done((bf16[3,1536,128]{2,1,0:T(8,128)(2,1)}, bf16[3,1536,128]{2,1,0:T(8,128)(2,1)S(1)}, u32[]{:S(2)}, u32[]{:S(2)}) %collective-permute-start.1) | collective-permute-done | bytes 1179680 | tf_op jit(solution)/shard_map/ppermute | solution.py:108
  163.6 5.5 %shard_map.62.total = f32[768,384]{1,0:T(8,128)S(1)} custom-call(bf16[768,6144]{1,0:T(8,128)(2,1)} %shard_map.55.normed, bf16[3,1536,768]{2,1,0:T(8,128)(2,1)} %bitcast.3.first, bf16[3,1536,768]{2,1,0:T(8,128)(2,1)} %collective-permute-done.second), custom_call_target="tpu_custom_call" | custom-call | flops 1811939328 | bytes 7077888 | tf_op jit(solution)/shard_map/pallas_call | solution.py:181
  169.1 5.5 %shard_map.59.total = f32[768,384]{1,0:T(8,128)S(1)} custom-call(bf16[768,6144]{1,0:T(8,128)(2,1)} %shard_map.55.normed, bf16[3,1536,768]{2,1,0:T(8,128)(2,1)} %bitcast.3.first, bf16[3,1536,768]{2,1,0:T(8,128)(2,1)} %collective-permute-done.second), custom_call_target="tpu_custom_call" | custom-call | flops 1811939328 | bytes 7077888 | tf_op jit(solution)/shard_map/pallas_call | solution.py:181
  174.6 5.5 %shard_map.56.total = f32[768,384]{1,0:T(8,128)S(1)} custom-call(bf16[768,6144]{1,0:T(8,128)(2,1)} %shard_map.55.normed, bf16[3,1536,768]{2,1,0:T(8,128)(2,1)} %bitcast.3.first, bf16[3,1536,768]{2,1,0:T(8,128)(2,1)} %collective-permute-done.second), custom_call_target="tpu_custom_call" | custom-call | flops 1811939328 | bytes 7077888 | tf_op jit(solution)/shard_map/pallas_call | solution.py:181
  180.1 5.8 %shard_map.72 = (bf16[3,32,768]{2,1,0:T(8,128)(2,1)S(1)}, bf16[3,32,768]{2,1,0:T(8,128)(2,1)S(1)}, bf16[3,32,768]{2,1,0:T(8,128)(2,1)S(1)}, bf16[3,32,768]{2,1,0:T(8,128)(2,1)S(1)}) custom-call(s32[1]{0:T(128)} %bitcast.quarter, f32[768,384]{1,0:T(8,128)S(1)} %shard_map.71.total, bf16[768,6144]{1,0:T(8,128)(2,1)} %shard_map.55.normed, ...), custom_call_target="tpu_custom_call" | custom-call | flops 1811939328 | bytes 7077888 | tf_op jit(solution)/shard_map/pallas_call | solution.py:212
  185.9 1.9 collective-permute-start.43
  187.8 5.8 %shard_map.69 = (bf16[3,32,768]{2,1,0:T(8,128)(2,1)S(1)}, bf16[3,32,768]{2,1,0:T(8,128)(2,1)S(1)}, bf16[3,32,768]{2,1,0:T(8,128)(2,1)S(1)}, bf16[3,32,768]{2,1,0:T(8,128)(2,1)S(1)}) custom-call(s32[1]{0:T(128)} %bitcast.quarter, f32[768,384]{1,0:T(8,128)S(1)} %shard_map.68.total, bf16[768,6144]{1,0:T(8,128)(2,1)} %shard_map.55.normed, ...), custom_call_target="tpu_custom_call" | custom-call | flops 1811939328 | bytes 7077888 | tf_op jit(solution)/shard_map/pallas_call | solution.py:212
  193.6 2.7 collective-permute-start.44
  196.2 5.8 %shard_map.66 = (bf16[3,32,768]{2,1,0:T(8,128)(2,1)S(1)}, bf16[3,32,768]{2,1,0:T(8,128)(2,1)S(1)}, bf16[3,32,768]{2,1,0:T(8,128)(2,1)S(1)}, bf16[3,32,768]{2,1,0:T(8,128)(2,1)S(1)}) custom-call(s32[1]{0:T(128)} %bitcast.quarter, f32[768,384]{1,0:T(8,128)S(1)} %shard_map.65.total, bf16[768,6144]{1,0:T(8,128)(2,1)} %shard_map.55.normed, ...), custom_call_target="tpu_custom_call" | custom-call | flops 1811939328 | bytes 7077888 | tf_op jit(solution)/shard_map/pallas_call | solution.py:212
  202.1 5.6 %shard_map.63 = (bf16[3,32,768]{2,1,0:T(8,128)(2,1)S(1)}, bf16[3,32,768]{2,1,0:T(8,128)(2,1)S(1)}, bf16[3,32,768]{2,1,0:T(8,128)(2,1)S(1)}, bf16[3,32,768]{2,1,0:T(8,128)(2,1)S(1)}) custom-call(s32[1]{0:T(128)} %bitcast.quarter, f32[768,384]{1,0:T(8,128)S(1)} %shard_map.62.total, bf16[768,6144]{1,0:T(8,128)(2,1)} %shard_map.55.normed, ...), custom_call_target="tpu_custom_call" | custom-call | flops 1811939328 | bytes 7077888 | tf_op jit(solution)/shard_map/pallas_call | solution.py:212
  208.5 3.5 %collective-permute-start.36 = (bf16[3,32,768]{2,1,0:T(8,128)(2,1)S(1)}, bf16[3,32,768]{2,1,0:T(8,128)(2,1)S(1)}, u32[]{:S(2)}, u32[]{:S(2)}) collective-permute-start(bf16[3,32,768]{2,1,0:T(8,128)(2,1)S(1)} %get-tuple-element.91), channel_id=1, source_target_pairs={{0,4},{1,5},{2,6},{3,7},{4,0},{5,1},{6,2},{7,3},{8,12},{9,13},{10,... | collective-permute-start | bytes 442376 | tf_op jit(solution)/shard_map/ppermute | solution.py:108
  212.6 3.8 %collective-permute-start.28 = (bf16[3,32,768]{2,1,0:T(8,128)(2,1)S(1)}, bf16[3,32,768]{2,1,0:T(8,128)(2,1)S(1)}, u32[]{:S(2)}, u32[]{:S(2)}) collective-permute-start(bf16[3,32,768]{2,1,0:T(8,128)(2,1)S(1)} %get-tuple-element.83), channel_id=1, source_target_pairs={{0,4},{1,5},{2,6},{3,7},{4,0},{5,1},{6,2},{7,3},{8,12},{9,13},{10,... | collective-permute-start | bytes 442376 | tf_op jit(solution)/shard_map/ppermute | solution.py:108
  216.4 5.0 %shard_map.60 = (bf16[3,32,768]{2,1,0:T(8,128)(2,1)S(1)}, bf16[3,32,768]{2,1,0:T(8,128)(2,1)S(1)}, bf16[3,32,768]{2,1,0:T(8,128)(2,1)S(1)}, bf16[3,32,768]{2,1,0:T(8,128)(2,1)S(1)}) custom-call(s32[1]{0:T(128)} %bitcast.quarter, f32[768,384]{1,0:T(8,128)S(1)} %shard_map.59.total, bf16[768,6144]{1,0:T(8,128)(2,1)} %shard_map.55.normed, ...), custom_call_target="tpu_custom_call" | custom-call | flops 1811939328 | bytes 7077888 | tf_op jit(solution)/shard_map/pallas_call | solution.py:212
  223.6 10.2 %collective-permute-start.20 = (bf16[3,32,768]{2,1,0:T(8,128)(2,1)S(1)}, bf16[3,32,768]{2,1,0:T(8,128)(2,1)S(1)}, u32[]{:S(2)}, u32[]{:S(2)}) collective-permute-start(bf16[3,32,768]{2,1,0:T(8,128)(2,1)S(1)} %get-tuple-element.75), channel_id=1, source_target_pairs={{0,4},{1,5},{2,6},{3,7},{4,0},{5,1},{6,2},{7,3},{8,12},{9,13},{10,... | collective-permute-start | bytes 442376 | tf_op jit(solution)/shard_map/ppermute | solution.py:108
  233.8 1.5 collective-permute-start.21
  235.3 5.7 %collective-permute-done.28.in2 = bf16[3,32,768]{2,1,0:T(8,128)(2,1)S(1)} collective-permute-done((bf16[3,32,768]{2,1,0:T(8,128)(2,1)S(1)}, bf16[3,32,768]{2,1,0:T(8,128)(2,1)S(1)}, u32[]{:S(2)}, u32[]{:S(2)}) %collective-permute-start.28) | collective-permute-done | bytes 147488 | tf_op jit(solution)/shard_map/ppermute | solution.py:108
  241.1 5.1 %shard_map.57 = (bf16[3,32,768]{2,1,0:T(8,128)(2,1)S(1)}, bf16[3,32,768]{2,1,0:T(8,128)(2,1)S(1)}, bf16[3,32,768]{2,1,0:T(8,128)(2,1)S(1)}, bf16[3,32,768]{2,1,0:T(8,128)(2,1)S(1)}) custom-call(s32[1]{0:T(128)} %bitcast.quarter, f32[768,384]{1,0:T(8,128)S(1)} %shard_map.56.total, bf16[768,6144]{1,0:T(8,128)(2,1)} %shard_map.55.normed, ...), custom_call_target="tpu_custom_call" | custom-call | flops 1811939328 | bytes 7077888 | tf_op jit(solution)/shard_map/pallas_call | solution.py:212
  246.2 3.5 %collective-permute-start.12 = (bf16[3,32,768]{2,1,0:T(8,128)(2,1)S(1)}, bf16[3,32,768]{2,1,0:T(8,128)(2,1)S(1)}, u32[]{:S(2)}, u32[]{:S(2)}) collective-permute-start(bf16[3,32,768]{2,1,0:T(8,128)(2,1)S(1)} %get-tuple-element.67), channel_id=1, source_target_pairs={{0,4},{1,5},{2,6},{3,7},{4,0},{5,1},{6,2},{7,3},{8,12},{9,13},{10,... | collective-permute-start | bytes 442376 | tf_op jit(solution)/shard_map/ppermute | solution.py:108
  251.4 1.7 shard_map.73
  253.1 7.9 %collective-permute-start.4 = (bf16[3,32,768]{2,1,0:T(8,128)(2,1)S(1)}, bf16[3,32,768]{2,1,0:T(8,128)(2,1)S(1)}, u32[]{:S(2)}, u32[]{:S(2)}) collective-permute-start(bf16[3,32,768]{2,1,0:T(8,128)(2,1)S(1)} %get-tuple-element.59), channel_id=1, source_target_pairs={{0,4},{1,5},{2,6},{3,7},{4,0},{5,1},{6,2},{7,3},{8,12},{9,13},{10,... | collective-permute-start | bytes 442376 | tf_op jit(solution)/shard_map/ppermute | solution.py:108
  261.0 2.1 collective-permute-start.5
  263.1 1.6 shard_map.70
  264.8 1.7 shard_map.67
  266.5 6.0 %collective-permute-start.47 = (bf16[32,768]{1,0:T(8,128)(2,1)S(1)}, bf16[32,768]{1,0:T(8,128)(2,1)S(1)}, u32[]{:S(2)}, u32[]{:S(2)}) collective-permute-start(bf16[32,768]{1,0:T(8,128)(2,1)S(1)} %get-tuple-element.103), channel_id=1, source_target_pairs={{0,4},{1,5},{2,6},{3,7},{4,0},{5,1},{6,2},{7,3},{8,12},{9,13},{10,... | collective-permute-start | bytes 147464 | tf_op jit(solution)/shard_map/ppermute | solution.py:108
  273.6 1.6 shard_map.64
  275.4 4.6 %collective-permute-start.39 = (bf16[32,768]{1,0:T(8,128)(2,1)S(1)}, bf16[32,768]{1,0:T(8,128)(2,1)S(1)}, u32[]{:S(2)}, u32[]{:S(2)}) collective-permute-start(bf16[32,768]{1,0:T(8,128)(2,1)S(1)} %get-tuple-element.95), channel_id=1, source_target_pairs={{0,4},{1,5},{2,6},{3,7},{4,0},{5,1},{6,2},{7,3},{8,12},{9,13},{10,... | collective-permute-start | bytes 147464 | tf_op jit(solution)/shard_map/ppermute | solution.py:108
  280.9 3.4 %collective-permute-start.31 = (bf16[32,768]{1,0:T(8,128)(2,1)S(1)}, bf16[32,768]{1,0:T(8,128)(2,1)S(1)}, u32[]{:S(2)}, u32[]{:S(2)}) collective-permute-start(bf16[32,768]{1,0:T(8,128)(2,1)S(1)} %get-tuple-element.87), channel_id=1, source_target_pairs={{0,4},{1,5},{2,6},{3,7},{4,0},{5,1},{6,2},{7,3},{8,12},{9,13},{10,... | collective-permute-start | bytes 147464 | tf_op jit(solution)/shard_map/ppermute | solution.py:108
  284.4 1.6 shard_map.61
  287.0 3.4 %collective-permute-start.23 = (bf16[32,768]{1,0:T(8,128)(2,1)S(1)}, bf16[32,768]{1,0:T(8,128)(2,1)S(1)}, u32[]{:S(2)}, u32[]{:S(2)}) collective-permute-start(bf16[32,768]{1,0:T(8,128)(2,1)S(1)} %get-tuple-element.79), channel_id=1, source_target_pairs={{0,4},{1,5},{2,6},{3,7},{4,0},{5,1},{6,2},{7,3},{8,12},{9,13},{10,... | collective-permute-start | bytes 147464 | tf_op jit(solution)/shard_map/ppermute | solution.py:108
  291.4 1.6 shard_map.58
  293.1 3.5 %collective-permute-start.15 = (bf16[32,768]{1,0:T(8,128)(2,1)S(1)}, bf16[32,768]{1,0:T(8,128)(2,1)S(1)}, u32[]{:S(2)}, u32[]{:S(2)}) collective-permute-start(bf16[32,768]{1,0:T(8,128)(2,1)S(1)} %get-tuple-element.71), channel_id=1, source_target_pairs={{0,4},{1,5},{2,6},{3,7},{4,0},{5,1},{6,2},{7,3},{8,12},{9,13},{10,... | collective-permute-start | bytes 147464 | tf_op jit(solution)/shard_map/ppermute | solution.py:108
  297.6 3.4 %collective-permute-start.7 = (bf16[32,768]{1,0:T(8,128)(2,1)S(1)}, bf16[32,768]{1,0:T(8,128)(2,1)S(1)}, u32[]{:S(2)}, u32[]{:S(2)}) collective-permute-start(bf16[32,768]{1,0:T(8,128)(2,1)S(1)} %get-tuple-element.63), channel_id=1, source_target_pairs={{0,4},{1,5},{2,6},{3,7},{4,0},{5,1},{6,2},{7,3},{8,12},{9,13},{10,... | collective-permute-start | bytes 147464 | tf_op jit(solution)/shard_map/ppermute | solution.py:108
  303.1 3.8 %collective-permute-done.8.refs_3_ = bf16[32,768]{1,0:T(8,128)(2,1)S(1)} collective-permute-done((bf16[32,768]{1,0:T(8,128)(2,1)S(1)}, bf16[32,768]{1,0:T(8,128)(2,1)S(1)}, u32[]{:S(2)}, u32[]{:S(2)}) %collective-permute-start.8) | collective-permute-done | bytes 49184 | tf_op jit(solution)/shard_map/ppermute | solution.py:108
  (80 shorter events, 16.4 us)
Async XLA Ops:
  7.1 94.9 %collective-permute-start = (bf16[3,1536,768]{2,1,0:T(8,128)(2,1)}, bf16[3,1536,768]{2,1,0:T(8,128)(2,1)}, u32[]{:S(2)}, u32[]{:S(2)}) collective-permute-start(bf16[3,1536,768]{2,1,0:T(8,128)(2,1)} %bitcast.3.first), channel_id=1, source_target_pairs={{0,8},{8,0},{16,24},{24,16},{1,9},{9,1},{17,25},{25,17},{2,10},{10... | collective-permute-start | bytes 21233672 | tf_op jit(solution)/shard_map/ppermute | solution.py:108
  7.6 29.4 %collective-permute-start.41 = (bf16[3,1536,128]{2,1,0:T(8,128)(2,1)S(1)}, bf16[3,1536,128]{2,1,0:T(8,128)(2,1)}, u32[]{:S(2)}, u32[]{:S(2)}) collective-permute-start(bf16[3,1536,128]{2,1,0:T(8,128)(2,1)S(1)} %get-tuple-element.105), channel_id=1, source_target_pairs={{0,16},{8,24},{16,0},{24,8},{1,17},{9,25},{17,1},{25,9},{2,18},{10... | collective-permute-start | bytes 3538952 | tf_op jit(solution)/shard_map/ppermute | solution.py:108
  10.0 52.2 %collective-permute-start.33 = (bf16[3,1536,128]{2,1,0:T(8,128)(2,1)S(1)}, bf16[3,1536,128]{2,1,0:T(8,128)(2,1)}, u32[]{:S(2)}, u32[]{:S(2)}) collective-permute-start(bf16[3,1536,128]{2,1,0:T(8,128)(2,1)S(1)} %get-tuple-element.106), channel_id=1, source_target_pairs={{0,16},{8,24},{16,0},{24,8},{1,17},{9,25},{17,1},{25,9},{2,18},{10... | collective-permute-start | bytes 3538952 | tf_op jit(solution)/shard_map/ppermute | solution.py:108
  10.1 77.4 %collective-permute-start.25 = (bf16[3,1536,128]{2,1,0:T(8,128)(2,1)S(1)}, bf16[3,1536,128]{2,1,0:T(8,128)(2,1)}, u32[]{:S(2)}, u32[]{:S(2)}) collective-permute-start(bf16[3,1536,128]{2,1,0:T(8,128)(2,1)S(1)} %get-tuple-element.107), channel_id=1, source_target_pairs={{0,16},{8,24},{16,0},{24,8},{1,17},{9,25},{17,1},{25,9},{2,18},{10... | collective-permute-start | bytes 3538952 | tf_op jit(solution)/shard_map/ppermute | solution.py:108
  12.1 100.6 %collective-permute-start.17 = (bf16[3,1536,128]{2,1,0:T(8,128)(2,1)}, bf16[3,1536,128]{2,1,0:T(8,128)(2,1)S(1)}, u32[]{:S(2)}, u32[]{:S(2)}) collective-permute-start(bf16[3,1536,128]{2,1,0:T(8,128)(2,1)} %get-tuple-element.108), channel_id=1, source_target_pairs={{0,16},{8,24},{16,0},{24,8},{1,17},{9,25},{17,1},{25,9},{2,18},{10... | collective-permute-start | bytes 3538952 | tf_op jit(solution)/shard_map/ppermute | solution.py:108
  37.0 101.0 %collective-permute-start.9 = (bf16[3,1536,128]{2,1,0:T(8,128)(2,1)}, bf16[3,1536,128]{2,1,0:T(8,128)(2,1)S(1)}, u32[]{:S(2)}, u32[]{:S(2)}) collective-permute-start(bf16[3,1536,128]{2,1,0:T(8,128)(2,1)} %get-tuple-element.109), channel_id=1, source_target_pairs={{0,16},{8,24},{16,0},{24,8},{1,17},{9,25},{17,1},{25,9},{2,18},{10... | collective-permute-start | bytes 3538952 | tf_op jit(solution)/shard_map/ppermute | solution.py:108
  62.2 100.8 %collective-permute-start.1 = (bf16[3,1536,128]{2,1,0:T(8,128)(2,1)}, bf16[3,1536,128]{2,1,0:T(8,128)(2,1)S(1)}, u32[]{:S(2)}, u32[]{:S(2)}) collective-permute-start(bf16[3,1536,128]{2,1,0:T(8,128)(2,1)} %slice.24), channel_id=1, source_target_pairs={{0,16},{8,24},{16,0},{24,8},{1,17},{9,25},{17,1},{25,9},{2,18},{10... | collective-permute-start | bytes 3538952 | tf_op jit(solution)/shard_map/ppermute | solution.py:108
  87.5 75.6 %collective-permute-start.42 = (bf16[3,1536,128]{2,1,0:T(8,128)(2,1)}, bf16[3,1536,128]{2,1,0:T(8,128)(2,1)}, u32[]{:S(2)}, u32[]{:S(2)}) collective-permute-start(bf16[3,1536,128]{2,1,0:T(8,128)(2,1)} %collective-permute-done.41.first), channel_id=1, source_target_pairs={{0,8},{8,0},{16,24},{24,16},{1,9},{9,1},{17,25},{25,17},{2,10},{10... | collective-permute-start | bytes 3538952 | tf_op jit(solution)/shard_map/ppermute | solution.py:108
  101.9 84.0 %collective-permute-start.34 = (bf16[3,1536,128]{2,1,0:T(8,128)(2,1)}, bf16[3,1536,128]{2,1,0:T(8,128)(2,1)}, u32[]{:S(2)}, u32[]{:S(2)}) collective-permute-start(bf16[3,1536,128]{2,1,0:T(8,128)(2,1)} %collective-permute-done.33.first), channel_id=1, source_target_pairs={{0,8},{8,0},{16,24},{24,16},{1,9},{9,1},{17,25},{25,17},{2,10},{10... | collective-permute-start | bytes 3538952 | tf_op jit(solution)/shard_map/ppermute | solution.py:108
  112.7 80.9 %collective-permute-start.26 = (bf16[3,1536,128]{2,1,0:T(8,128)(2,1)}, bf16[3,1536,128]{2,1,0:T(8,128)(2,1)}, u32[]{:S(2)}, u32[]{:S(2)}) collective-permute-start(bf16[3,1536,128]{2,1,0:T(8,128)(2,1)} %collective-permute-done.25.first), channel_id=1, source_target_pairs={{0,8},{8,0},{16,24},{24,16},{1,9},{9,1},{17,25},{25,17},{2,10},{10... | collective-permute-start | bytes 3538952 | tf_op jit(solution)/shard_map/ppermute | solution.py:108
  138.0 64.0 %collective-permute-start.18 = (bf16[3,1536,128]{2,1,0:T(8,128)(2,1)S(1)}, bf16[3,1536,128]{2,1,0:T(8,128)(2,1)}, u32[]{:S(2)}, u32[]{:S(2)}) collective-permute-start(bf16[3,1536,128]{2,1,0:T(8,128)(2,1)S(1)} %collective-permute-done.17.first), channel_id=1, source_target_pairs={{0,8},{8,0},{16,24},{24,16},{1,9},{9,1},{17,25},{25,17},{2,10},{10... | collective-permute-start | bytes 3538952 | tf_op jit(solution)/shard_map/ppermute | solution.py:108
  163.1 44.6 %collective-permute-start.10 = (bf16[3,1536,128]{2,1,0:T(8,128)(2,1)S(1)}, bf16[3,1536,128]{2,1,0:T(8,128)(2,1)S(1)}, u32[]{:S(2)}, u32[]{:S(2)}) collective-permute-start(bf16[3,1536,128]{2,1,0:T(8,128)(2,1)S(1)} %collective-permute-done.9.first), channel_id=1, source_target_pairs={{0,8},{8,0},{16,24},{24,16},{1,9},{9,1},{17,25},{25,17},{2,10},{10... | collective-permute-start | bytes 3538952 | tf_op jit(solution)/shard_map/ppermute | solution.py:108
  163.1 45.4 %collective-permute-start.2 = (bf16[3,1536,128]{2,1,0:T(8,128)(2,1)S(1)}, bf16[3,1536,128]{2,1,0:T(8,128)(2,1)S(1)}, u32[]{:S(2)}, u32[]{:S(2)}) collective-permute-start(bf16[3,1536,128]{2,1,0:T(8,128)(2,1)S(1)} %collective-permute-done.1.first), channel_id=1, source_target_pairs={{0,8},{8,0},{16,24},{24,16},{1,9},{9,1},{17,25},{25,17},{2,10},{10... | collective-permute-start | bytes 3538952 | tf_op jit(solution)/shard_map/ppermute | solution.py:108
  185.9 26.1 %collective-permute-start.43 = (bf16[3,32,768]{2,1,0:T(8,128)(2,1)S(1)}, bf16[3,32,768]{2,1,0:T(8,128)(2,1)S(1)}, u32[]{:S(2)}, u32[]{:S(2)}) collective-permute-start(bf16[3,32,768]{2,1,0:T(8,128)(2,1)S(1)} %get-tuple-element.98), channel_id=1, source_target_pairs={{0,2},{1,3},{2,0},{3,1},{4,6},{5,7},{6,4},{7,5},{8,10},{9,11},{10,... | collective-permute-start | bytes 442376 | tf_op jit(solution)/shard_map/ppermute | solution.py:108
  193.6 18.6 %collective-permute-start.44 = (bf16[3,32,768]{2,1,0:T(8,128)(2,1)S(1)}, bf16[3,32,768]{2,1,0:T(8,128)(2,1)S(1)}, u32[]{:S(2)}, u32[]{:S(2)}) collective-permute-start(bf16[3,32,768]{2,1,0:T(8,128)(2,1)S(1)} %get-tuple-element.99), channel_id=1, source_target_pairs={{0,4},{1,5},{2,6},{3,7},{4,0},{5,1},{6,2},{7,3},{8,12},{9,13},{10,... | collective-permute-start | bytes 442376 | tf_op jit(solution)/shard_map/ppermute | solution.py:108
  202.0 10.6 %collective-permute-start.45 = (bf16[3,32,768]{2,1,0:T(8,128)(2,1)S(1)}, bf16[3,32,768]{2,1,0:T(8,128)(2,1)S(1)}, u32[]{:S(2)}, u32[]{:S(2)}) collective-permute-start(bf16[3,32,768]{2,1,0:T(8,128)(2,1)S(1)} %get-tuple-element.100), channel_id=1, source_target_pairs={{0,6},{1,7},{2,4},{3,5},{4,2},{5,3},{6,0},{7,1},{8,14},{9,15},{10,... | collective-permute-start | bytes 442376 | tf_op jit(solution)/shard_map/ppermute | solution.py:108
  207.7 13.7 %collective-permute-start.35 = (bf16[3,32,768]{2,1,0:T(8,128)(2,1)S(1)}, bf16[3,32,768]{2,1,0:T(8,128)(2,1)S(1)}, u32[]{:S(2)}, u32[]{:S(2)}) collective-permute-start(bf16[3,32,768]{2,1,0:T(8,128)(2,1)S(1)} %get-tuple-element.90), channel_id=1, source_target_pairs={{0,2},{1,3},{2,0},{3,1},{4,6},{5,7},{6,4},{7,5},{8,10},{9,11},{10,... | collective-permute-start | bytes 442376 | tf_op jit(solution)/shard_map/ppermute | solution.py:108
  208.5 14.5 %collective-permute-start.36 = (bf16[3,32,768]{2,1,0:T(8,128)(2,1)S(1)}, bf16[3,32,768]{2,1,0:T(8,128)(2,1)S(1)}, u32[]{:S(2)}, u32[]{:S(2)}) collective-permute-start(bf16[3,32,768]{2,1,0:T(8,128)(2,1)S(1)} %get-tuple-element.91), channel_id=1, source_target_pairs={{0,4},{1,5},{2,6},{3,7},{4,0},{5,1},{6,2},{7,3},{8,12},{9,13},{10,... | collective-permute-start | bytes 442376 | tf_op jit(solution)/shard_map/ppermute | solution.py:108
  212.0 11.6 %collective-permute-start.37 = (bf16[3,32,768]{2,1,0:T(8,128)(2,1)S(1)}, bf16[3,32,768]{2,1,0:T(8,128)(2,1)S(1)}, u32[]{:S(2)}, u32[]{:S(2)}) collective-permute-start(bf16[3,32,768]{2,1,0:T(8,128)(2,1)S(1)} %get-tuple-element.92), channel_id=1, source_target_pairs={{0,6},{1,7},{2,4},{3,5},{4,2},{5,3},{6,0},{7,1},{8,14},{9,15},{10,... | collective-permute-start | bytes 442376 | tf_op jit(solution)/shard_map/ppermute | solution.py:108
  212.2 21.6 %collective-permute-start.27 = (bf16[3,32,768]{2,1,0:T(8,128)(2,1)S(1)}, bf16[3,32,768]{2,1,0:T(8,128)(2,1)S(1)}, u32[]{:S(2)}, u32[]{:S(2)}) collective-permute-start(bf16[3,32,768]{2,1,0:T(8,128)(2,1)S(1)} %get-tuple-element.82), channel_id=1, source_target_pairs={{0,2},{1,3},{2,0},{3,1},{4,6},{5,7},{6,4},{7,5},{8,10},{9,11},{10,... | collective-permute-start | bytes 442376 | tf_op jit(solution)/shard_map/ppermute | solution.py:108
  212.6 28.5 %collective-permute-start.28 = (bf16[3,32,768]{2,1,0:T(8,128)(2,1)S(1)}, bf16[3,32,768]{2,1,0:T(8,128)(2,1)S(1)}, u32[]{:S(2)}, u32[]{:S(2)}) collective-permute-start(bf16[3,32,768]{2,1,0:T(8,128)(2,1)S(1)} %get-tuple-element.83), channel_id=1, source_target_pairs={{0,4},{1,5},{2,6},{3,7},{4,0},{5,1},{6,2},{7,3},{8,12},{9,13},{10,... | collective-permute-start | bytes 442376 | tf_op jit(solution)/shard_map/ppermute | solution.py:108
  221.4 24.7 %collective-permute-start.29 = (bf16[3,32,768]{2,1,0:T(8,128)(2,1)S(1)}, bf16[3,32,768]{2,1,0:T(8,128)(2,1)S(1)}, u32[]{:S(2)}, u32[]{:S(2)}) collective-permute-start(bf16[3,32,768]{2,1,0:T(8,128)(2,1)S(1)} %get-tuple-element.84), channel_id=1, source_target_pairs={{0,6},{1,7},{2,4},{3,5},{4,2},{5,3},{6,0},{7,1},{8,14},{9,15},{10,... | collective-permute-start | bytes 442376 | tf_op jit(solution)/shard_map/ppermute | solution.py:108
  222.9 26.7 %collective-permute-start.19 = (bf16[3,32,768]{2,1,0:T(8,128)(2,1)S(1)}, bf16[3,32,768]{2,1,0:T(8,128)(2,1)S(1)}, u32[]{:S(2)}, u32[]{:S(2)}) collective-permute-start(bf16[3,32,768]{2,1,0:T(8,128)(2,1)S(1)} %get-tuple-element.74), channel_id=1, source_target_pairs={{0,2},{1,3},{2,0},{3,1},{4,6},{5,7},{6,4},{7,5},{8,10},{9,11},{10,... | collective-permute-start | bytes 442376 | tf_op jit(solution)/shard_map/ppermute | solution.py:108
  223.6 27.6 %collective-permute-start.20 = (bf16[3,32,768]{2,1,0:T(8,128)(2,1)S(1)}, bf16[3,32,768]{2,1,0:T(8,128)(2,1)S(1)}, u32[]{:S(2)}, u32[]{:S(2)}) collective-permute-start(bf16[3,32,768]{2,1,0:T(8,128)(2,1)S(1)} %get-tuple-element.75), channel_id=1, source_target_pairs={{0,4},{1,5},{2,6},{3,7},{4,0},{5,1},{6,2},{7,3},{8,12},{9,13},{10,... | collective-permute-start | bytes 442376 | tf_op jit(solution)/shard_map/ppermute | solution.py:108
  233.8 19.2 %collective-permute-start.21 = (bf16[3,32,768]{2,1,0:T(8,128)(2,1)S(1)}, bf16[3,32,768]{2,1,0:T(8,128)(2,1)S(1)}, u32[]{:S(2)}, u32[]{:S(2)}) collective-permute-start(bf16[3,32,768]{2,1,0:T(8,128)(2,1)S(1)} %get-tuple-element.76), channel_id=1, source_target_pairs={{0,6},{1,7},{2,4},{3,5},{4,2},{5,3},{6,0},{7,1},{8,14},{9,15},{10,... | collective-permute-start | bytes 442376 | tf_op jit(solution)/shard_map/ppermute | solution.py:108
  241.1 19.9 %collective-permute-start.11 = (bf16[3,32,768]{2,1,0:T(8,128)(2,1)S(1)}, bf16[3,32,768]{2,1,0:T(8,128)(2,1)S(1)}, u32[]{:S(2)}, u32[]{:S(2)}) collective-permute-start(bf16[3,32,768]{2,1,0:T(8,128)(2,1)S(1)} %get-tuple-element.66), channel_id=1, source_target_pairs={{0,2},{1,3},{2,0},{3,1},{4,6},{5,7},{6,4},{7,5},{8,10},{9,11},{10,... | collective-permute-start | bytes 442376 | tf_op jit(solution)/shard_map/ppermute | solution.py:108
  246.2 20.3 %collective-permute-start.12 = (bf16[3,32,768]{2,1,0:T(8,128)(2,1)S(1)}, bf16[3,32,768]{2,1,0:T(8,128)(2,1)S(1)}, u32[]{:S(2)}, u32[]{:S(2)}) collective-permute-start(bf16[3,32,768]{2,1,0:T(8,128)(2,1)S(1)} %get-tuple-element.67), channel_id=1, source_target_pairs={{0,4},{1,5},{2,6},{3,7},{4,0},{5,1},{6,2},{7,3},{8,12},{9,13},{10,... | collective-permute-start | bytes 442376 | tf_op jit(solution)/shard_map/ppermute | solution.py:108
  249.6 16.9 %collective-permute-start.13 = (bf16[3,32,768]{2,1,0:T(8,128)(2,1)S(1)}, bf16[3,32,768]{2,1,0:T(8,128)(2,1)S(1)}, u32[]{:S(2)}, u32[]{:S(2)}) collective-permute-start(bf16[3,32,768]{2,1,0:T(8,128)(2,1)S(1)} %get-tuple-element.68), channel_id=1, source_target_pairs={{0,6},{1,7},{2,4},{3,5},{4,2},{5,3},{6,0},{7,1},{8,14},{9,15},{10,... | collective-permute-start | bytes 442376 | tf_op jit(solution)/shard_map/ppermute | solution.py:108
  251.2 21.3 %collective-permute-start.3 = (bf16[3,32,768]{2,1,0:T(8,128)(2,1)S(1)}, bf16[3,32,768]{2,1,0:T(8,128)(2,1)S(1)}, u32[]{:S(2)}, u32[]{:S(2)}) collective-permute-start(bf16[3,32,768]{2,1,0:T(8,128)(2,1)S(1)} %get-tuple-element.58), channel_id=1, source_target_pairs={{0,2},{1,3},{2,0},{3,1},{4,6},{5,7},{6,4},{7,5},{8,10},{9,11},{10,... | collective-permute-start | bytes 442376 | tf_op jit(solution)/shard_map/ppermute | solution.py:108
  253.1 22.2 %collective-permute-start.4 = (bf16[3,32,768]{2,1,0:T(8,128)(2,1)S(1)}, bf16[3,32,768]{2,1,0:T(8,128)(2,1)S(1)}, u32[]{:S(2)}, u32[]{:S(2)}) collective-permute-start(bf16[3,32,768]{2,1,0:T(8,128)(2,1)S(1)} %get-tuple-element.59), channel_id=1, source_target_pairs={{0,4},{1,5},{2,6},{3,7},{4,0},{5,1},{6,2},{7,3},{8,12},{9,13},{10,... | collective-permute-start | bytes 442376 | tf_op jit(solution)/shard_map/ppermute | solution.py:108
  261.0 14.4 %collective-permute-start.5 = (bf16[3,32,768]{2,1,0:T(8,128)(2,1)S(1)}, bf16[3,32,768]{2,1,0:T(8,128)(2,1)S(1)}, u32[]{:S(2)}, u32[]{:S(2)}) collective-permute-start(bf16[3,32,768]{2,1,0:T(8,128)(2,1)S(1)} %get-tuple-element.60), channel_id=1, source_target_pairs={{0,6},{1,7},{2,4},{3,5},{4,2},{5,3},{6,0},{7,1},{8,14},{9,15},{10,... | collective-permute-start | bytes 442376 | tf_op jit(solution)/shard_map/ppermute | solution.py:108
  266.5 13.5 %collective-permute-start.46 = (bf16[32,768]{1,0:T(8,128)(2,1)S(1)}, bf16[32,768]{1,0:T(8,128)(2,1)S(1)}, u32[]{:S(2)}, u32[]{:S(2)}) collective-permute-start(bf16[32,768]{1,0:T(8,128)(2,1)S(1)} %get-tuple-element.102), channel_id=1, source_target_pairs={{0,2},{1,3},{2,0},{3,1},{4,6},{5,7},{6,4},{7,5},{8,10},{9,11},{10,... | collective-permute-start | bytes 147464 | tf_op jit(solution)/shard_map/ppermute | solution.py:108
  266.5 14.4 %collective-permute-start.47 = (bf16[32,768]{1,0:T(8,128)(2,1)S(1)}, bf16[32,768]{1,0:T(8,128)(2,1)S(1)}, u32[]{:S(2)}, u32[]{:S(2)}) collective-permute-start(bf16[32,768]{1,0:T(8,128)(2,1)S(1)} %get-tuple-element.103), channel_id=1, source_target_pairs={{0,4},{1,5},{2,6},{3,7},{4,0},{5,1},{6,2},{7,3},{8,12},{9,13},{10,... | collective-permute-start | bytes 147464 | tf_op jit(solution)/shard_map/ppermute | solution.py:108
  272.5 8.4 %collective-permute-start.48 = (bf16[32,768]{1,0:T(8,128)(2,1)S(1)}, bf16[32,768]{1,0:T(8,128)(2,1)S(1)}, u32[]{:S(2)}, u32[]{:S(2)}) collective-permute-start(bf16[32,768]{1,0:T(8,128)(2,1)S(1)} %get-tuple-element.104), channel_id=1, source_target_pairs={{0,6},{1,7},{2,4},{3,5},{4,2},{5,3},{6,0},{7,1},{8,14},{9,15},{10,... | collective-permute-start | bytes 147464 | tf_op jit(solution)/shard_map/ppermute | solution.py:108
  275.3 10.7 %collective-permute-start.38 = (bf16[32,768]{1,0:T(8,128)(2,1)S(1)}, bf16[32,768]{1,0:T(8,128)(2,1)S(1)}, u32[]{:S(2)}, u32[]{:S(2)}) collective-permute-start(bf16[32,768]{1,0:T(8,128)(2,1)S(1)} %get-tuple-element.94), channel_id=1, source_target_pairs={{0,2},{1,3},{2,0},{3,1},{4,6},{5,7},{6,4},{7,5},{8,10},{9,11},{10,... | collective-permute-start | bytes 147464 | tf_op jit(solution)/shard_map/ppermute | solution.py:108
  275.4 11.7 %collective-permute-start.39 = (bf16[32,768]{1,0:T(8,128)(2,1)S(1)}, bf16[32,768]{1,0:T(8,128)(2,1)S(1)}, u32[]{:S(2)}, u32[]{:S(2)}) collective-permute-start(bf16[32,768]{1,0:T(8,128)(2,1)S(1)} %get-tuple-element.95), channel_id=1, source_target_pairs={{0,4},{1,5},{2,6},{3,7},{4,0},{5,1},{6,2},{7,3},{8,12},{9,13},{10,... | collective-permute-start | bytes 147464 | tf_op jit(solution)/shard_map/ppermute | solution.py:108
  280.0 7.1 %collective-permute-start.40 = (bf16[32,768]{1,0:T(8,128)(2,1)S(1)}, bf16[32,768]{1,0:T(8,128)(2,1)S(1)}, u32[]{:S(2)}, u32[]{:S(2)}) collective-permute-start(bf16[32,768]{1,0:T(8,128)(2,1)S(1)} %get-tuple-element.96), channel_id=1, source_target_pairs={{0,6},{1,7},{2,4},{3,5},{4,2},{5,3},{6,0},{7,1},{8,14},{9,15},{10,... | collective-permute-start | bytes 147464 | tf_op jit(solution)/shard_map/ppermute | solution.py:108
  280.9 9.6 %collective-permute-start.30 = (bf16[32,768]{1,0:T(8,128)(2,1)S(1)}, bf16[32,768]{1,0:T(8,128)(2,1)S(1)}, u32[]{:S(2)}, u32[]{:S(2)}) collective-permute-start(bf16[32,768]{1,0:T(8,128)(2,1)S(1)} %get-tuple-element.86), channel_id=1, source_target_pairs={{0,2},{1,3},{2,0},{3,1},{4,6},{5,7},{6,4},{7,5},{8,10},{9,11},{10,... | collective-permute-start | bytes 147464 | tf_op jit(solution)/shard_map/ppermute | solution.py:108
  280.9 10.5 %collective-permute-start.31 = (bf16[32,768]{1,0:T(8,128)(2,1)S(1)}, bf16[32,768]{1,0:T(8,128)(2,1)S(1)}, u32[]{:S(2)}, u32[]{:S(2)}) collective-permute-start(bf16[32,768]{1,0:T(8,128)(2,1)S(1)} %get-tuple-element.87), channel_id=1, source_target_pairs={{0,4},{1,5},{2,6},{3,7},{4,0},{5,1},{6,2},{7,3},{8,12},{9,13},{10,... | collective-permute-start | bytes 147464 | tf_op jit(solution)/shard_map/ppermute | solution.py:108
  286.0 7.1 %collective-permute-start.32 = (bf16[32,768]{1,0:T(8,128)(2,1)S(1)}, bf16[32,768]{1,0:T(8,128)(2,1)S(1)}, u32[]{:S(2)}, u32[]{:S(2)}) collective-permute-start(bf16[32,768]{1,0:T(8,128)(2,1)S(1)} %get-tuple-element.88), channel_id=1, source_target_pairs={{0,6},{1,7},{2,4},{3,5},{4,2},{5,3},{6,0},{7,1},{8,14},{9,15},{10,... | collective-permute-start | bytes 147464 | tf_op jit(solution)/shard_map/ppermute | solution.py:108
  287.0 9.6 %collective-permute-start.22 = (bf16[32,768]{1,0:T(8,128)(2,1)S(1)}, bf16[32,768]{1,0:T(8,128)(2,1)S(1)}, u32[]{:S(2)}, u32[]{:S(2)}) collective-permute-start(bf16[32,768]{1,0:T(8,128)(2,1)S(1)} %get-tuple-element.78), channel_id=1, source_target_pairs={{0,2},{1,3},{2,0},{3,1},{4,6},{5,7},{6,4},{7,5},{8,10},{9,11},{10,... | collective-permute-start | bytes 147464 | tf_op jit(solution)/shard_map/ppermute | solution.py:108
  287.0 10.5 %collective-permute-start.23 = (bf16[32,768]{1,0:T(8,128)(2,1)S(1)}, bf16[32,768]{1,0:T(8,128)(2,1)S(1)}, u32[]{:S(2)}, u32[]{:S(2)}) collective-permute-start(bf16[32,768]{1,0:T(8,128)(2,1)S(1)} %get-tuple-element.79), channel_id=1, source_target_pairs={{0,4},{1,5},{2,6},{3,7},{4,0},{5,1},{6,2},{7,3},{8,12},{9,13},{10,... | collective-permute-start | bytes 147464 | tf_op jit(solution)/shard_map/ppermute | solution.py:108
  290.5 7.1 %collective-permute-start.24 = (bf16[32,768]{1,0:T(8,128)(2,1)S(1)}, bf16[32,768]{1,0:T(8,128)(2,1)S(1)}, u32[]{:S(2)}, u32[]{:S(2)}) collective-permute-start(bf16[32,768]{1,0:T(8,128)(2,1)S(1)} %get-tuple-element.80), channel_id=1, source_target_pairs={{0,6},{1,7},{2,4},{3,5},{4,2},{5,3},{6,0},{7,1},{8,14},{9,15},{10,... | collective-permute-start | bytes 147464 | tf_op jit(solution)/shard_map/ppermute | solution.py:108
  291.4 9.6 %collective-permute-start.14 = (bf16[32,768]{1,0:T(8,128)(2,1)S(1)}, bf16[32,768]{1,0:T(8,128)(2,1)S(1)}, u32[]{:S(2)}, u32[]{:S(2)}) collective-permute-start(bf16[32,768]{1,0:T(8,128)(2,1)S(1)} %get-tuple-element.70), channel_id=1, source_target_pairs={{0,2},{1,3},{2,0},{3,1},{4,6},{5,7},{6,4},{7,5},{8,10},{9,11},{10,... | collective-permute-start | bytes 147464 | tf_op jit(solution)/shard_map/ppermute | solution.py:108
  293.1 8.9 %collective-permute-start.15 = (bf16[32,768]{1,0:T(8,128)(2,1)S(1)}, bf16[32,768]{1,0:T(8,128)(2,1)S(1)}, u32[]{:S(2)}, u32[]{:S(2)}) collective-permute-start(bf16[32,768]{1,0:T(8,128)(2,1)S(1)} %get-tuple-element.71), channel_id=1, source_target_pairs={{0,4},{1,5},{2,6},{3,7},{4,0},{5,1},{6,2},{7,3},{8,12},{9,13},{10,... | collective-permute-start | bytes 147464 | tf_op jit(solution)/shard_map/ppermute | solution.py:108
  296.6 5.9 %collective-permute-start.16 = (bf16[32,768]{1,0:T(8,128)(2,1)S(1)}, bf16[32,768]{1,0:T(8,128)(2,1)S(1)}, u32[]{:S(2)}, u32[]{:S(2)}) collective-permute-start(bf16[32,768]{1,0:T(8,128)(2,1)S(1)} %get-tuple-element.72), channel_id=1, source_target_pairs={{0,6},{1,7},{2,4},{3,5},{4,2},{5,3},{6,0},{7,1},{8,14},{9,15},{10,... | collective-permute-start | bytes 147464 | tf_op jit(solution)/shard_map/ppermute | solution.py:108
  297.6 5.5 %collective-permute-start.7 = (bf16[32,768]{1,0:T(8,128)(2,1)S(1)}, bf16[32,768]{1,0:T(8,128)(2,1)S(1)}, u32[]{:S(2)}, u32[]{:S(2)}) collective-permute-start(bf16[32,768]{1,0:T(8,128)(2,1)S(1)} %get-tuple-element.63), channel_id=1, source_target_pairs={{0,4},{1,5},{2,6},{3,7},{4,0},{5,1},{6,2},{7,3},{8,12},{9,13},{10,... | collective-permute-start | bytes 147464 | tf_op jit(solution)/shard_map/ppermute | solution.py:108
  301.0 5.9 %collective-permute-start.8 = (bf16[32,768]{1,0:T(8,128)(2,1)S(1)}, bf16[32,768]{1,0:T(8,128)(2,1)S(1)}, u32[]{:S(2)}, u32[]{:S(2)}) collective-permute-start(bf16[32,768]{1,0:T(8,128)(2,1)S(1)} %get-tuple-element.64), channel_id=1, source_target_pairs={{0,6},{1,7},{2,4},{3,5},{4,2},{5,3},{6,0},{7,1},{8,14},{9,15},{10,... | collective-permute-start | bytes 147464 | tf_op jit(solution)/shard_map/ppermute | solution.py:108
  (4 other events, 26.0 us)

commit v2 on v1

--- a/solution.py
+++ b/solution.py
@@ -129,17 +129,24 @@
 
 
 def norm_kernel(parts, place, tokens, gain, out):
-    width = tokens.shape[1] // parts
-    values = tokens[...].astype(jnp.float32)
-    centre = jnp.mean(values, axis=-1, keepdims=True)
-    centred = values - centre
-    spread = jnp.mean(centred * centred, axis=-1, keepdims=True)
-    scale = lax.rsqrt(spread + norm_eps)
-    for rel in range(parts):
-        start = pl.multiple_of((place[0] ^ rel) * width, LANES)
-        piece = tokens[:, pl.ds(start, width)].astype(jnp.float32)
-        piece = (piece - centre) * scale * gain[:, pl.ds(start, width)]
-        out[:, rel * width : (rel + 1) * width] = piece.astype(jnp.bfloat16)
+    rows, whole = tokens.shape
+    width = whole // parts
+    tile = 16
+
+    def one(index, _):
+        at = pl.ds(pl.multiple_of(index * tile, tile), tile)
+        centre = jnp.mean(tokens[at, :].astype(jnp.float32), axis=-1, keepdims=True)
+        centred = tokens[at, :].astype(jnp.float32) - centre
+        spread = jnp.mean(centred * centred, axis=-1, keepdims=True)
+        scale = lax.rsqrt(spread + norm_eps)
+        for rel in range(parts):
+            start = pl.multiple_of((place[0] ^ rel) * width, LANES)
+            piece = tokens[at, pl.ds(start, width)].astype(jnp.float32)
+            piece = (piece - centre) * scale * gain[:, pl.ds(start, width)]
+            out[at, rel * width : (rel + 1) * width] = piece.astype(jnp.bfloat16)
+        return 0
+
+    lax.fori_loop(0, rows // tile, one, 0, unroll=4)
 
 
 def norm_tokens(place, tokens, gain, parts):
@@ -164,67 +171,173 @@
     return jnp.concatenate([weight[p] for p in range(weight.shape[0])], axis=1)
 
 
-def product(normed, first, second):
+STEPS = 2
+SLOTS = 3
+
+
+def multiply(normed, weights, first, chunk, near, skip, total, rows_in, cols_in, sems):
+    parts = len(weights)
+    kinds, block, lanes = cols_in.shape[1:]
+    steps = parts * STEPS
+    ahead = SLOTS - 1
+
+    def row_copy(step, slot):
+        at = pl.ds(pl.multiple_of((step + skip * STEPS) * block, LANES), block)
+        return pltpu.make_async_copy(normed.at[:, at], rows_in.at[slot], sems.at[0, slot])
+
+    def col_copy(rel, step, slot):
+        at = pl.ds(pl.multiple_of((step - rel * STEPS) * block, LANES), block)
+        kind, lane = (first, chunk * LANES) if rel < near else (0, 0)
+        source = weights[rel].at[pl.ds(kind, kinds), at, pl.ds(lane, lanes)]
+        return pltpu.make_async_copy(source, cols_in.at[slot], sems.at[1, slot])
+
+    def fetch(step, slot):
+        row_copy(step, slot).start()
+        for rel in range(parts):
+
+            @pl.when(step // STEPS == rel)
+            def _():
+                col_copy(rel, step, slot).start()
+
+    def one(step, _):
+        slot = step % SLOTS
+
+        @pl.when(step + ahead < steps)
+        def _():
+            fetch(step + ahead, (step + ahead) % SLOTS)
+
+        row_copy(step, slot).wait()
+        col_copy(parts - 1, (parts - 1) * STEPS, slot).wait()
+        total[...] += jnp.dot(
+            rows_in[slot], wide(cols_in[slot]), preferred_element_type=jnp.float32
+        )
+        return 0
+
+    for step in range(ahead):
+        fetch(jnp.int32(step), step)
+    lax.fori_loop(0, steps, one, 0)
+
+
+def multiply_scratch(rows, depth, kinds, lanes):
+    block = depth // STEPS
+    return [
+        pltpu.VMEM((SLOTS, rows, block), jnp.bfloat16),
+        pltpu.VMEM((SLOTS, kinds, block, lanes), jnp.bfloat16),
+        pltpu.SemaphoreType.DMA((2, SLOTS)),
+    ]
+
+
+def project_kernel(parts, near, skip, chunk, split, quarter, *refs):
+    normed, weights = refs[0], refs[1 : parts + 1]
+    head = parts + 1 + (skip > 0)
+    outs, (total, hold, rows_in, cols_in, sems) = refs[head:-5], refs[-5:]
+    total[...] = refs[parts + 1][...] if skip else jnp.zeros_like(total)
+    multiply(normed, weights, 0, chunk, near, skip, total, rows_in, cols_in, sems)
+    for kind in range(total.shape[1] // LANES):
+        done = total[:, kind * LANES : (kind + 1) * LANES].astype(jnp.bfloat16)
+        (hold if split else outs[0])[kind] = done.T
+    if split:
+        part = LANES // SPLITS
+        for rel, out in enumerate(outs):
+            start = pl.multiple_of((quarter[0] ^ rel) * part, part)
+            out[...] = hold[:, pl.ds(start, part), :]
+
+
+def project(quarter, normed, near, far, chunk, split, begun):
+    rows, _ = normed.shape
+    skip = 0 if begun is None else len(near)
+    weights = far if skip else near + far
+    kinds, depth, _ = far[0].shape
+    cols = kinds * LANES
+    part = LANES // SPLITS if split else LANES
+    count = SPLITS if split else 1
+    total_spec = [pl.BlockSpec((rows, cols), lambda i, s: (0, 0))] if skip else []
+    kernel = functools.partial(
+        project_kernel, len(weights), len(weights) - len(far), skip, chunk, split
+    )
+    return call(
+        kernel,
+        (1,),
+        [pl.BlockSpec(memory_space=pltpu.HBM)] * (len(weights) + 1) + total_spec,
+        [pl.BlockSpec((kinds, part, rows), lambda i, s: (0, 0, 0))] * count,
+        [jax.ShapeDtypeStruct((kinds, part, rows), jnp.bfloat16)] * count,
+        2 * rows * len(weights) * depth * cols,
+        2 * (rows + cols) * len(weights) * depth,
+        1,
+        [
+            pltpu.VMEM((rows, cols), jnp.float32),
+            pltpu.VMEM((kinds, LANES, rows), jnp.bfloat16),
+        ]
+        + multiply_scratch(rows, depth, kinds, LANES),
+    )(quarter, normed, *weights, *([begun] if skip else []))
+
+
+def near_kernel(parts, first, chunk, normed, *refs):
+    weights, (out, total, rows_in, cols_in, sems) = refs[:parts], refs[parts:]
+    total[...] = jnp.zeros_like(total)
+    multiply(normed, weights, first, chunk, parts, 0, total, rows_in, cols_in, sems)
+    out[...] = total[...]
+
+
+def near_sums(normed, near, name, chunk, count):
+    rows, _ = normed.shape
+    parts = len(near)
+    first, last = UNIT_KINDS[name]
+    depth = near[0].shape[1]
+    cols = (last - first) * count * LANES
+    return call(
+        functools.partial(near_kernel, parts, first, chunk),
+        (1,),
+        [pl.BlockSpec(memory_space=pltpu.HBM)] * (parts + 1),
+        pl.BlockSpec((rows, cols), lambda i: (0, 0)),
+        jax.ShapeDtypeStruct((rows, cols), jnp.float32),
+        2 * rows * parts * depth * cols,
+        2 * (rows + cols) * parts * depth,
+        0,
+        [pltpu.VMEM((rows, cols), jnp.float32)]
+        + multiply_scratch(rows, depth, last - first, count * LANES),
+    )(normed, *near)
+
+
+def tail_kernel(total, normed, first, second, *refs):
+    shares, out = refs[:-1], refs[-1]
     depth = first.shape[1]
-    total = jnp.dot(normed[:, :depth], wide(first), preferred_element_type=jnp.float32)
-    return total + jnp.dot(normed[:, depth:], wide(second), preferred_element_type=jnp.float32)
-
-
-def near_kernel(normed, first, second, out):
-    out[...] = product(normed, first, second)
-
-
-def near_product(normed, first, second, chunk):
+    value = total[...]
+    value += jnp.dot(normed[:, :depth], first[0], preferred_element_type=jnp.float32)
+    value += jnp.dot(normed[:, depth:], second[0], preferred_element_type=jnp.float32)
+    value = value.astype(jnp.bfloat16).T
+    part = LANES // SPLITS
+    for index, weights in enumerate(shares):
+        attended = []
+        for head in range(SPLITS):
+            at = index * LANES + head * part
+            term = jnp.dot(
+                value[at : at + part], weights[head], preferred_element_type=jnp.float32
+            )
+            attended.append(term.astype(jnp.bfloat16))
+        out[:, index * LANES : (index + 1) * LANES] = jnp.concatenate(attended, axis=0).T
+
+
+def tail(total, normed, first, second, *shares):
     rows, width = normed.shape
-    kinds, depth, _ = first.shape
-    cols = kinds * LANES
-    return call(
-        near_kernel,
+    depth = first.shape[1]
+    cols = len(shares) * LANES
+    return call(
+        tail_kernel,
         (rows // PATCHES,),
         [
-            pl.BlockSpec((PATCHES, width // 2), lambda i: (i, 0)),
-            pl.BlockSpec((kinds, depth, LANES), lambda i: (0, 0, chunk)),
-            pl.BlockSpec((kinds, depth, LANES), lambda i: (0, 0, chunk)),
-        ],
+            pl.BlockSpec((PATCHES, cols), lambda i: (i, 0)),
+            pl.BlockSpec((PATCHES, width // 2), lambda i: (i, 1)),
+            pl.BlockSpec((1, depth, cols), lambda i: (0, 0, 0)),
+            pl.BlockSpec((1, depth, cols), lambda i: (0, 0, 0)),
+        ]
+        + [pl.BlockSpec((SPLITS, PATCHES, PATCHES), lambda i: (0, 0, i))] * len(shares),
         pl.BlockSpec((PATCHES, cols), lambda i: (i, 0)),
-        jax.ShapeDtypeStruct((rows, cols), jnp.float32),
+        jax.ShapeDtypeStruct((rows, cols), jnp.bfloat16),
         rows * width * cols,
-        rows * width + 2 * cols * width // 2,
+        rows * width + width * cols,
         0,
-    )(normed, first, second)
-
-
-def far_kernel(quarter, total, normed, first, second, out0, out1, out2, out3, hold):
-    done = (total[...] + product(normed, first, second)).astype(jnp.bfloat16)
-    part = hold.shape[1] // SPLITS
-    for kind in range(hold.shape[0]):
-        hold[kind] = done[:, kind * LANES : (kind + 1) * LANES].T
-    for rel, out in enumerate((out0, out1, out2, out3)):
-        start = pl.multiple_of((quarter[0] ^ rel) * part, part)
-        out[...] = hold[:, pl.ds(start, part), :]
-
-
-def far_product(quarter, total, normed, first, second):
-    rows, width = normed.shape
-    kinds, depth, _ = first.shape
-    cols = kinds * LANES
-    part = LANES // SPLITS
-    return call(
-        far_kernel,
-        (rows // PATCHES,),
-        [
-            pl.BlockSpec((PATCHES, cols), lambda i, s: (i, 0)),
-            pl.BlockSpec((PATCHES, width // 2), lambda i, s: (i, 1)),
-            pl.BlockSpec((kinds, depth, LANES), lambda i, s: (0, 0, 0)),
-            pl.BlockSpec((kinds, depth, LANES), lambda i, s: (0, 0, 0)),
-        ],
-        [pl.BlockSpec((kinds, part, PATCHES), lambda i, s: (0, 0, i))] * SPLITS,
-        [jax.ShapeDtypeStruct((kinds, part, rows), jnp.bfloat16)] * SPLITS,
-        rows * width * cols,
-        rows * width + 2 * cols * width // 2,
-        1,
-        [pltpu.VMEM((kinds, LANES, PATCHES), jnp.bfloat16)],
-    )(quarter, total, normed, first, second)
+    )(total, normed, first, second, *shares)
 
 
 def head_layer_norm(values, gain_rows):
@@ -234,33 +347,36 @@
     return centred * lax.rsqrt(spread + norm_eps) * gain_rows
 
 
-def attend_kernel(quarter, in0, in1, in2, in3, q_gain, k_gain, out0, out1, out2, out3):
-    pieces = (in0, in1, in2, in3)
-    part = in0.shape[1]
-
-    def gains(ref):
-        return jnp.concatenate(
-            [
-                ref[pl.ds(pl.multiple_of((quarter[0] ^ rel) * part, part), part), :]
-                for rel in range(SPLITS)
-            ],
-            axis=0,
-        )
-
-    def features(kind):
-        return jnp.concatenate([piece[kind] for piece in pieces], axis=0)
-
-    query = head_layer_norm(features(0).astype(jnp.float32), gains(q_gain))
+def softmax_of(query, key, q_rows, k_rows):
+    query = head_layer_norm(query.astype(jnp.float32), q_rows)
     query = (query * HEAD_DIM ** (-0.5)).astype(jnp.bfloat16)
-    key = head_layer_norm(features(1).astype(jnp.float32), gains(k_gain)).astype(jnp.bfloat16)
+    key = head_layer_norm(key.astype(jnp.float32), k_rows).astype(jnp.bfloat16)
     scores = lax.dot_general(
         key, query, (((0,), (0,)), ((), ())), preferred_element_type=jnp.float32
     )
     raised = jnp.exp(scores)
-    weights = (raised / jnp.sum(raised, axis=0, keepdims=True)).astype(jnp.bfloat16)
-    attended = jnp.dot(features(2), weights, preferred_element_type=jnp.float32)
+    return (raised / jnp.sum(raised, axis=0, keepdims=True)).astype(jnp.bfloat16)
+
+
+def gain_rows(quarter, ref):
+    part = ref.shape[0] // SPLITS
+    rows = []
+    for rel in range(SPLITS):
+        start = pl.multiple_of((quarter[0] ^ rel) * part, part)
+        rows.append(ref[pl.ds(start, part), :])
+    return jnp.concatenate(rows, axis=0)
+
+
+def attend_kernel(quarter, *refs):
+    pieces, (q_gain, k_gain), outs = refs[:SPLITS], refs[SPLITS : SPLITS + 2], refs[-SPLITS:]
+    part = pieces[0].shape[1]
+    query, key, value = (
+        jnp.concatenate([piece[kind] for piece in pieces], axis=0) for kind in range(3)
+    )
+    weights = softmax_of(query, key, gain_rows(quarter, q_gain), gain_rows(quarter, k_gain))
+    attended = jnp.dot(value, weights, preferred_element_type=jnp.float32)
     attended = attended.astype(jnp.bfloat16)
-    for rel, out in enumerate((out0, out1, out2, out3)):
+    for rel, out in enumerate(outs):
         out[...] = attended[rel * part : (rel + 1) * part]
 
 
@@ -280,35 +396,132 @@
     )(quarter, *pieces, q_gain, k_gain)
 
 
-def finish_kernel(quarter, *refs):
+def weigh_kernel(quarter, *refs):
+    pieces, (q_gain, k_gain), out = refs[:SPLITS], refs[SPLITS : SPLITS + 2], refs[-1]
+    part = HEAD_DIM // SPLITS
+    q_rows, k_rows = gain_rows(quarter, q_gain), gain_rows(quarter, k_gain)
+    for head in range(SPLITS):
+        query, key = (
+            jnp.concatenate(
+                [piece[kind, head * part : (head + 1) * part] for piece in pieces], axis=0
+            )
+            for kind in range(2)
+        )
+        out[head] = softmax_of(query, key, q_rows, k_rows)
+
+
+def weigh(quarter, pieces, q_gain, k_gain):
+    kinds, lanes, rows = pieces[0].shape
+    gain_spec = pl.BlockSpec((HEAD_DIM, PATCHES), lambda i, s: (0, 0))
+    return call(
+        weigh_kernel,
+        (rows // PATCHES,),
+        [pl.BlockSpec((kinds, lanes, PATCHES), lambda i, s: (0, 0, i))] * SPLITS
+        + [gain_spec, gain_spec],
+        pl.BlockSpec((SPLITS, PATCHES, PATCHES), lambda i, s: (0, 0, i)),
+        jax.ShapeDtypeStruct((SPLITS, PATCHES, rows), jnp.bfloat16),
+        rows * PATCHES * HEAD_DIM * 80,
+        rows * HEAD_DIM * 32,
+        1,
+    )(quarter, *pieces, q_gain, k_gain)
+
+
+def finish_kernel(early, quarter, *refs):
     out, hold = refs[-2:]
-    pieces = refs[:-2]
+    pieces, tails = refs[: early * SPLITS], refs[early * SPLITS : -2]
     part = pieces[0].shape[0]
-    for chunk in range(len(pieces) // SPLITS):
+    for chunk in range(early):
         for rel in range(SPLITS):
             start = pl.multiple_of((quarter[0] ^ rel) * part, part)
             hold[pl.ds(start, part), :] = pieces[chunk * SPLITS + rel][...]
         out[:, chunk * LANES : (chunk + 1) * LANES] = hold[...].T
-
-
-def finish(quarter, pieces):
+    out[:, early * LANES :] = tails[0][...]
+
+
+def finish(quarter, pieces, tails):
     part, rows = pieces[0].shape
-    width = part * len(pieces)
-    return call(
-        finish_kernel,
+    early = len(pieces) // SPLITS
+    width = early * LANES + tails[0].shape[1]
+    return call(
+        functools.partial(finish_kernel, early),
         (1,),
-        [pl.BlockSpec((part, rows), lambda i, s: (0, 0))] * len(pieces),
+        [pl.BlockSpec((part, rows), lambda i, s: (0, 0))] * len(pieces)
+        + [pl.BlockSpec(tails[0].shape, lambda i, s: (0, 0))],
         pl.BlockSpec((rows, width), lambda i, s: (0, 0)),
         jax.ShapeDtypeStruct((rows, width), jnp.bfloat16),
         rows * width * 100,
         rows * width * 4,
         1,
         [pltpu.VMEM((LANES, rows), jnp.bfloat16)],
-    )(quarter, *pieces)
+    )(quarter, *pieces, *tails)
 
 
 def after(value, *others):
     return lax.optimization_barrier((value, *others))[0]
+
+
+UNIT_KINDS = {"all": (0, 3), "pair": (0, 2), "value": (2, 3)}
+
+
+def sequence(chunks):
+    early = chunks - chunks // 2
+    pairs = [("pair", c, 1) for c in range(early, chunks)]
+    units = []
+    for c in range(early - 1):
+        units += [("all", c, 1)] + pairs[c : c + 1]
+    units += pairs[early - 1 :] + [("all", early - 1, 1)]
+    return units + [("value", early, chunks - early)]
+
+
+def exchange(values, groups):
+    return [values[0]] + [swap(values[rel], "mp", rel * groups) for rel in range(1, SPLITS)]
+
+
+def gather(own, groups):
+    beside = swap(own, "mp", groups)
+    far = swap(own, "mp", 3 * groups)
+    middle = swap(far, "mp", groups)
+    return [own, beside, middle, far]
+
+
+def cut_kernel(units, source, *outs):
+    kind = pl.program_id(0)
+    for (name, chunk, count), out in zip(units, outs):
+        first, last = UNIT_KINDS[name]
+
+        @pl.when((kind >= first) & (kind < last))
+        def _():
+            out[...] = source[:, :, chunk * LANES : (chunk + count) * LANES]
+
+
+def cut(weight, units):
+    kinds, depth, width = weight.shape
+    blocks = 2
+    block = depth // blocks
+
+    def spec(name, _, count):
+        first, last = UNIT_KINDS[name]
+
+        def place(kind, index):
+            at = jnp.where(kind < first, 0, jnp.where(kind < last, index, blocks - 1))
+            return jnp.clip(kind - first, 0, last - first - 1), at, 0
+
+        return pl.BlockSpec((1, block, count * LANES), place)
+
+    def shape(name, _, count):
+        first, last = UNIT_KINDS[name]
+        return jax.ShapeDtypeStruct((last - first, depth, count * LANES), weight.dtype)
+
+    return call(
+        functools.partial(cut_kernel, units),
+        (kinds, blocks),
+        [pl.BlockSpec((1, block, width), lambda kind, index: (kind, index, 0))],
+        [spec(*unit) for unit in units],
+        [shape(*unit) for unit in units],
+        weight.size * 500,
+        weight.size * 4,
+        0,
+    )(weight)
 
 
 def chunked_body(tokens, ln_gain, w_qkv, q_gain, k_gain):
@@ -317,27 +530,35 @@
     place = lax.axis_index("dp").astype(jnp.int32)[None]
     quarter = (lax.axis_index("mp") // groups).astype(jnp.int32)[None]
     weight = jnp.transpose(w_qkv, (1, 0, 2))
-    chunks = weight.shape[2] // LANES
+    units = sequence(weight.shape[2] // LANES)
     slices = [weight[:, :, :LANES]]
-    rest = after(weight, slices[0])
-    slices += [rest[:, :, c * LANES : (c + 1) * LANES] for c in range(1, chunks)]
-    beside = [swap(slices[c], "dp", 2) for c in range(chunks)]
+    slices += cut(after(weight, slices[0]), units[1:])
+    beside = [swap(slices[n], "dp", 2) for n in range(len(units))]
     paired = swap(after(weight, slices[1]), "dp", 1)
     normed = norm_tokens(place, tokens, ln_gain, parts)
     wide_q = jnp.broadcast_to(q_gain[:, None], (HEAD_DIM, PATCHES))
     wide_k = jnp.broadcast_to(k_gain[:, None], (HEAD_DIM, PATCHES))
-    returned = []
-    for c in range(chunks):
-        total = near_product(normed, weight, paired, c)
-        across = swap(beside[c], "dp", 1)
-        pieces = far_product(quarter, total, normed, beside[c], across)
-        moved = [pieces[0]] + [swap(pieces[rel], "mp", rel * groups) for rel in range(1, SPLITS)]
-        results = attend(quarter, moved, wide_q, wide_k)
-        returned += [results[0]] + [
-            swap(results[rel], "mp", rel * groups)
-            for rel in range(1, SPLITS)
-        ]
-    return finish(quarter, returned)
+    near = (weight, paired)
+    returned, tails, shares = [], [], []
+    for n, (kind, chunk, count) in enumerate(units):
+        across = swap(beside[n], "dp", 1)
+        far = (beside[n], across)
+        begun = None
+        if n >= len(units) - 2:
+            begun = near_sums(normed, near, kind, chunk, count)
+        if kind == "value":
+            tails.append(tail(begun, normed, *far, *shares))
+            continue
+        split = kind == "all"
+        pieces = project(quarter, normed, near, far, chunk, split, begun)
+        if split:
+            moved = exchange(pieces, groups)
+            results = attend(quarter, moved, wide_q, wide_k)
+            returned += exchange(results, groups)
+        else:
+            moved = gather(pieces[0], groups)
+            shares.append(weigh(quarter, moved, wide_q, wide_k))
+    return finish(quarter, returned, tails)
 
 
 def body(tokens, ln_gain, w_qkv, q_gain, k_gain):

time: 309 us -> 328 us (1.061)
  waiting for transfers between devices: 128 us -> 143 us
  starting transfers between devices: 81 us -> 87.8 us
    ppermute x49 -> x42, waiting for transfers between devices: 128 us -> 143 us  [swap(): return lax.ppermute(value, axis, [(i, i ^ mask) for i in range(length)])]
    ppermute x49 -> x42, starting transfers between devices: 81 us -> 87.8 us  [swap(): return lax.ppermute(value, axis, [(i, i ^ mask) for i in range(length)])]
    unnamed x6 -> x24, local copies, waits for them, and re-layouts: 0.75 us -> 6.02 us
    pallas_call x6 -> x3, Pallas kernels: 9.92 us -> 4.97 us  [attend(): call(attend_kernel, (rows // PATCHES,), [pl.BlockSpec((kinds, part, PATCH...]
    slice x1 -> x0, local copies, waits for them, and re-layouts: 4.7 us -> none  [chunked_body(): slices += [rest[:, :, c * LANES:(c + 1) * LANES] for c in range(1, chunks)]]
    pallas_call x13 -> x14, Pallas kernels: 67.4 us -> 71.2 us  [the longest x6 40.9 us: project(): call(kernel, (1,), [pl.BlockSpec(memory_space=pltpu.HBM)] * (len(weights)...]
  transfers between devices with their start and end apart: 49 -> 42, of which waited for: 12 -> 8; matrix products, arithmetic and copies ran while one was open for 0% -> 0% of each run, Pallas kernels for 29% -> 25%
where the time goes in v2:
time: 328 us; the launch traced here: 327 us
  waiting for transfers between devices  143 us (44%)
  Pallas kernels  88.5 us (27%)
  starting transfers between devices  87.8 us (27%)
  local copies, waits for them, and re-layouts  7.53 us (2%)
    ppermute x42, waiting for transfers between devices, swap(): return lax.ppermute(value, axis, [(i, i ^ mask) for i in range(length)])  143 us
    ppermute x42, starting transfers between devices, swap(): return lax.ppermute(value, axis, [(i, i ^ mask) for i in range(length)])  87.8 us
    pallas_call x6, Pallas kernels, project(): call(kernel, (1,), [pl.BlockSpec(memory_space=pltpu.HBM)] * (len(weights)...  40.9 us
    pallas_call x1, Pallas kernels, norm_tokens(): call(functools.partial(norm_kernel, parts), (rows // block,), [pl.BlockSp...  12.4 us
    pallas_call x2, Pallas kernels, near_sums(): call(functools.partial(near_kernel, parts, first, chunk), (1,), [pl.Block...  9.51 us
    pallas_call x3, Pallas kernels, weigh(): call(weigh_kernel, (rows // PATCHES,), [pl.BlockSpec((kinds, lanes, PATCH...  6.82 us
  transfers between devices with their start and end apart: 42, of which 8 were waited for; matrix products, arithmetic and copies ran while one was open for 0% of the time, Pallas kernels for 25%

profile of v2, /device:TPU:0, one launch (start us, length us, event | category | flops | bytes accessed | tf_op | source)
XLA Modules:
  0.0 327.4 jit_solution(874840800404576371)
XLA Ops:
  0.0 1.3 slice.4
  1.4 6.5 %shard_map.56 = (bf16[2,1536,128]{2,1,0:T(8,128)(2,1)S(1)}, bf16[3,1536,128]{2,1,0:T(8,128)(2,1)}, bf16[2,1536,128]{2,1,0:T(8,128)(2,1)S(1)}, bf16[2,1536,128]{2...) custom-call(bf16[3,1536,768]{2,1,0:T(8,128)(2,1)} %bitcast.3.source.refs_1_.refs_0_), custom_call_target="tpu_custom_call" | custom-call | flops 1769472000 | bytes 14155776 | tf_op jit(solution)/shard_map/pallas_call | solution.py:515
  9.4 2.5 collective-permute-start.1
  11.9 2.0 collective-permute-start.32
  13.9 41.6 %collective-permute-done.27.refs_3_ = bf16[2,1536,128]{2,1,0:T(8,128)(2,1)S(1)} collective-permute-done((bf16[2,1536,128]{2,1,0:T(8,128)(2,1)S(1)}, bf16[2,1536,128]{2,1,0:T(8,128)(2,1)S(1)}, u32[]{:S(2)}, u32[]{:S(2)}) %collective-permute-start.27) | collective-permute-done | bytes 786464 | tf_op jit(solution)/shard_map/ppermute | solution.py:108
  55.6 2.0 collective-permute-start.17
  57.6 14.8 %collective-permute-done.32.refs_3_ = bf16[2,1536,128]{2,1,0:T(8,128)(2,1)S(1)} collective-permute-done((bf16[2,1536,128]{2,1,0:T(8,128)(2,1)S(1)}, bf16[2,1536,128]{2,1,0:T(8,128)(2,1)S(1)}, u32[]{:S(2)}, u32[]{:S(2)}) %collective-permute-start.32) | collective-permute-done | bytes 786464 | tf_op jit(solution)/shard_map/ppermute | solution.py:108
  73.3 2.0 collective-permute-start.37
  75.3 64.3 %collective-permute-done.37.refs_3_ = bf16[2,1536,128]{2,1,0:T(8,128)(2,1)S(1)} collective-permute-done((bf16[2,1536,128]{2,1,0:T(8,128)(2,1)}, bf16[2,1536,128]{2,1,0:T(8,128)(2,1)S(1)}, u32[]{:S(2)}, u32[]{:S(2)}) %collective-permute-start.37) | collective-permute-done | bytes 786464 | tf_op jit(solution)/shard_map/ppermute | solution.py:108
  140.6 1.7 collective-permute-start.25
  143.7 12.4 %shard_map.55.refs_0_.normed = bf16[768,6144]{1,0:T(8,128)(2,1)} custom-call(s32[1]{0:T(128)} %bitcast.1.place, bf16[768,6144]{1,0:T(8,128)(2,1)} %tokens.1, f32[1,6144]{1,0:T(1,128)S(1)} %bitcast.4), custom_call_target="tpu_custom_call" | custom-call | flops 5662310400 | bytes 18874368 | tf_op jit(solution)/shard_map/pallas_call | solution.py:155
  156.5 8.2 %shard_map.57 = (bf16[3,32,768]{2,1,0:T(8,128)(2,1)S(1)}, bf16[3,32,768]{2,1,0:T(8,128)(2,1)S(1)}, bf16[3,32,768]{2,1,0:T(8,128)(2,1)S(1)}, bf16[3,32,768]{2,1,0:T(8,128)(2,1)S(1)}) custom-call(s32[1]{0:T(128)} %bitcast.quarter, bf16[768,6144]{1,0:T(8,128)(2,1)} %shard_map.55.refs_0_.normed, bf16[3,1536,768]{2,1,0:T(8,128)(2,1)} %bitcast.3.source.refs_1_.refs_0_, ...), custom_call_target="tpu_custom_call" | custom-call | flops 3623878656 | bytes 14155776 | tf_op jit(solution)/shard_map/pallas_call | solution.py:258
  164.9 4.8 %shard_map.61.refs_3_ = f32[768,384]{1,0:T(8,128)S(1)} custom-call(bf16[768,6144]{1,0:T(8,128)(2,1)} %shard_map.55.refs_0_.normed, bf16[3,1536,768]{2,1,0:T(8,128)(2,1)} %bitcast.3.source.refs_1_.refs_0_, bf16[3,1536,768]{2,1,0:T(8,128)(2,1)} %collective-permute-done.refs_2_.refs_1_), custom_call_target="tpu_custom_call" | custom-call | flops 1811939328 | bytes 7077888 | tf_op jit(solution)/shard_map/pallas_call | solution.py:288
  169.7 6.5 %shard_map.65.refs_0_ = bf16[2,128,768]{2,1,0:T(8,128)(2,1)S(1)} custom-call(s32[1]{0:T(128)} %bitcast.quarter, bf16[768,6144]{1,0:T(8,128)(2,1)} %shard_map.55.refs_0_.normed, bf16[3,1536,768]{2,1,0:T(8,128)(2,1)} %bitcast.3.source.refs_1_.refs_0_, bf16[3,1536,768]{2,1,0:T(8,128)(2,1)} %collective-permute-done.refs_2_.refs_1_, ...), custom_call_target="tpu_custom_call" | custom-call | flops 2415919104 | bytes 12582912 | tf_op jit(solution)/shard_map/pallas_call | solution.py:258
  176.3 1.6 collective-permute-start.3
  177.9 8.3 %shard_map.59 = (bf16[3,32,768]{2,1,0:T(8,128)(2,1)S(1)}, bf16[3,32,768]{2,1,0:T(8,128)(2,1)S(1)}, bf16[3,32,768]{2,1,0:T(8,128)(2,1)S(1)}, bf16[3,32,768]{2,1,0:T(8,128)(2,1)S(1)}) custom-call(s32[1]{0:T(128)} %bitcast.quarter, bf16[768,6144]{1,0:T(8,128)(2,1)} %shard_map.55.refs_0_.normed, bf16[3,1536,768]{2,1,0:T(8,128)(2,1)} %bitcast.3.source.refs_1_.refs_0_, ...), custom_call_target="tpu_custom_call" | custom-call | flops 3623878656 | bytes 14155776 | tf_op jit(solution)/shard_map/pallas_call | solution.py:258
  186.2 2.7 collective-permute-start.4
  189.8 4.8 %shard_map.62 = (bf16[3,32,768]{2,1,0:T(8,128)(2,1)S(1)}, bf16[3,32,768]{2,1,0:T(8,128)(2,1)S(1)}, bf16[3,32,768]{2,1,0:T(8,128)(2,1)S(1)}, bf16[3,32,768]{2,1,0:T(8,128)(2,1)S(1)}) custom-call(s32[1]{0:T(128)} %bitcast.quarter, bf16[768,6144]{1,0:T(8,128)(2,1)} %shard_map.55.refs_0_.normed, bf16[3,1536,128]{2,1,0:T(8,128)(2,1)S(1)} %collective-permute-done.17.refs_1_, ...), custom_call_target="tpu_custom_call" | custom-call | flops 1811939328 | bytes 7077888 | tf_op jit(solution)/shard_map/pallas_call | solution.py:258
  194.6 3.6 %collective-permute-start.12 = (bf16[3,32,768]{2,1,0:T(8,128)(2,1)S(1)}, bf16[3,32,768]{2,1,0:T(8,128)(2,1)S(1)}, u32[]{:S(2)}, u32[]{:S(2)}) collective-permute-start(bf16[3,32,768]{2,1,0:T(8,128)(2,1)S(1)} %get-tuple-element.51), channel_id=1, source_target_pairs={{0,4},{1,5},{2,6},{3,7},{4,0},{5,1},{6,2},{7,3},{8,12},{9,13},{10,... | collective-permute-start | bytes 442376 | tf_op jit(solution)/shard_map/ppermute | solution.py:108
  198.4 2.0 collective-permute-done.4.refs_2_
  200.4 10.9 %collective-permute-start.20 = (bf16[3,32,768]{2,1,0:T(8,128)(2,1)S(1)}, bf16[3,32,768]{2,1,0:T(8,128)(2,1)S(1)}, u32[]{:S(2)}, u32[]{:S(2)}) collective-permute-start(bf16[3,32,768]{2,1,0:T(8,128)(2,1)S(1)} %get-tuple-element.60), channel_id=1, source_target_pairs={{0,4},{1,5},{2,6},{3,7},{4,0},{5,1},{6,2},{7,3},{8,12},{9,13},{10,... | collective-permute-start | bytes 442376 | tf_op jit(solution)/shard_map/ppermute | solution.py:108
  211.8 6.5 %shard_map.67.refs_0_ = bf16[2,128,768]{2,1,0:T(8,128)(2,1)S(1)} custom-call(s32[1]{0:T(128)} %bitcast.quarter, bf16[768,6144]{1,0:T(8,128)(2,1)} %shard_map.55.refs_0_.normed, bf16[3,1536,768]{2,1,0:T(8,128)(2,1)} %bitcast.3.source.refs_1_.refs_0_, bf16[3,1536,768]{2,1,0:T(8,128)(2,1)} %collective-permute-done.refs_2_.refs_1_, ...), custom_call_target="tpu_custom_call" | custom-call | flops 2415919104 | bytes 12582912 | tf_op jit(solution)/shard_map/pallas_call | solution.py:258
  218.4 8.9 %collective-permute-start.29 = (bf16[2,128,768]{2,1,0:T(8,128)(2,1)S(1)}, bf16[2,128,768]{2,1,0:T(8,128)(2,1)S(1)}, u32[]{:S(2)}, u32[]{:S(2)}) collective-permute-start(bf16[2,128,768]{2,1,0:T(8,128)(2,1)S(1)} %shard_map.65.refs_0_), channel_id=1, source_target_pairs={{0,2},{1,3},{2,0},{3,1},{4,6},{5,7},{6,4},{7,5},{8,10},{9,11},{10,... | collective-permute-start | bytes 1179656 | tf_op jit(solution)/shard_map/ppermute | solution.py:108
  227.3 3.4 %collective-permute-start.21 = (bf16[3,32,768]{2,1,0:T(8,128)(2,1)S(1)}, bf16[3,32,768]{2,1,0:T(8,128)(2,1)S(1)}, u32[]{:S(2)}, u32[]{:S(2)}) collective-permute-start(bf16[3,32,768]{2,1,0:T(8,128)(2,1)S(1)} %get-tuple-element.61), channel_id=1, source_target_pairs={{0,6},{1,7},{2,4},{3,5},{4,2},{5,3},{6,0},{7,1},{8,14},{9,15},{10,... | collective-permute-start | bytes 442376 | tf_op jit(solution)/shard_map/ppermute | solution.py:108
  230.7 2.6 collective-permute-start.35
  233.3 6.5 %shard_map.69.refs_0_ = bf16[2,128,768]{2,1,0:T(8,128)(2,1)S(1)} custom-call(s32[1]{0:T(128)} %bitcast.quarter, bf16[768,6144]{1,0:T(8,128)(2,1)} %shard_map.55.refs_0_.normed, bf16[3,1536,768]{2,1,0:T(8,128)(2,1)} %bitcast.3.source.refs_1_.refs_0_, bf16[3,1536,768]{2,1,0:T(8,128)(2,1)} %collective-permute-done.refs_2_.refs_1_, ...), custom_call_target="tpu_custom_call" | custom-call | flops 2415919104 | bytes 12582912 | tf_op jit(solution)/shard_map/pallas_call | solution.py:258
  239.9 4.0 %collective-permute-done.21.refs_3_ = bf16[3,32,768]{2,1,0:T(8,128)(2,1)S(1)} collective-permute-done((bf16[3,32,768]{2,1,0:T(8,128)(2,1)S(1)}, bf16[3,32,768]{2,1,0:T(8,128)(2,1)S(1)}, u32[]{:S(2)}, u32[]{:S(2)}) %collective-permute-start.21) | collective-permute-done | bytes 147488 | tf_op jit(solution)/shard_map/ppermute | solution.py:108
  244.4 20.2 %collective-permute-start.31 = (bf16[2,128,768]{2,1,0:T(8,128)(2,1)S(1)}, bf16[2,128,768]{2,1,0:T(8,128)(2,1)S(1)}, u32[]{:S(2)}, u32[]{:S(2)}) collective-permute-start(bf16[2,128,768]{2,1,0:T(8,128)(2,1)S(1)} %collective-permute-done.30.refs_3_), channel_id=1, source_target_pairs={{0,2},{1,3},{2,0},{3,1},{4,6},{5,7},{6,4},{7,5},{8,10},{9,11},{10,... | collective-permute-start | bytes 1179656 | tf_op jit(solution)/shard_map/ppermute | solution.py:108
  264.6 4.7 %shard_map.64.total = f32[768,384]{1,0:T(8,128)S(1)} custom-call(bf16[768,6144]{1,0:T(8,128)(2,1)} %shard_map.55.refs_0_.normed, bf16[3,1536,768]{2,1,0:T(8,128)(2,1)} %bitcast.3.source.refs_1_.refs_0_, bf16[3,1536,768]{2,1,0:T(8,128)(2,1)} %collective-permute-done.refs_2_.refs_1_), custom_call_target="tpu_custom_call" | custom-call | flops 1811939328 | bytes 7077888 | tf_op jit(solution)/shard_map/pallas_call | solution.py:288
  269.4 2.0 collective-permute-start.36
  271.6 1.7 shard_map.58
  273.3 1.7 shard_map.60
  275.0 3.9 %collective-permute-start.39 = (bf16[2,128,768]{2,1,0:T(8,128)(2,1)S(1)}, bf16[2,128,768]{2,1,0:T(8,128)(2,1)S(1)}, u32[]{:S(2)}, u32[]{:S(2)}) collective-permute-start(bf16[2,128,768]{2,1,0:T(8,128)(2,1)S(1)} %shard_map.69.refs_0_), channel_id=1, source_target_pairs={{0,2},{1,3},{2,0},{3,1},{4,6},{5,7},{6,4},{7,5},{8,10},{9,11},{10,... | collective-permute-start | bytes 1179656 | tf_op jit(solution)/shard_map/ppermute | solution.py:108
  278.9 1.6 shard_map.63
  280.6 2.3 shard_map.66.refs_0_
  282.9 2.2 collective-permute-start.6
  285.0 6.5 %collective-permute-done.36.refs_2_ = bf16[2,128,768]{2,1,0:T(8,128)(2,1)S(1)} collective-permute-done((bf16[2,128,768]{2,1,0:T(8,128)(2,1)S(1)}, bf16[2,128,768]{2,1,0:T(8,128)(2,1)S(1)}, u32[]{:S(2)}, u32[]{:S(2)}) %collective-permute-start.36) | collective-permute-done | bytes 393248 | tf_op jit(solution)/shard_map/ppermute | solution.py:108
  291.5 1.3 collective-permute-start.7
  292.9 2.3 shard_map.68.refs_1_
  296.3 4.2 %collective-permute-done.39.refs_1_ = bf16[2,128,768]{2,1,0:T(8,128)(2,1)S(1)} collective-permute-done((bf16[2,128,768]{2,1,0:T(8,128)(2,1)S(1)}, bf16[2,128,768]{2,1,0:T(8,128)(2,1)S(1)}, u32[]{:S(2)}, u32[]{:S(2)}) %collective-permute-start.39) | collective-permute-done | bytes 393248 | tf_op jit(solution)/shard_map/ppermute | solution.py:108
  300.5 1.3 collective-permute-start.8
  301.8 5.5 %collective-permute-done.41.refs_2_ = bf16[2,128,768]{2,1,0:T(8,128)(2,1)S(1)} collective-permute-done((bf16[2,128,768]{2,1,0:T(8,128)(2,1)S(1)}, bf16[2,128,768]{2,1,0:T(8,128)(2,1)S(1)}, u32[]{:S(2)}, u32[]{:S(2)}) %collective-permute-start.41) | collective-permute-done | bytes 393248 | tf_op jit(solution)/shard_map/ppermute | solution.py:108
  307.3 2.3 collective-permute-start.14
  309.5 2.3 shard_map.70.refs_2_
  313.9 1.6 collective-permute-start.16
  316.6 1.7 collective-permute-start.23
  318.3 1.6 collective-permute-start.24
  319.8 6.2 %shard_map.71.refs_12_ = bf16[768,384]{1,0:T(8,128)(2,1)S(1)} custom-call(f32[768,384]{1,0:T(8,128)S(1)} %shard_map.64.total, bf16[768,6144]{1,0:T(8,128)(2,1)} %shard_map.55.refs_0_.normed, bf16[1,1536,384]{2,1,0:T(8,128)(2,1)S(1)} %collective-permute-done.25.first, bf16[1,1536,384]{2,1,0:T(8,128)(2,1)S(1)} %collective-permute-done.26.second, ...), custom_call_target="tpu_custom_call" | custom-call | flops 1811939328 | bytes 7077888 | tf_op jit(solution)/shard_map/pallas_call | solution.py:325
  (81 shorter events, 13.3 us)
Async XLA Ops:
  8.9 147.1 %collective-permute-start = (bf16[3,1536,768]{2,1,0:T(8,128)(2,1)}, bf16[3,1536,768]{2,1,0:T(8,128)(2,1)}, u32[]{:S(2)}, u32[]{:S(2)}) collective-permute-start(bf16[3,1536,768]{2,1,0:T(8,128)(2,1)} %bitcast.3.source.refs_1_.refs_0_), channel_id=1, source_target_pairs={{0,8},{8,0},{16,24},{24,16},{1,9},{9,1},{17,25},{25,17},{2,10},{10... | collective-permute-start | bytes 21233672 | tf_op jit(solution)/shard_map/ppermute | solution.py:108
  9.4 48.2 %collective-permute-start.1 = (bf16[3,1536,128]{2,1,0:T(8,128)(2,1)S(1)}, bf16[3,1536,128]{2,1,0:T(8,128)(2,1)}, u32[]{:S(2)}, u32[]{:S(2)}) collective-permute-start(bf16[3,1536,128]{2,1,0:T(8,128)(2,1)S(1)} %slice.4), channel_id=1, source_target_pairs={{0,16},{8,24},{16,0},{24,8},{1,17},{9,25},{17,1},{25,9},{2,18},{10... | collective-permute-start | bytes 3538952 | tf_op jit(solution)/shard_map/ppermute | solution.py:108
  11.9 43.7 %collective-permute-start.27 = (bf16[2,1536,128]{2,1,0:T(8,128)(2,1)S(1)}, bf16[2,1536,128]{2,1,0:T(8,128)(2,1)S(1)}, u32[]{:S(2)}, u32[]{:S(2)}) collective-permute-start(bf16[2,1536,128]{2,1,0:T(8,128)(2,1)S(1)} %get-tuple-element.38), channel_id=1, source_target_pairs={{0,16},{8,24},{16,0},{24,8},{1,17},{9,25},{17,1},{25,9},{2,18},{10... | collective-permute-start | bytes 2359304 | tf_op jit(solution)/shard_map/ppermute | solution.py:108
  11.9 60.5 %collective-permute-start.32 = (bf16[2,1536,128]{2,1,0:T(8,128)(2,1)S(1)}, bf16[2,1536,128]{2,1,0:T(8,128)(2,1)S(1)}, u32[]{:S(2)}, u32[]{:S(2)}) collective-permute-start(bf16[2,1536,128]{2,1,0:T(8,128)(2,1)S(1)} %get-tuple-element.67), channel_id=1, source_target_pairs={{0,16},{8,24},{16,0},{24,8},{1,17},{9,25},{17,1},{25,9},{2,18},{10... | collective-permute-start | bytes 2359304 | tf_op jit(solution)/shard_map/ppermute | solution.py:108
  13.9 128.4 %collective-permute-start.9 = (bf16[3,1536,128]{2,1,0:T(8,128)(2,1)}, bf16[3,1536,128]{2,1,0:T(8,128)(2,1)S(1)}, u32[]{:S(2)}, u32[]{:S(2)}) collective-permute-start(bf16[3,1536,128]{2,1,0:T(8,128)(2,1)} %get-tuple-element.48), channel_id=1, source_target_pairs={{0,16},{8,24},{16,0},{24,8},{1,17},{9,25},{17,1},{25,9},{2,18},{10... | collective-permute-start | bytes 3538952 | tf_op jit(solution)/shard_map/ppermute | solution.py:108
  55.6 17.8 %copy-start.6 = (bf16[2,1536,128]{2,1,0:T(8,128)(2,1)}, bf16[2,1536,128]{2,1,0:T(8,128)(2,1)S(1)}, u32[]{:S(2)}) copy-start(bf16[2,1536,128]{2,1,0:T(8,128)(2,1)S(1)} %collective-permute-done.27.refs_3_) | copy-start | bytes 2359300
  55.6 86.8 %collective-permute-start.17 = (bf16[3,1536,128]{2,1,0:T(8,128)(2,1)}, bf16[3,1536,128]{2,1,0:T(8,128)(2,1)S(1)}, u32[]{:S(2)}, u32[]{:S(2)}) collective-permute-start(bf16[3,1536,128]{2,1,0:T(8,128)(2,1)} %get-tuple-element.57), channel_id=1, source_target_pairs={{0,16},{8,24},{16,0},{24,8},{1,17},{9,25},{17,1},{25,9},{2,18},{10... | collective-permute-start | bytes 3538952 | tf_op jit(solution)/shard_map/ppermute | solution.py:108
  57.6 85.3 %collective-permute-start.2 = (bf16[3,1536,128]{2,1,0:T(8,128)(2,1)}, bf16[3,1536,128]{2,1,0:T(8,128)(2,1)}, u32[]{:S(2)}, u32[]{:S(2)}) collective-permute-start(bf16[3,1536,128]{2,1,0:T(8,128)(2,1)} %collective-permute-done.1.refs_3_), channel_id=1, source_target_pairs={{0,8},{8,0},{16,24},{24,16},{1,9},{9,1},{17,25},{25,17},{2,10},{10... | collective-permute-start | bytes 3538952 | tf_op jit(solution)/shard_map/ppermute | solution.py:108
  73.3 66.3 %collective-permute-start.37 = (bf16[2,1536,128]{2,1,0:T(8,128)(2,1)}, bf16[2,1536,128]{2,1,0:T(8,128)(2,1)S(1)}, u32[]{:S(2)}, u32[]{:S(2)}) collective-permute-start(bf16[2,1536,128]{2,1,0:T(8,128)(2,1)} %get-tuple-element.68), channel_id=1, source_target_pairs={{0,16},{8,24},{16,0},{24,8},{1,17},{9,25},{17,1},{25,9},{2,18},{10... | collective-permute-start | bytes 2359304 | tf_op jit(solution)/shard_map/ppermute | solution.py:108
  140.6 45.6 %collective-permute-start.25 = (bf16[1,1536,384]{2,1,0:T(8,128)(2,1)}, bf16[1,1536,384]{2,1,0:T(8,128)(2,1)S(1)}, u32[]{:S(2)}, u32[]{:S(2)}) collective-permute-start(bf16[1,1536,384]{2,1,0:T(8,128)(2,1)} %copy-done.8), channel_id=1, source_target_pairs={{0,16},{8,24},{16,0},{24,8},{1,17},{9,25},{17,1},{25,9},{2,18},{10... | collective-permute-start | bytes 3538952 | tf_op jit(solution)/shard_map/ppermute | solution.py:108
  142.3 22.4 %collective-permute-start.28 = (bf16[2,1536,128]{2,1,0:T(8,128)(2,1)}, bf16[2,1536,128]{2,1,0:T(8,128)(2,1)}, u32[]{:S(2)}, u32[]{:S(2)}) collective-permute-start(bf16[2,1536,128]{2,1,0:T(8,128)(2,1)} %copy-done.6), channel_id=1, source_target_pairs={{0,8},{8,0},{16,24},{24,16},{1,9},{9,1},{17,25},{25,17},{2,10},{10... | collective-permute-start | bytes 2359304 | tf_op jit(solution)/shard_map/ppermute | solution.py:108
  142.3 33.9 %collective-permute-start.10 = (bf16[3,1536,128]{2,1,0:T(8,128)(2,1)S(1)}, bf16[3,1536,128]{2,1,0:T(8,128)(2,1)}, u32[]{:S(2)}, u32[]{:S(2)}) collective-permute-start(bf16[3,1536,128]{2,1,0:T(8,128)(2,1)S(1)} %collective-permute-done.9.refs_3_), channel_id=1, source_target_pairs={{0,8},{8,0},{16,24},{24,16},{1,9},{9,1},{17,25},{25,17},{2,10},{10... | collective-permute-start | bytes 3538952 | tf_op jit(solution)/shard_map/ppermute | solution.py:108
  142.9 46.3 %collective-permute-start.18 = (bf16[3,1536,128]{2,1,0:T(8,128)(2,1)S(1)}, bf16[3,1536,128]{2,1,0:T(8,128)(2,1)}, u32[]{:S(2)}, u32[]{:S(2)}) collective-permute-start(bf16[3,1536,128]{2,1,0:T(8,128)(2,1)S(1)} %collective-permute-done.17.refs_1_), channel_id=1, source_target_pairs={{0,8},{8,0},{16,24},{24,16},{1,9},{9,1},{17,25},{25,17},{2,10},{10... | collective-permute-start | bytes 3538952 | tf_op jit(solution)/shard_map/ppermute | solution.py:108
  156.0 32.8 %collective-permute-start.33 = (bf16[2,1536,128]{2,1,0:T(8,128)(2,1)}, bf16[2,1536,128]{2,1,0:T(8,128)(2,1)S(1)}, u32[]{:S(2)}, u32[]{:S(2)}) collective-permute-start(bf16[2,1536,128]{2,1,0:T(8,128)(2,1)} %copy-done.4), channel_id=1, source_target_pairs={{0,8},{8,0},{16,24},{24,16},{1,9},{9,1},{17,25},{25,17},{2,10},{10... | collective-permute-start | bytes 2359304 | tf_op jit(solution)/shard_map/ppermute | solution.py:108
  156.5 8.3 %copy-start.3 = (bf16[2,1536,128]{2,1,0:T(8,128)(2,1)S(1)}, bf16[2,1536,128]{2,1,0:T(8,128)(2,1)}, u32[]{:S(2)}) copy-start(bf16[2,1536,128]{2,1,0:T(8,128)(2,1)} %copy-done.2) | copy-start | bytes 2359300
  164.7 5.0 %copy-start.7 = (bf16[2,1536,128]{2,1,0:T(8,128)(2,1)S(1)}, bf16[2,1536,128]{2,1,0:T(8,128)(2,1)}, u32[]{:S(2)}) copy-start(bf16[2,1536,128]{2,1,0:T(8,128)(2,1)} %copy-done.6) | copy-start | bytes 2359300
  164.7 29.9 %collective-permute-start.38 = (bf16[2,1536,128]{2,1,0:T(8,128)(2,1)S(1)}, bf16[2,1536,128]{2,1,0:T(8,128)(2,1)S(1)}, u32[]{:S(2)}, u32[]{:S(2)}) collective-permute-start(bf16[2,1536,128]{2,1,0:T(8,128)(2,1)S(1)} %copy-done.3), channel_id=1, source_target_pairs={{0,8},{8,0},{16,24},{24,16},{1,9},{9,1},{17,25},{25,17},{2,10},{10... | collective-permute-start | bytes 2359304 | tf_op jit(solution)/shard_map/ppermute | solution.py:108
  176.3 21.9 %collective-permute-start.3 = (bf16[3,32,768]{2,1,0:T(8,128)(2,1)S(1)}, bf16[3,32,768]{2,1,0:T(8,128)(2,1)S(1)}, u32[]{:S(2)}, u32[]{:S(2)}) collective-permute-start(bf16[3,32,768]{2,1,0:T(8,128)(2,1)S(1)} %get-tuple-element.41), channel_id=1, source_target_pairs={{0,2},{1,3},{2,0},{3,1},{4,6},{5,7},{6,4},{7,5},{8,10},{9,11},{10,... | collective-permute-start | bytes 442376 | tf_op jit(solution)/shard_map/ppermute | solution.py:108
  186.2 14.2 %collective-permute-start.4 = (bf16[3,32,768]{2,1,0:T(8,128)(2,1)S(1)}, bf16[3,32,768]{2,1,0:T(8,128)(2,1)S(1)}, u32[]{:S(2)}, u32[]{:S(2)}) collective-permute-start(bf16[3,32,768]{2,1,0:T(8,128)(2,1)S(1)} %get-tuple-element.42), channel_id=1, source_target_pairs={{0,4},{1,5},{2,6},{3,7},{4,0},{5,1},{6,2},{7,3},{8,12},{9,13},{10,... | collective-permute-start | bytes 442376 | tf_op jit(solution)/shard_map/ppermute | solution.py:108
  188.9 11.5 %collective-permute-start.5 = (bf16[3,32,768]{2,1,0:T(8,128)(2,1)S(1)}, bf16[3,32,768]{2,1,0:T(8,128)(2,1)S(1)}, u32[]{:S(2)}, u32[]{:S(2)}) collective-permute-start(bf16[3,32,768]{2,1,0:T(8,128)(2,1)S(1)} %get-tuple-element.43), channel_id=1, source_target_pairs={{0,6},{1,7},{2,4},{3,5},{4,2},{5,3},{6,0},{7,1},{8,14},{9,15},{10,... | collective-permute-start | bytes 442376 | tf_op jit(solution)/shard_map/ppermute | solution.py:108
  189.1 22.7 %copy-start.5 = (bf16[2,1536,128]{2,1,0:T(8,128)(2,1)S(1)}, bf16[2,1536,128]{2,1,0:T(8,128)(2,1)}, u32[]{:S(2)}) copy-start(bf16[2,1536,128]{2,1,0:T(8,128)(2,1)} %copy-done.4) | copy-start | bytes 2359300
  189.1 22.2 %collective-permute-start.11 = (bf16[3,32,768]{2,1,0:T(8,128)(2,1)S(1)}, bf16[3,32,768]{2,1,0:T(8,128)(2,1)S(1)}, u32[]{:S(2)}, u32[]{:S(2)}) collective-permute-start(bf16[3,32,768]{2,1,0:T(8,128)(2,1)S(1)} %get-tuple-element.50), channel_id=1, source_target_pairs={{0,2},{1,3},{2,0},{3,1},{4,6},{5,7},{6,4},{7,5},{8,10},{9,11},{10,... | collective-permute-start | bytes 442376 | tf_op jit(solution)/shard_map/ppermute | solution.py:108
  194.6 23.7 %collective-permute-start.12 = (bf16[3,32,768]{2,1,0:T(8,128)(2,1)S(1)}, bf16[3,32,768]{2,1,0:T(8,128)(2,1)S(1)}, u32[]{:S(2)}, u32[]{:S(2)}) collective-permute-start(bf16[3,32,768]{2,1,0:T(8,128)(2,1)S(1)} %get-tuple-element.51), channel_id=1, source_target_pairs={{0,4},{1,5},{2,6},{3,7},{4,0},{5,1},{6,2},{7,3},{8,12},{9,13},{10,... | collective-permute-start | bytes 442376 | tf_op jit(solution)/shard_map/ppermute | solution.py:108
  198.2 20.2 %collective-permute-start.13 = (bf16[3,32,768]{2,1,0:T(8,128)(2,1)S(1)}, bf16[3,32,768]{2,1,0:T(8,128)(2,1)S(1)}, u32[]{:S(2)}, u32[]{:S(2)}) collective-permute-start(bf16[3,32,768]{2,1,0:T(8,128)(2,1)S(1)} %get-tuple-element.52), channel_id=1, source_target_pairs={{0,6},{1,7},{2,4},{3,5},{4,2},{5,3},{6,0},{7,1},{8,14},{9,15},{10,... | collective-permute-start | bytes 442376 | tf_op jit(solution)/shard_map/ppermute | solution.py:108
  200.4 26.9 %collective-permute-start.19 = (bf16[3,32,768]{2,1,0:T(8,128)(2,1)S(1)}, bf16[3,32,768]{2,1,0:T(8,128)(2,1)S(1)}, u32[]{:S(2)}, u32[]{:S(2)}) collective-permute-start(bf16[3,32,768]{2,1,0:T(8,128)(2,1)S(1)} %get-tuple-element.59), channel_id=1, source_target_pairs={{0,2},{1,3},{2,0},{3,1},{4,6},{5,7},{6,4},{7,5},{8,10},{9,11},{10,... | collective-permute-start | bytes 442376 | tf_op jit(solution)/shard_map/ppermute | solution.py:108
  200.4 30.3 %collective-permute-start.20 = (bf16[3,32,768]{2,1,0:T(8,128)(2,1)S(1)}, bf16[3,32,768]{2,1,0:T(8,128)(2,1)S(1)}, u32[]{:S(2)}, u32[]{:S(2)}) collective-permute-start(bf16[3,32,768]{2,1,0:T(8,128)(2,1)S(1)} %get-tuple-element.60), channel_id=1, source_target_pairs={{0,4},{1,5},{2,6},{3,7},{4,0},{5,1},{6,2},{7,3},{8,12},{9,13},{10,... | collective-permute-start | bytes 442376 | tf_op jit(solution)/shard_map/ppermute | solution.py:108
  211.3 33.0 %collective-permute-start.30 = (bf16[2,128,768]{2,1,0:T(8,128)(2,1)S(1)}, bf16[2,128,768]{2,1,0:T(8,128)(2,1)S(1)}, u32[]{:S(2)}, u32[]{:S(2)}) collective-permute-start(bf16[2,128,768]{2,1,0:T(8,128)(2,1)S(1)} %shard_map.65.refs_0_), channel_id=1, source_target_pairs={{0,6},{1,7},{2,4},{3,5},{4,2},{5,3},{6,0},{7,1},{8,14},{9,15},{10,... | collective-permute-start | bytes 1179656 | tf_op jit(solution)/shard_map/ppermute | solution.py:108
  218.3 94.8 %collective-permute-start.26 = (bf16[1,1536,384]{2,1,0:T(8,128)(2,1)S(1)}, bf16[1,1536,384]{2,1,0:T(8,128)(2,1)S(1)}, u32[]{:S(2)}, u32[]{:S(2)}) collective-permute-start(bf16[1,1536,384]{2,1,0:T(8,128)(2,1)S(1)} %collective-permute-done.25.first), channel_id=1, source_target_pairs={{0,8},{8,0},{16,24},{24,16},{1,9},{9,1},{17,25},{25,17},{2,10},{10... | collective-permute-start | bytes 3538952 | tf_op jit(solution)/shard_map/ppermute | solution.py:108
  218.4 50.9 %collective-permute-start.29 = (bf16[2,128,768]{2,1,0:T(8,128)(2,1)S(1)}, bf16[2,128,768]{2,1,0:T(8,128)(2,1)S(1)}, u32[]{:S(2)}, u32[]{:S(2)}) collective-permute-start(bf16[2,128,768]{2,1,0:T(8,128)(2,1)S(1)} %shard_map.65.refs_0_), channel_id=1, source_target_pairs={{0,2},{1,3},{2,0},{3,1},{4,6},{5,7},{6,4},{7,5},{8,10},{9,11},{10,... | collective-permute-start | bytes 1179656 | tf_op jit(solution)/shard_map/ppermute | solution.py:108
  227.3 16.6 %collective-permute-start.21 = (bf16[3,32,768]{2,1,0:T(8,128)(2,1)S(1)}, bf16[3,32,768]{2,1,0:T(8,128)(2,1)S(1)}, u32[]{:S(2)}, u32[]{:S(2)}) collective-permute-start(bf16[3,32,768]{2,1,0:T(8,128)(2,1)S(1)} %get-tuple-element.61), channel_id=1, source_target_pairs={{0,6},{1,7},{2,4},{3,5},{4,2},{5,3},{6,0},{7,1},{8,14},{9,15},{10,... | collective-permute-start | bytes 442376 | tf_op jit(solution)/shard_map/ppermute | solution.py:108
  230.7 38.7 %collective-permute-start.35 = (bf16[2,128,768]{2,1,0:T(8,128)(2,1)S(1)}, bf16[2,128,768]{2,1,0:T(8,128)(2,1)S(1)}, u32[]{:S(2)}, u32[]{:S(2)}) collective-permute-start(bf16[2,128,768]{2,1,0:T(8,128)(2,1)S(1)} %shard_map.67.refs_0_), channel_id=1, source_target_pairs={{0,6},{1,7},{2,4},{3,5},{4,2},{5,3},{6,0},{7,1},{8,14},{9,15},{10,... | collective-permute-start | bytes 1179656 | tf_op jit(solution)/shard_map/ppermute | solution.py:108
  239.9 31.6 %copy-start.10 = (f32[128]{0:T(128)S(1)}, f32[128]{0:T(128)}, u32[]{:S(2)}) copy-start(f32[128]{0:T(128)} %param.8) | copy-start | bytes 1540
  239.9 31.7 %copy-start.11 = (f32[128]{0:T(128)S(1)}, f32[128]{0:T(128)}, u32[]{:S(2)}) copy-start(f32[128]{0:T(128)} %param.9) | copy-start | bytes 1540
  243.9 31.0 %collective-permute-start.40 = (bf16[2,128,768]{2,1,0:T(8,128)(2,1)S(1)}, bf16[2,128,768]{2,1,0:T(8,128)(2,1)S(1)}, u32[]{:S(2)}, u32[]{:S(2)}) collective-permute-start(bf16[2,128,768]{2,1,0:T(8,128)(2,1)S(1)} %shard_map.69.refs_0_), channel_id=1, source_target_pairs={{0,6},{1,7},{2,4},{3,5},{4,2},{5,3},{6,0},{7,1},{8,14},{9,15},{10,... | collective-permute-start | bytes 1179656 | tf_op jit(solution)/shard_map/ppermute | solution.py:108
  244.4 34.5 %collective-permute-start.31 = (bf16[2,128,768]{2,1,0:T(8,128)(2,1)S(1)}, bf16[2,128,768]{2,1,0:T(8,128)(2,1)S(1)}, u32[]{:S(2)}, u32[]{:S(2)}) collective-permute-start(bf16[2,128,768]{2,1,0:T(8,128)(2,1)S(1)} %collective-permute-done.30.refs_3_), channel_id=1, source_target_pairs={{0,2},{1,3},{2,0},{3,1},{4,6},{5,7},{6,4},{7,5},{8,10},{9,11},{10,... | collective-permute-start | bytes 1179656 | tf_op jit(solution)/shard_map/ppermute | solution.py:108
  269.3 13.5 %collective-permute-start.34 = (bf16[2,128,768]{2,1,0:T(8,128)(2,1)S(1)}, bf16[2,128,768]{2,1,0:T(8,128)(2,1)S(1)}, u32[]{:S(2)}, u32[]{:S(2)}) collective-permute-start(bf16[2,128,768]{2,1,0:T(8,128)(2,1)S(1)} %shard_map.67.refs_0_), channel_id=1, source_target_pairs={{0,2},{1,3},{2,0},{3,1},{4,6},{5,7},{6,4},{7,5},{8,10},{9,11},{10,... | collective-permute-start | bytes 1179656 | tf_op jit(solution)/shard_map/ppermute | solution.py:108
  269.4 22.1 %collective-permute-start.36 = (bf16[2,128,768]{2,1,0:T(8,128)(2,1)S(1)}, bf16[2,128,768]{2,1,0:T(8,128)(2,1)S(1)}, u32[]{:S(2)}, u32[]{:S(2)}) collective-permute-start(bf16[2,128,768]{2,1,0:T(8,128)(2,1)S(1)} %collective-permute-done.35.refs_3_), channel_id=1, source_target_pairs={{0,2},{1,3},{2,0},{3,1},{4,6},{5,7},{6,4},{7,5},{8,10},{9,11},{10,... | collective-permute-start | bytes 1179656 | tf_op jit(solution)/shard_map/ppermute | solution.py:108
  275.0 25.5 %collective-permute-start.39 = (bf16[2,128,768]{2,1,0:T(8,128)(2,1)S(1)}, bf16[2,128,768]{2,1,0:T(8,128)(2,1)S(1)}, u32[]{:S(2)}, u32[]{:S(2)}) collective-permute-start(bf16[2,128,768]{2,1,0:T(8,128)(2,1)S(1)} %shard_map.69.refs_0_), channel_id=1, source_target_pairs={{0,2},{1,3},{2,0},{3,1},{4,6},{5,7},{6,4},{7,5},{8,10},{9,11},{10,... | collective-permute-start | bytes 1179656 | tf_op jit(solution)/shard_map/ppermute | solution.py:108
  278.9 28.4 %collective-permute-start.41 = (bf16[2,128,768]{2,1,0:T(8,128)(2,1)S(1)}, bf16[2,128,768]{2,1,0:T(8,128)(2,1)S(1)}, u32[]{:S(2)}, u32[]{:S(2)}) collective-permute-start(bf16[2,128,768]{2,1,0:T(8,128)(2,1)S(1)} %collective-permute-done.40.refs_3_), channel_id=1, source_target_pairs={{0,2},{1,3},{2,0},{3,1},{4,6},{5,7},{6,4},{7,5},{8,10},{9,11},{10,... | collective-permute-start | bytes 1179656 | tf_op jit(solution)/shard_map/ppermute | solution.py:108
  282.9 31.0 %collective-permute-start.6 = (bf16[32,768]{1,0:T(8,128)(2,1)S(1)}, bf16[32,768]{1,0:T(8,128)(2,1)S(1)}, u32[]{:S(2)}, u32[]{:S(2)}) collective-permute-start(bf16[32,768]{1,0:T(8,128)(2,1)S(1)} %get-tuple-element.45), channel_id=1, source_target_pairs={{0,2},{1,3},{2,0},{3,1},{4,6},{5,7},{6,4},{7,5},{8,10},{9,11},{10,... | collective-permute-start | bytes 147464 | tf_op jit(solution)/shard_map/ppermute | solution.py:108
  291.5 23.9 %collective-permute-start.7 = (bf16[32,768]{1,0:T(8,128)(2,1)S(1)}, bf16[32,768]{1,0:T(8,128)(2,1)S(1)}, u32[]{:S(2)}, u32[]{:S(2)}) collective-permute-start(bf16[32,768]{1,0:T(8,128)(2,1)S(1)} %get-tuple-element.46), channel_id=1, source_target_pairs={{0,4},{1,5},{2,6},{3,7},{4,0},{5,1},{6,2},{7,3},{8,12},{9,13},{10,... | collective-permute-start | bytes 147464 | tf_op jit(solution)/shard_map/ppermute | solution.py:108
  300.5 16.1 %collective-permute-start.8 = (bf16[32,768]{1,0:T(8,128)(2,1)S(1)}, bf16[32,768]{1,0:T(8,128)(2,1)S(1)}, u32[]{:S(2)}, u32[]{:S(2)}) collective-permute-start(bf16[32,768]{1,0:T(8,128)(2,1)S(1)} %get-tuple-element.47), channel_id=1, source_target_pairs={{0,6},{1,7},{2,4},{3,5},{4,2},{5,3},{6,0},{7,1},{8,14},{9,15},{10,... | collective-permute-start | bytes 147464 | tf_op jit(solution)/shard_map/ppermute | solution.py:108
  307.3 11.0 %collective-permute-start.14 = (bf16[32,768]{1,0:T(8,128)(2,1)S(1)}, bf16[32,768]{1,0:T(8,128)(2,1)S(1)}, u32[]{:S(2)}, u32[]{:S(2)}) collective-permute-start(bf16[32,768]{1,0:T(8,128)(2,1)S(1)} %get-tuple-element.54), channel_id=1, source_target_pairs={{0,2},{1,3},{2,0},{3,1},{4,6},{5,7},{6,4},{7,5},{8,10},{9,11},{10,... | collective-permute-start | bytes 147464 | tf_op jit(solution)/shard_map/ppermute | solution.py:108
  313.1 13.0 %collective-permute-start.15 = (bf16[32,768]{1,0:T(8,128)(2,1)S(1)}, bf16[32,768]{1,0:T(8,128)(2,1)S(1)}, u32[]{:S(2)}, u32[]{:S(2)}) collective-permute-start(bf16[32,768]{1,0:T(8,128)(2,1)S(1)} %get-tuple-element.55), channel_id=1, source_target_pairs={{0,4},{1,5},{2,6},{3,7},{4,0},{5,1},{6,2},{7,3},{8,12},{9,13},{10,... | collective-permute-start | bytes 147464 | tf_op jit(solution)/shard_map/ppermute | solution.py:108
  313.9 12.2 %collective-permute-start.16 = (bf16[32,768]{1,0:T(8,128)(2,1)S(1)}, bf16[32,768]{1,0:T(8,128)(2,1)S(1)}, u32[]{:S(2)}, u32[]{:S(2)}) collective-permute-start(bf16[32,768]{1,0:T(8,128)(2,1)S(1)} %get-tuple-element.56), channel_id=1, source_target_pairs={{0,6},{1,7},{2,4},{3,5},{4,2},{5,3},{6,0},{7,1},{8,14},{9,15},{10,... | collective-permute-start | bytes 147464 | tf_op jit(solution)/shard_map/ppermute | solution.py:108
  315.4 10.6 %collective-permute-start.22 = (bf16[32,768]{1,0:T(8,128)(2,1)S(1)}, bf16[32,768]{1,0:T(8,128)(2,1)S(1)}, u32[]{:S(2)}, u32[]{:S(2)}) collective-permute-start(bf16[32,768]{1,0:T(8,128)(2,1)S(1)} %get-tuple-element.63), channel_id=1, source_target_pairs={{0,2},{1,3},{2,0},{3,1},{4,6},{5,7},{6,4},{7,5},{8,10},{9,11},{10,... | collective-permute-start | bytes 147464 | tf_op jit(solution)/shard_map/ppermute | solution.py:108
  316.6 9.5 %collective-permute-start.23 = (bf16[32,768]{1,0:T(8,128)(2,1)S(1)}, bf16[32,768]{1,0:T(8,128)(2,1)S(1)}, u32[]{:S(2)}, u32[]{:S(2)}) collective-permute-start(bf16[32,768]{1,0:T(8,128)(2,1)S(1)} %get-tuple-element.64), channel_id=1, source_target_pairs={{0,4},{1,5},{2,6},{3,7},{4,0},{5,1},{6,2},{7,3},{8,12},{9,13},{10,... | collective-permute-start | bytes 147464 | tf_op jit(solution)/shard_map/ppermute | solution.py:108
  318.3 7.8 %collective-permute-start.24 = (bf16[32,768]{1,0:T(8,128)(2,1)S(1)}, bf16[32,768]{1,0:T(8,128)(2,1)S(1)}, u32[]{:S(2)}, u32[]{:S(2)}) collective-permute-start(bf16[32,768]{1,0:T(8,128)(2,1)S(1)} %get-tuple-element.65), channel_id=1, source_target_pairs={{0,6},{1,7},{2,4},{3,5},{4,2},{5,3},{6,0},{7,1},{8,14},{9,15},{10,... | collective-permute-start | bytes 147464 | tf_op jit(solution)/shard_map/ppermute | solution.py:108
  (6 other events, 6.0 us)

commit v3 on v2

--- a/solution.py
+++ b/solution.py
@@ -123,7 +123,7 @@
             flops=flops, bytes_accessed=bytes_accessed, transcendentals=0
         ),
         compiler_params=pltpu.CompilerParams(
-            dimension_semantics=("arbitrary",) * len(grid), vmem_limit_bytes=48 * 2**20
+            dimension_semantics=("arbitrary",) * len(grid), vmem_limit_bytes=43 * 2**20
         ),
     )
 
@@ -318,7 +318,7 @@
         out[:, index * LANES : (index + 1) * LANES] = jnp.concatenate(attended, axis=0).T
 
 
-def tail(total, normed, first, second, *shares):
+def tail(total, normed, first, second, skip, *shares):
     rows, width = normed.shape
     depth = first.shape[1]
     cols = len(shares) * LANES
@@ -326,7 +326,7 @@
         tail_kernel,
         (rows // PATCHES,),
         [
-            pl.BlockSpec((PATCHES, cols), lambda i: (i, 0)),
+            pl.BlockSpec((PATCHES, cols), lambda i: (i, skip // len(shares))),
             pl.BlockSpec((PATCHES, width // 2), lambda i: (i, 1)),
             pl.BlockSpec((1, depth, cols), lambda i: (0, 0, 0)),
             pl.BlockSpec((1, depth, cols), lambda i: (0, 0, 0)),
@@ -435,18 +435,21 @@
             start = pl.multiple_of((quarter[0] ^ rel) * part, part)
             hold[pl.ds(start, part), :] = pieces[chunk * SPLITS + rel][...]
         out[:, chunk * LANES : (chunk + 1) * LANES] = hold[...].T
-    out[:, early * LANES :] = tails[0][...]
+    start = early * LANES
+    for last in tails:
+        out[:, start : start + last.shape[1]] = last[...]
+        start += last.shape[1]
 
 
 def finish(quarter, pieces, tails):
     part, rows = pieces[0].shape
     early = len(pieces) // SPLITS
-    width = early * LANES + tails[0].shape[1]
+    width = early * LANES + sum(last.shape[1] for last in tails)
     return call(
         functools.partial(finish_kernel, early),
         (1,),
         [pl.BlockSpec((part, rows), lambda i, s: (0, 0))] * len(pieces)
-        + [pl.BlockSpec(tails[0].shape, lambda i, s: (0, 0))],
+        + [pl.BlockSpec(last.shape, lambda i, s: (0, 0)) for last in tails],
         pl.BlockSpec((rows, width), lambda i, s: (0, 0)),
         jax.ShapeDtypeStruct((rows, width), jnp.bfloat16),
         rows * width * 100,
@@ -466,11 +469,12 @@
 def sequence(chunks):
     early = chunks - chunks // 2
     pairs = [("pair", c, 1) for c in range(early, chunks)]
-    units = []
-    for c in range(early - 1):
-        units += [("all", c, 1)] + pairs[c : c + 1]
-    units += pairs[early - 1 :] + [("all", early - 1, 1)]
-    return units + [("value", early, chunks - early)]
+    units = pairs[:1]
+    for c in range(early):
+        units += pairs[c + 1 : c + 2] + [("all", c, 1)]
+    most = max(chunks - early - 1, 1)
+    units.append(("value", early, most))
+    return units + [("value", c, 1) for c in range(early + most, chunks)]
 
 
 def exchange(values, groups):
@@ -531,7 +535,9 @@
     quarter = (lax.axis_index("mp") // groups).astype(jnp.int32)[None]
     weight = jnp.transpose(w_qkv, (1, 0, 2))
     units = sequence(weight.shape[2] // LANES)
-    slices = [weight[:, :, :LANES]]
+    first, last = UNIT_KINDS[units[0][0]]
+    start = units[0][1] * LANES
+    slices = [weight[first:last, :, start : start + units[0][2] * LANES]]
     slices += cut(after(weight, slices[0]), units[1:])
     beside = [swap(slices[n], "dp", 2) for n in range(len(units))]
     paired = swap(after(weight, slices[1]), "dp", 1)
@@ -543,12 +549,17 @@
     for n, (kind, chunk, count) in enumerate(units):
         across = swap(beside[n], "dp", 1)
         far = (beside[n], across)
+        if kind == "value":
+            if not tails:
+                late = sum(unit[2] for unit in units[n:])
+                begun = near_sums(normed, near, kind, chunk, late)
+            skip = chunk - (len(returned) // SPLITS)
+            mine = shares[skip : skip + count]
+            tails.append(tail(begun, normed, *far, skip, *mine))
+            continue
         begun = None
-        if n >= len(units) - 2:
+        if units[n + 1][0] == "value":
             begun = near_sums(normed, near, kind, chunk, count)
-        if kind == "value":
-            tails.append(tail(begun, normed, *far, *shares))
-            continue
         split = kind == "all"
         pieces = project(quarter, normed, near, far, chunk, split, begun)
         if split:

time: 328 us -> 316 us (0.963)
  starting transfers between devices: 87.8 us -> 70.1 us
  waiting for transfers between devices: 143 us -> 147 us
    ppermute x42 -> x44, starting transfers between devices: 87.8 us -> 70.1 us  [swap(): return lax.ppermute(value, axis, [(i, i ^ mask) for i in range(length)])]
    ppermute x42 -> x44, waiting for transfers between devices: 143 us -> 147 us  [swap(): return lax.ppermute(value, axis, [(i, i ^ mask) for i in range(length)])]
    pallas_call x1 -> x2, Pallas kernels: 6.2 us -> 9.72 us  [tail(): call(tail_kernel, (rows // PATCHES,), [pl.BlockSpec((PATCHES, cols), lamb...]
    unnamed x24 -> x20, local copies, waits for them, and re-layouts: 6.02 us -> 6.97 us
  transfers between devices with their start and end apart: 42 -> 44, of which waited for: 8 -> 10; matrix products, arithmetic and copies ran while one was open for 0% -> 0% of each run, Pallas kernels for 25% -> 26%
where the time goes in v3:
time: 316 us; the launch traced here: 315 us
  waiting for transfers between devices  147 us (47%)
  Pallas kernels  89.3 us (28%)
  starting transfers between devices  70.1 us (22%)
  local copies, waits for them, and re-layouts  8.31 us (3%)
    ppermute x44, waiting for transfers between devices, swap(): return lax.ppermute(value, axis, [(i, i ^ mask) for i in range(length)])  147 us
    ppermute x44, starting transfers between devices, swap(): return lax.ppermute(value, axis, [(i, i ^ mask) for i in range(length)])  70.1 us
    pallas_call x6, Pallas kernels, project(): call(kernel, (1,), [pl.BlockSpec(memory_space=pltpu.HBM)] * (len(weights)...  41 us
    pallas_call x1, Pallas kernels, norm_tokens(): call(functools.partial(norm_kernel, parts), (rows // block,), [pl.BlockSp...  9.82 us
    pallas_call x2, Pallas kernels, tail(): call(tail_kernel, (rows // PATCHES,), [pl.BlockSpec((PATCHES, cols), lamb...  9.72 us
    pallas_call x2, Pallas kernels, near_sums(): call(functools.partial(near_kernel, parts, first, chunk), (1,), [pl.Block...  9.48 us
    unnamed x20, local copies, waits for them, and re-layouts  6.97 us
    pallas_call x3, Pallas kernels, weigh(): call(weigh_kernel, (rows // PATCHES,), [pl.BlockSpec((kinds, lanes, PATCH...  6.82 us
  transfers between devices with their start and end apart: 44, of which 10 were waited for; matrix products, arithmetic and copies ran while one was open for 0% of the time, Pallas kernels for 26%

profile of v3, /device:TPU:0, one launch (start us, length us, event | category | flops | bytes accessed | tf_op | source)
XLA Modules:
  0.0 315.2 jit_solution(2018077874253270844)
XLA Ops:
  1.2 6.3 %shard_map.56 = (bf16[2,1536,128]{2,1,0:T(8,128)(2,1)}, bf16[3,1536,128]{2,1,0:T(8,128)(2,1)S(1)}, bf16[2,1536,128]{2,1,0:T(8,128)(2,1)S(1)}, bf16[3,1536,128]{2...) custom-call(bf16[3,1536,768]{2,1,0:T(8,128)(2,1)} %bitcast.3.source., ...), custom_call_target="tpu_custom_call" | custom-call | flops 1769472000 | bytes 14155776 | tf_op jit(solution)/shard_map/pallas_call | solution.py:519
  10.5 2.5 collective-permute-start.1
  13.0 2.0 collective-permute-start.9
  15.0 24.8 %collective-permute-done.1.refs_3_ = bf16[3,1536,128]{2,1,0:T(8,128)(2,1)S(1)} collective-permute-done((bf16[3,1536,128]{2,1,0:T(8,128)(2,1)S(1)}, bf16[3,1536,128]{2,1,0:T(8,128)(2,1)S(1)}, u32[]{:S(2)}, u32[]{:S(2)}) %collective-permute-start.1) | collective-permute-done | bytes 1179680 | tf_op jit(solution)/shard_map/ppermute | solution.py:108
  39.8 16.8 %collective-permute-done.27.refs_3_ = bf16[2,1536,128]{2,1,0:T(8,128)(2,1)S(1)} collective-permute-done((bf16[2,1536,128]{2,1,0:T(8,128)(2,1)S(1)}, bf16[2,1536,128]{2,1,0:T(8,128)(2,1)S(1)}, u32[]{:S(2)}, u32[]{:S(2)}) %collective-permute-start.27) | collective-permute-done | bytes 786464 | tf_op jit(solution)/shard_map/ppermute | solution.py:108
  56.7 2.0 collective-permute-start.32
  58.7 23.3 %collective-permute-done.9.refs_3_ = bf16[3,1536,128]{2,1,0:T(8,128)(2,1)S(1)} collective-permute-done((bf16[3,1536,128]{2,1,0:T(8,128)(2,1)S(1)}, bf16[3,1536,128]{2,1,0:T(8,128)(2,1)S(1)}, u32[]{:S(2)}, u32[]{:S(2)}) %collective-permute-start.9) | collective-permute-done | bytes 1179680 | tf_op jit(solution)/shard_map/ppermute | solution.py:108
  82.0 42.1 %collective-permute-done.32.refs_3_ = bf16[2,1536,128]{2,1,0:T(8,128)(2,1)} collective-permute-done((bf16[2,1536,128]{2,1,0:T(8,128)(2,1)}, bf16[2,1536,128]{2,1,0:T(8,128)(2,1)}, u32[]{:S(2)}, u32[]{:S(2)}) %collective-permute-start.32) | collective-permute-done | bytes 786464 | tf_op jit(solution)/shard_map/ppermute | solution.py:108
  124.0 1.7 collective-permute-start.39
  127.0 9.8 %shard_map.55.refs_0_.normed = bf16[768,6144]{1,0:T(8,128)(2,1)S(1)} custom-call(s32[1]{0:T(128)} %bitcast.1.place, bf16[768,6144]{1,0:T(8,128)(2,1)} %tokens.1, f32[1,6144]{1,0:T(1,128)S(1)} %bitcast.4), custom_call_target="tpu_custom_call" | custom-call | flops 5662310400 | bytes 18874368 | tf_op jit(solution)/shard_map/pallas_call | solution.py:155
  136.8 3.7 %copy-done = bf16[768,6144]{1,0:T(8,128)(2,1)} copy-done((bf16[768,6144]{1,0:T(8,128)(2,1)}, bf16[768,6144]{1,0:T(8,128)(2,1)S(1)}, u32[]{:S(2)}) %copy-start) | copy-done | bytes 9437208
  140.8 8.3 %shard_map.57 = (bf16[3,32,768]{2,1,0:T(8,128)(2,1)S(1)}, bf16[3,32,768]{2,1,0:T(8,128)(2,1)S(1)}, bf16[3,32,768]{2,1,0:T(8,128)(2,1)S(1)}, bf16[3,32,768]{2,1,0:T(8,128)(2,1)S(1)}) custom-call(s32[1]{0:T(128)} %bitcast.quarter, bf16[768,6144]{1,0:T(8,128)(2,1)} %copy-done, bf16[3,1536,768]{2,1,0:T(8,128)(2,1)} %bitcast.3.source.refs_1_.refs_0_, ...), custom_call_target="tpu_custom_call" | custom-call | flops 3623878656 | bytes 14155776 | tf_op jit(solution)/shard_map/pallas_call | solution.py:258
  149.8 6.5 %shard_map.65.refs_0_ = bf16[2,128,768]{2,1,0:T(8,128)(2,1)S(1)} custom-call(s32[1]{0:T(128)} %bitcast.quarter, bf16[768,6144]{1,0:T(8,128)(2,1)} %copy-done, bf16[3,1536,768]{2,1,0:T(8,128)(2,1)} %bitcast.3.source.refs_1_.refs_0_, bf16[3,1536,768]{2,1,0:T(8,128)(2,1)} %collective-permute-done.refs_2_.refs_1_, bf16[2,1536,128]{2,1,0:T(8,128)(2,1)S(1)} %copy-done.2, ...), custom_call_target="tpu_custom_call" | custom-call | flops 2415919104 | bytes 12582912 | tf_op jit(solution)/shard_map/pallas_call | solution.py:258
  156.3 1.8 collective-permute-start.37
  158.1 4.8 %shard_map.61.refs_3_ = f32[768,384]{1,0:T(8,128)S(1)} custom-call(bf16[768,6144]{1,0:T(8,128)(2,1)} %copy-done, bf16[3,1536,768]{2,1,0:T(8,128)(2,1)} %bitcast.3.source.refs_1_.refs_0_, bf16[3,1536,768]{2,1,0:T(8,128)(2,1)} %collective-permute-done.refs_2_.refs_1_), custom_call_target="tpu_custom_call" | custom-call | flops 1811939328 | bytes 7077888 | tf_op jit(solution)/shard_map/pallas_call | solution.py:288
  162.9 8.3 %shard_map.59 = (bf16[3,32,768]{2,1,0:T(8,128)(2,1)S(1)}, bf16[3,32,768]{2,1,0:T(8,128)(2,1)S(1)}, bf16[3,32,768]{2,1,0:T(8,128)(2,1)S(1)}, bf16[3,32,768]{2,1,0:T(8,128)(2,1)S(1)}) custom-call(s32[1]{0:T(128)} %bitcast.quarter, bf16[768,6144]{1,0:T(8,128)(2,1)} %copy-done, bf16[3,1536,768]{2,1,0:T(8,128)(2,1)} %bitcast.3.source.refs_1_.refs_0_, ...), custom_call_target="tpu_custom_call" | custom-call | flops 3623878656 | bytes 14155776 | tf_op jit(solution)/shard_map/pallas_call | solution.py:258
  172.8 2.6 collective-permute-start.4
  175.6 4.8 %shard_map.62 = (bf16[3,32,768]{2,1,0:T(8,128)(2,1)S(1)}, bf16[3,32,768]{2,1,0:T(8,128)(2,1)S(1)}, bf16[3,32,768]{2,1,0:T(8,128)(2,1)S(1)}, bf16[3,32,768]{2,1,0:T(8,128)(2,1)S(1)}) custom-call(s32[1]{0:T(128)} %bitcast.quarter, bf16[768,6144]{1,0:T(8,128)(2,1)} %copy-done, bf16[3,1536,128]{2,1,0:T(8,128)(2,1)S(1)} %collective-permute-done.17.refs_1_, ...), custom_call_target="tpu_custom_call" | custom-call | flops 1811939328 | bytes 7077888 | tf_op jit(solution)/shard_map/pallas_call | solution.py:258
  181.2 3.5 %collective-permute-start.12 = (bf16[3,32,768]{2,1,0:T(8,128)(2,1)S(1)}, bf16[3,32,768]{2,1,0:T(8,128)(2,1)S(1)}, u32[]{:S(2)}, u32[]{:S(2)}) collective-permute-start(bf16[3,32,768]{2,1,0:T(8,128)(2,1)S(1)} %get-tuple-element.53), channel_id=1, source_target_pairs={{0,4},{1,5},{2,6},{3,7},{4,0},{5,1},{6,2},{7,3},{8,12},{9,13},{10,... | collective-permute-start | bytes 442376 | tf_op jit(solution)/shard_map/ppermute | solution.py:108
  184.9 1.9 collective-permute-done.4.refs_2_
  186.8 2.4 collective-permute-start.30
  189.2 6.5 %shard_map.67.refs_0_ = bf16[2,128,768]{2,1,0:T(8,128)(2,1)S(1)} custom-call(s32[1]{0:T(128)} %bitcast.quarter, bf16[768,6144]{1,0:T(8,128)(2,1)} %copy-done, bf16[3,1536,768]{2,1,0:T(8,128)(2,1)} %bitcast.3.source.refs_1_.refs_0_, bf16[3,1536,768]{2,1,0:T(8,128)(2,1)} %collective-permute-done.refs_2_.refs_1_, ...), custom_call_target="tpu_custom_call" | custom-call | flops 2415919104 | bytes 12582912 | tf_op jit(solution)/shard_map/pallas_call | solution.py:258
  195.7 9.2 %collective-permute-start.29 = (bf16[2,128,768]{2,1,0:T(8,128)(2,1)S(1)}, bf16[2,128,768]{2,1,0:T(8,128)(2,1)S(1)}, u32[]{:S(2)}, u32[]{:S(2)}) collective-permute-start(bf16[2,128,768]{2,1,0:T(8,128)(2,1)S(1)} %shard_map.65.refs_0_), channel_id=1, source_target_pairs={{0,2},{1,3},{2,0},{3,1},{4,6},{5,7},{6,4},{7,5},{8,10},{9,11},{10,... | collective-permute-start | bytes 1179656 | tf_op jit(solution)/shard_map/ppermute | solution.py:108
  204.9 2.9 collective-permute-done.12.refs_2_
  207.9 2.3 collective-permute-start.21
  211.7 6.5 %shard_map.70.refs_0_ = bf16[2,128,768]{2,1,0:T(8,128)(2,1)S(1)} custom-call(s32[1]{0:T(128)} %bitcast.quarter, bf16[768,6144]{1,0:T(8,128)(2,1)} %copy-done, bf16[3,1536,768]{2,1,0:T(8,128)(2,1)} %bitcast.3.source.refs_1_.refs_0_, bf16[3,1536,768]{2,1,0:T(8,128)(2,1)} %collective-permute-done.refs_2_.refs_1_, ...), custom_call_target="tpu_custom_call" | custom-call | flops 2415919104 | bytes 12582912 | tf_op jit(solution)/shard_map/pallas_call | solution.py:258
  218.2 19.1 %collective-permute-done.20.refs_2_ = bf16[3,32,768]{2,1,0:T(8,128)(2,1)S(1)} collective-permute-done((bf16[3,32,768]{2,1,0:T(8,128)(2,1)S(1)}, bf16[3,32,768]{2,1,0:T(8,128)(2,1)S(1)}, u32[]{:S(2)}, u32[]{:S(2)}) %collective-permute-start.20) | collective-permute-done | bytes 147488 | tf_op jit(solution)/shard_map/ppermute | solution.py:108
  237.3 2.3 collective-permute-start.42
  239.7 4.7 %shard_map.64.total = f32[768,384]{1,0:T(8,128)S(1)} custom-call(bf16[768,6144]{1,0:T(8,128)(2,1)} %copy-done, bf16[3,1536,768]{2,1,0:T(8,128)(2,1)} %bitcast.3.source.refs_1_.refs_0_, bf16[3,1536,768]{2,1,0:T(8,128)(2,1)} %collective-permute-done.refs_2_.refs_1_), custom_call_target="tpu_custom_call" | custom-call | flops 1811939328 | bytes 7077888 | tf_op jit(solution)/shard_map/pallas_call | solution.py:288
  244.4 7.7 %collective-permute-start.34 = (bf16[2,128,768]{2,1,0:T(8,128)(2,1)S(1)}, bf16[2,128,768]{2,1,0:T(8,128)(2,1)S(1)}, u32[]{:S(2)}, u32[]{:S(2)}) collective-permute-start(bf16[2,128,768]{2,1,0:T(8,128)(2,1)S(1)} %shard_map.67.refs_0_), channel_id=1, source_target_pairs={{0,2},{1,3},{2,0},{3,1},{4,6},{5,7},{6,4},{7,5},{8,10},{9,11},{10,... | collective-permute-start | bytes 1179656 | tf_op jit(solution)/shard_map/ppermute | solution.py:108
  252.1 5.8 %collective-permute-start.36 = (bf16[2,128,768]{2,1,0:T(8,128)(2,1)S(1)}, bf16[2,128,768]{2,1,0:T(8,128)(2,1)S(1)}, u32[]{:S(2)}, u32[]{:S(2)}) collective-permute-start(bf16[2,128,768]{2,1,0:T(8,128)(2,1)S(1)} %collective-permute-done.35.refs_3_), channel_id=1, source_target_pairs={{0,2},{1,3},{2,0},{3,1},{4,6},{5,7},{6,4},{7,5},{8,10},{9,11},{10,... | collective-permute-start | bytes 1179656 | tf_op jit(solution)/shard_map/ppermute | solution.py:108
  258.1 1.7 shard_map.58
  259.8 1.7 shard_map.60
  261.5 3.5 %collective-permute-start.41 = (bf16[2,128,768]{2,1,0:T(8,128)(2,1)S(1)}, bf16[2,128,768]{2,1,0:T(8,128)(2,1)S(1)}, u32[]{:S(2)}, u32[]{:S(2)}) collective-permute-start(bf16[2,128,768]{2,1,0:T(8,128)(2,1)S(1)} %shard_map.70.refs_0_), channel_id=1, source_target_pairs={{0,2},{1,3},{2,0},{3,1},{4,6},{5,7},{6,4},{7,5},{8,10},{9,11},{10,... | collective-permute-start | bytes 1179656 | tf_op jit(solution)/shard_map/ppermute | solution.py:108
  266.6 2.3 shard_map.66.refs_0_
  269.0 3.9 %collective-permute-done.36.refs_2_ = bf16[2,128,768]{2,1,0:T(8,128)(2,1)S(1)} collective-permute-done((bf16[2,128,768]{2,1,0:T(8,128)(2,1)S(1)}, bf16[2,128,768]{2,1,0:T(8,128)(2,1)S(1)}, u32[]{:S(2)}, u32[]{:S(2)}) %collective-permute-start.36) | collective-permute-done | bytes 393248 | tf_op jit(solution)/shard_map/ppermute | solution.py:108
  273.0 2.4 collective-permute-start.6
  275.4 2.3 shard_map.68.refs_1_
  277.6 3.7 %collective-permute-done.41.refs_1_ = bf16[2,128,768]{2,1,0:T(8,128)(2,1)S(1)} collective-permute-done((bf16[2,128,768]{2,1,0:T(8,128)(2,1)S(1)}, bf16[2,128,768]{2,1,0:T(8,128)(2,1)S(1)}, u32[]{:S(2)}, u32[]{:S(2)}) %collective-permute-start.41) | collective-permute-done | bytes 393248 | tf_op jit(solution)/shard_map/ppermute | solution.py:108
  282.4 8.5 %collective-permute-done.43.refs_2_ = bf16[2,128,768]{2,1,0:T(8,128)(2,1)S(1)} collective-permute-done((bf16[2,128,768]{2,1,0:T(8,128)(2,1)S(1)}, bf16[2,128,768]{2,1,0:T(8,128)(2,1)S(1)}, u32[]{:S(2)}, u32[]{:S(2)}) %collective-permute-start.43) | collective-permute-done | bytes 393248 | tf_op jit(solution)/shard_map/ppermute | solution.py:108
  290.9 2.1 collective-permute-start.8
  292.9 2.3 shard_map.71.refs_0_
  295.3 5.2 %shard_map.69.refs_12_ = bf16[768,256]{1,0:T(8,128)(2,1)S(1)} custom-call(f32[768,384]{1,0:T(8,128)S(1)} %shard_map.64.total, bf16[768,6144]{1,0:T(8,128)(2,1)} %copy-done, bf16[1,1536,256]{2,1,0:T(8,128)(2,1)S(1)} %collective-permute-done.25.first, bf16[1,1536,256]{2,1,0:T(8,128)(2,1)S(1)} %collective-permute-done.26.second, ...), custom_call_target="tpu_custom_call" | custom-call | flops 1207959552 | bytes 6291456 | tf_op jit(solution)/shard_map/pallas_call | solution.py:325
  300.5 2.3 collective-permute-start.15
  302.9 2.1 collective-permute-start.16
  305.0 2.3 collective-permute-start.23
  307.3 2.1 collective-permute-start.24
  309.4 4.5 %shard_map.72.refs_13_ = bf16[768,128]{1,0:T(8,128)(2,1)S(1)} custom-call(f32[768,384]{1,0:T(8,128)S(1)} %shard_map.64.total, bf16[768,6144]{1,0:T(8,128)(2,1)} %copy-done, bf16[1,1536,128]{2,1,0:T(8,128)(2,1)S(1)} %collective-permute-done.37.first, bf16[1,1536,128]{2,1,0:T(8,128)(2,1)S(1)} %collective-permute-done.38.second, ...), custom_call_target="tpu_custom_call" | custom-call | flops 603979776 | bytes 5505024 | tf_op jit(solution)/shard_map/pallas_call | solution.py:325
  (82 shorter events, 15.2 us)
Async XLA Ops:
  10.0 130.5 %collective-permute-start = (bf16[3,1536,768]{2,1,0:T(8,128)(2,1)}, bf16[3,1536,768]{2,1,0:T(8,128)(2,1)}, u32[]{:S(2)}, u32[]{:S(2)}) collective-permute-start(bf16[3,1536,768]{2,1,0:T(8,128)(2,1)} %bitcast.3.source.refs_1_.refs_0_), channel_id=1, source_target_pairs={{0,8},{8,0},{16,24},{24,16},{1,9},{9,1},{17,25},{25,17},{2,10},{10... | collective-permute-start | bytes 21233672 | tf_op jit(solution)/shard_map/ppermute | solution.py:108
  10.5 29.3 %collective-permute-start.1 = (bf16[3,1536,128]{2,1,0:T(8,128)(2,1)S(1)}, bf16[3,1536,128]{2,1,0:T(8,128)(2,1)S(1)}, u32[]{:S(2)}, u32[]{:S(2)}) collective-permute-start(bf16[3,1536,128]{2,1,0:T(8,128)(2,1)S(1)} %get-tuple-element.41), channel_id=1, source_target_pairs={{0,16},{8,24},{16,0},{24,8},{1,17},{9,25},{17,1},{25,9},{2,18},{10... | collective-permute-start | bytes 3538952 | tf_op jit(solution)/shard_map/ppermute | solution.py:108
  13.0 43.7 %collective-permute-start.27 = (bf16[2,1536,128]{2,1,0:T(8,128)(2,1)S(1)}, bf16[2,1536,128]{2,1,0:T(8,128)(2,1)S(1)}, u32[]{:S(2)}, u32[]{:S(2)}) collective-permute-start(bf16[2,1536,128]{2,1,0:T(8,128)(2,1)S(1)} %slice.4), channel_id=1, source_target_pairs={{0,16},{8,24},{16,0},{24,8},{1,17},{9,25},{17,1},{25,9},{2,18},{10... | collective-permute-start | bytes 2359304 | tf_op jit(solution)/shard_map/ppermute | solution.py:108
  13.0 68.9 %collective-permute-start.9 = (bf16[3,1536,128]{2,1,0:T(8,128)(2,1)S(1)}, bf16[3,1536,128]{2,1,0:T(8,128)(2,1)S(1)}, u32[]{:S(2)}, u32[]{:S(2)}) collective-permute-start(bf16[3,1536,128]{2,1,0:T(8,128)(2,1)S(1)} %get-tuple-element.50), channel_id=1, source_target_pairs={{0,16},{8,24},{16,0},{24,8},{1,17},{9,25},{17,1},{25,9},{2,18},{10... | collective-permute-start | bytes 3538952 | tf_op jit(solution)/shard_map/ppermute | solution.py:108
  15.0 110.7 %collective-permute-start.17 = (bf16[3,1536,128]{2,1,0:T(8,128)(2,1)}, bf16[3,1536,128]{2,1,0:T(8,128)(2,1)S(1)}, u32[]{:S(2)}, u32[]{:S(2)}) collective-permute-start(bf16[3,1536,128]{2,1,0:T(8,128)(2,1)} %get-tuple-element.59), channel_id=1, source_target_pairs={{0,16},{8,24},{16,0},{24,8},{1,17},{9,25},{17,1},{25,9},{2,18},{10... | collective-permute-start | bytes 3538952 | tf_op jit(solution)/shard_map/ppermute | solution.py:108
  39.8 85.9 %collective-permute-start.2 = (bf16[3,1536,128]{2,1,0:T(8,128)(2,1)S(1)}, bf16[3,1536,128]{2,1,0:T(8,128)(2,1)}, u32[]{:S(2)}, u32[]{:S(2)}) collective-permute-start(bf16[3,1536,128]{2,1,0:T(8,128)(2,1)S(1)} %collective-permute-done.1.refs_3_), channel_id=1, source_target_pairs={{0,8},{8,0},{16,24},{24,16},{1,9},{9,1},{17,25},{25,17},{2,10},{10... | collective-permute-start | bytes 3538952 | tf_op jit(solution)/shard_map/ppermute | solution.py:108
  56.7 25.3 %copy-start.1 = (bf16[2,1536,128]{2,1,0:T(8,128)(2,1)}, bf16[2,1536,128]{2,1,0:T(8,128)(2,1)S(1)}, u32[]{:S(2)}) copy-start(bf16[2,1536,128]{2,1,0:T(8,128)(2,1)S(1)} %collective-permute-done.27.refs_3_) | copy-start | bytes 2359300
  56.7 67.3 %collective-permute-start.32 = (bf16[2,1536,128]{2,1,0:T(8,128)(2,1)}, bf16[2,1536,128]{2,1,0:T(8,128)(2,1)}, u32[]{:S(2)}, u32[]{:S(2)}) collective-permute-start(bf16[2,1536,128]{2,1,0:T(8,128)(2,1)} %get-tuple-element.39), channel_id=1, source_target_pairs={{0,16},{8,24},{16,0},{24,8},{1,17},{9,25},{17,1},{25,9},{2,18},{10... | collective-permute-start | bytes 2359304 | tf_op jit(solution)/shard_map/ppermute | solution.py:108
  81.9 74.4 %collective-permute-start.10 = (bf16[3,1536,128]{2,1,0:T(8,128)(2,1)S(1)}, bf16[3,1536,128]{2,1,0:T(8,128)(2,1)}, u32[]{:S(2)}, u32[]{:S(2)}) collective-permute-start(bf16[3,1536,128]{2,1,0:T(8,128)(2,1)S(1)} %collective-permute-done.9.refs_3_), channel_id=1, source_target_pairs={{0,8},{8,0},{16,24},{24,16},{1,9},{9,1},{17,25},{25,17},{2,10},{10... | collective-permute-start | bytes 3538952 | tf_op jit(solution)/shard_map/ppermute | solution.py:108
  124.0 25.2 %collective-permute-start.39 = (bf16[2,1536,128]{2,1,0:T(8,128)(2,1)}, bf16[2,1536,128]{2,1,0:T(8,128)(2,1)}, u32[]{:S(2)}, u32[]{:S(2)}) collective-permute-start(bf16[2,1536,128]{2,1,0:T(8,128)(2,1)} %copy-done.4), channel_id=1, source_target_pairs={{0,16},{8,24},{16,0},{24,8},{1,17},{9,25},{17,1},{25,9},{2,18},{10... | collective-permute-start | bytes 2359304 | tf_op jit(solution)/shard_map/ppermute | solution.py:108
  125.7 23.5 %collective-permute-start.28 = (bf16[2,1536,128]{2,1,0:T(8,128)(2,1)}, bf16[2,1536,128]{2,1,0:T(8,128)(2,1)}, u32[]{:S(2)}, u32[]{:S(2)}) collective-permute-start(bf16[2,1536,128]{2,1,0:T(8,128)(2,1)} %copy-done.1), channel_id=1, source_target_pairs={{0,8},{8,0},{16,24},{24,16},{1,9},{9,1},{17,25},{25,17},{2,10},{10... | collective-permute-start | bytes 2359304 | tf_op jit(solution)/shard_map/ppermute | solution.py:108
  125.8 49.7 %collective-permute-start.18 = (bf16[3,1536,128]{2,1,0:T(8,128)(2,1)S(1)}, bf16[3,1536,128]{2,1,0:T(8,128)(2,1)}, u32[]{:S(2)}, u32[]{:S(2)}) collective-permute-start(bf16[3,1536,128]{2,1,0:T(8,128)(2,1)S(1)} %collective-permute-done.17.refs_1_), channel_id=1, source_target_pairs={{0,8},{8,0},{16,24},{24,16},{1,9},{9,1},{17,25},{25,17},{2,10},{10... | collective-permute-start | bytes 3538952 | tf_op jit(solution)/shard_map/ppermute | solution.py:108
  140.5 32.3 %collective-permute-start.25 = (bf16[1,1536,256]{2,1,0:T(8,128)(2,1)}, bf16[1,1536,256]{2,1,0:T(8,128)(2,1)S(1)}, u32[]{:S(2)}, u32[]{:S(2)}) collective-permute-start(bf16[1,1536,256]{2,1,0:T(8,128)(2,1)} %copy-done.3), channel_id=1, source_target_pairs={{0,16},{8,24},{16,0},{24,8},{1,17},{9,25},{17,1},{25,9},{2,18},{10... | collective-permute-start | bytes 2359304 | tf_op jit(solution)/shard_map/ppermute | solution.py:108
  140.8 8.9 %copy-start.2 = (bf16[2,1536,128]{2,1,0:T(8,128)(2,1)S(1)}, bf16[2,1536,128]{2,1,0:T(8,128)(2,1)}, u32[]{:S(2)}) copy-start(bf16[2,1536,128]{2,1,0:T(8,128)(2,1)} %copy-done.1) | copy-start | bytes 2359300
  149.2 31.3 %collective-permute-start.33 = (bf16[2,1536,128]{2,1,0:T(8,128)(2,1)}, bf16[2,1536,128]{2,1,0:T(8,128)(2,1)S(1)}, u32[]{:S(2)}, u32[]{:S(2)}) collective-permute-start(bf16[2,1536,128]{2,1,0:T(8,128)(2,1)} %collective-permute-done.32.refs_3_), channel_id=1, source_target_pairs={{0,8},{8,0},{16,24},{24,16},{1,9},{9,1},{17,25},{25,17},{2,10},{10... | collective-permute-start | bytes 2359304 | tf_op jit(solution)/shard_map/ppermute | solution.py:108
  149.3 31.9 %collective-permute-start.40 = (bf16[2,1536,128]{2,1,0:T(8,128)(2,1)}, bf16[2,1536,128]{2,1,0:T(8,128)(2,1)S(1)}, u32[]{:S(2)}, u32[]{:S(2)}) collective-permute-start(bf16[2,1536,128]{2,1,0:T(8,128)(2,1)} %collective-permute-done.39.refs_3_), channel_id=1, source_target_pairs={{0,8},{8,0},{16,24},{24,16},{1,9},{9,1},{17,25},{25,17},{2,10},{10... | collective-permute-start | bytes 2359304 | tf_op jit(solution)/shard_map/ppermute | solution.py:108
  156.3 14.8 %collective-permute-start.37 = (bf16[1,1536,128]{2,1,0:T(8,128)(2,1)S(1)}, bf16[1,1536,128]{2,1,0:T(8,128)(2,1)S(1)}, u32[]{:S(2)}, u32[]{:S(2)}) collective-permute-start(bf16[1,1536,128]{2,1,0:T(8,128)(2,1)S(1)} %copy-done.6), channel_id=1, source_target_pairs={{0,16},{8,24},{16,0},{24,8},{1,17},{9,25},{17,1},{25,9},{2,18},{10... | collective-permute-start | bytes 1179656 | tf_op jit(solution)/shard_map/ppermute | solution.py:108
  171.2 13.5 %collective-permute-start.3 = (bf16[3,32,768]{2,1,0:T(8,128)(2,1)S(1)}, bf16[3,32,768]{2,1,0:T(8,128)(2,1)S(1)}, u32[]{:S(2)}, u32[]{:S(2)}) collective-permute-start(bf16[3,32,768]{2,1,0:T(8,128)(2,1)S(1)} %get-tuple-element.43), channel_id=1, source_target_pairs={{0,2},{1,3},{2,0},{3,1},{4,6},{5,7},{6,4},{7,5},{8,10},{9,11},{10,... | collective-permute-start | bytes 442376 | tf_op jit(solution)/shard_map/ppermute | solution.py:108
  172.8 14.0 %collective-permute-start.4 = (bf16[3,32,768]{2,1,0:T(8,128)(2,1)S(1)}, bf16[3,32,768]{2,1,0:T(8,128)(2,1)S(1)}, u32[]{:S(2)}, u32[]{:S(2)}) collective-permute-start(bf16[3,32,768]{2,1,0:T(8,128)(2,1)S(1)} %get-tuple-element.44), channel_id=1, source_target_pairs={{0,4},{1,5},{2,6},{3,7},{4,0},{5,1},{6,2},{7,3},{8,12},{9,13},{10,... | collective-permute-start | bytes 442376 | tf_op jit(solution)/shard_map/ppermute | solution.py:108
  175.4 11.4 %collective-permute-start.5 = (bf16[3,32,768]{2,1,0:T(8,128)(2,1)S(1)}, bf16[3,32,768]{2,1,0:T(8,128)(2,1)S(1)}, u32[]{:S(2)}, u32[]{:S(2)}) collective-permute-start(bf16[3,32,768]{2,1,0:T(8,128)(2,1)S(1)} %get-tuple-element.45), channel_id=1, source_target_pairs={{0,6},{1,7},{2,4},{3,5},{4,2},{5,3},{6,0},{7,1},{8,14},{9,15},{10,... | collective-permute-start | bytes 442376 | tf_op jit(solution)/shard_map/ppermute | solution.py:108
  180.5 15.3 %collective-permute-start.11 = (bf16[3,32,768]{2,1,0:T(8,128)(2,1)S(1)}, bf16[3,32,768]{2,1,0:T(8,128)(2,1)S(1)}, u32[]{:S(2)}, u32[]{:S(2)}) collective-permute-start(bf16[3,32,768]{2,1,0:T(8,128)(2,1)S(1)} %get-tuple-element.52), channel_id=1, source_target_pairs={{0,2},{1,3},{2,0},{3,1},{4,6},{5,7},{6,4},{7,5},{8,10},{9,11},{10,... | collective-permute-start | bytes 442376 | tf_op jit(solution)/shard_map/ppermute | solution.py:108
  181.2 26.6 %collective-permute-start.12 = (bf16[3,32,768]{2,1,0:T(8,128)(2,1)S(1)}, bf16[3,32,768]{2,1,0:T(8,128)(2,1)S(1)}, u32[]{:S(2)}, u32[]{:S(2)}) collective-permute-start(bf16[3,32,768]{2,1,0:T(8,128)(2,1)S(1)} %get-tuple-element.53), channel_id=1, source_target_pairs={{0,4},{1,5},{2,6},{3,7},{4,0},{5,1},{6,2},{7,3},{8,12},{9,13},{10,... | collective-permute-start | bytes 442376 | tf_op jit(solution)/shard_map/ppermute | solution.py:108
  184.7 23.2 %collective-permute-start.13 = (bf16[3,32,768]{2,1,0:T(8,128)(2,1)S(1)}, bf16[3,32,768]{2,1,0:T(8,128)(2,1)S(1)}, u32[]{:S(2)}, u32[]{:S(2)}) collective-permute-start(bf16[3,32,768]{2,1,0:T(8,128)(2,1)S(1)} %get-tuple-element.54), channel_id=1, source_target_pairs={{0,6},{1,7},{2,4},{3,5},{4,2},{5,3},{6,0},{7,1},{8,14},{9,15},{10,... | collective-permute-start | bytes 442376 | tf_op jit(solution)/shard_map/ppermute | solution.py:108
  186.8 23.4 %collective-permute-start.19 = (bf16[3,32,768]{2,1,0:T(8,128)(2,1)S(1)}, bf16[3,32,768]{2,1,0:T(8,128)(2,1)S(1)}, u32[]{:S(2)}, u32[]{:S(2)}) collective-permute-start(bf16[3,32,768]{2,1,0:T(8,128)(2,1)S(1)} %get-tuple-element.61), channel_id=1, source_target_pairs={{0,2},{1,3},{2,0},{3,1},{4,6},{5,7},{6,4},{7,5},{8,10},{9,11},{10,... | collective-permute-start | bytes 442376 | tf_op jit(solution)/shard_map/ppermute | solution.py:108
  186.8 52.8 %collective-permute-start.30 = (bf16[2,128,768]{2,1,0:T(8,128)(2,1)S(1)}, bf16[2,128,768]{2,1,0:T(8,128)(2,1)S(1)}, u32[]{:S(2)}, u32[]{:S(2)}) collective-permute-start(bf16[2,128,768]{2,1,0:T(8,128)(2,1)S(1)} %shard_map.65.refs_0_), channel_id=1, source_target_pairs={{0,6},{1,7},{2,4},{3,5},{4,2},{5,3},{6,0},{7,1},{8,14},{9,15},{10,... | collective-permute-start | bytes 1179656 | tf_op jit(solution)/shard_map/ppermute | solution.py:108
  195.7 48.7 %collective-permute-start.29 = (bf16[2,128,768]{2,1,0:T(8,128)(2,1)S(1)}, bf16[2,128,768]{2,1,0:T(8,128)(2,1)S(1)}, u32[]{:S(2)}, u32[]{:S(2)}) collective-permute-start(bf16[2,128,768]{2,1,0:T(8,128)(2,1)S(1)} %shard_map.65.refs_0_), channel_id=1, source_target_pairs={{0,2},{1,3},{2,0},{3,1},{4,6},{5,7},{6,4},{7,5},{8,10},{9,11},{10,... | collective-permute-start | bytes 1179656 | tf_op jit(solution)/shard_map/ppermute | solution.py:108
  207.9 29.5 %collective-permute-start.20 = (bf16[3,32,768]{2,1,0:T(8,128)(2,1)S(1)}, bf16[3,32,768]{2,1,0:T(8,128)(2,1)S(1)}, u32[]{:S(2)}, u32[]{:S(2)}) collective-permute-start(bf16[3,32,768]{2,1,0:T(8,128)(2,1)S(1)} %get-tuple-element.62), channel_id=1, source_target_pairs={{0,4},{1,5},{2,6},{3,7},{4,0},{5,1},{6,2},{7,3},{8,12},{9,13},{10,... | collective-permute-start | bytes 442376 | tf_op jit(solution)/shard_map/ppermute | solution.py:108
  207.9 31.8 %collective-permute-start.21 = (bf16[3,32,768]{2,1,0:T(8,128)(2,1)S(1)}, bf16[3,32,768]{2,1,0:T(8,128)(2,1)S(1)}, u32[]{:S(2)}, u32[]{:S(2)}) collective-permute-start(bf16[3,32,768]{2,1,0:T(8,128)(2,1)S(1)} %get-tuple-element.63), channel_id=1, source_target_pairs={{0,6},{1,7},{2,4},{3,5},{4,2},{5,3},{6,0},{7,1},{8,14},{9,15},{10,... | collective-permute-start | bytes 442376 | tf_op jit(solution)/shard_map/ppermute | solution.py:108
  210.1 42.0 %collective-permute-start.35 = (bf16[2,128,768]{2,1,0:T(8,128)(2,1)S(1)}, bf16[2,128,768]{2,1,0:T(8,128)(2,1)S(1)}, u32[]{:S(2)}, u32[]{:S(2)}) collective-permute-start(bf16[2,128,768]{2,1,0:T(8,128)(2,1)S(1)} %shard_map.67.refs_0_), channel_id=1, source_target_pairs={{0,6},{1,7},{2,4},{3,5},{4,2},{5,3},{6,0},{7,1},{8,14},{9,15},{10,... | collective-permute-start | bytes 1179656 | tf_op jit(solution)/shard_map/ppermute | solution.py:108
  218.2 39.7 %copy-start.8 = (f32[128]{0:T(128)S(1)}, f32[128]{0:T(128)}, u32[]{:S(2)}) copy-start(f32[128]{0:T(128)} %param.8) | copy-start | bytes 1540
  218.2 39.8 %copy-start.9 = (f32[128]{0:T(128)S(1)}, f32[128]{0:T(128)}, u32[]{:S(2)}) copy-start(f32[128]{0:T(128)} %param.9) | copy-start | bytes 1540
  237.3 24.1 %collective-permute-start.42 = (bf16[2,128,768]{2,1,0:T(8,128)(2,1)S(1)}, bf16[2,128,768]{2,1,0:T(8,128)(2,1)S(1)}, u32[]{:S(2)}, u32[]{:S(2)}) collective-permute-start(bf16[2,128,768]{2,1,0:T(8,128)(2,1)S(1)} %shard_map.70.refs_0_), channel_id=1, source_target_pairs={{0,6},{1,7},{2,4},{3,5},{4,2},{5,3},{6,0},{7,1},{8,14},{9,15},{10,... | collective-permute-start | bytes 1179656 | tf_op jit(solution)/shard_map/ppermute | solution.py:108
  239.6 25.3 %collective-permute-start.31 = (bf16[2,128,768]{2,1,0:T(8,128)(2,1)S(1)}, bf16[2,128,768]{2,1,0:T(8,128)(2,1)S(1)}, u32[]{:S(2)}, u32[]{:S(2)}) collective-permute-start(bf16[2,128,768]{2,1,0:T(8,128)(2,1)S(1)} %collective-permute-done.30.refs_3_), channel_id=1, source_target_pairs={{0,2},{1,3},{2,0},{3,1},{4,6},{5,7},{6,4},{7,5},{8,10},{9,11},{10,... | collective-permute-start | bytes 1179656 | tf_op jit(solution)/shard_map/ppermute | solution.py:108
  239.6 55.6 %collective-permute-start.26 = (bf16[1,1536,256]{2,1,0:T(8,128)(2,1)S(1)}, bf16[1,1536,256]{2,1,0:T(8,128)(2,1)S(1)}, u32[]{:S(2)}, u32[]{:S(2)}) collective-permute-start(bf16[1,1536,256]{2,1,0:T(8,128)(2,1)S(1)} %collective-permute-done.25.first), channel_id=1, source_target_pairs={{0,8},{8,0},{16,24},{24,16},{1,9},{9,1},{17,25},{25,17},{2,10},{10... | collective-permute-start | bytes 2359304 | tf_op jit(solution)/shard_map/ppermute | solution.py:108
  244.4 24.5 %collective-permute-start.34 = (bf16[2,128,768]{2,1,0:T(8,128)(2,1)S(1)}, bf16[2,128,768]{2,1,0:T(8,128)(2,1)S(1)}, u32[]{:S(2)}, u32[]{:S(2)}) collective-permute-start(bf16[2,128,768]{2,1,0:T(8,128)(2,1)S(1)} %shard_map.67.refs_0_), channel_id=1, source_target_pairs={{0,2},{1,3},{2,0},{3,1},{4,6},{5,7},{6,4},{7,5},{8,10},{9,11},{10,... | collective-permute-start | bytes 1179656 | tf_op jit(solution)/shard_map/ppermute | solution.py:108
  252.1 20.8 %collective-permute-start.36 = (bf16[2,128,768]{2,1,0:T(8,128)(2,1)S(1)}, bf16[2,128,768]{2,1,0:T(8,128)(2,1)S(1)}, u32[]{:S(2)}, u32[]{:S(2)}) collective-permute-start(bf16[2,128,768]{2,1,0:T(8,128)(2,1)S(1)} %collective-permute-done.35.refs_3_), channel_id=1, source_target_pairs={{0,2},{1,3},{2,0},{3,1},{4,6},{5,7},{6,4},{7,5},{8,10},{9,11},{10,... | collective-permute-start | bytes 1179656 | tf_op jit(solution)/shard_map/ppermute | solution.py:108
  261.5 19.9 %collective-permute-start.41 = (bf16[2,128,768]{2,1,0:T(8,128)(2,1)S(1)}, bf16[2,128,768]{2,1,0:T(8,128)(2,1)S(1)}, u32[]{:S(2)}, u32[]{:S(2)}) collective-permute-start(bf16[2,128,768]{2,1,0:T(8,128)(2,1)S(1)} %shard_map.70.refs_0_), channel_id=1, source_target_pairs={{0,2},{1,3},{2,0},{3,1},{4,6},{5,7},{6,4},{7,5},{8,10},{9,11},{10,... | collective-permute-start | bytes 1179656 | tf_op jit(solution)/shard_map/ppermute | solution.py:108
  265.0 25.9 %collective-permute-start.43 = (bf16[2,128,768]{2,1,0:T(8,128)(2,1)S(1)}, bf16[2,128,768]{2,1,0:T(8,128)(2,1)S(1)}, u32[]{:S(2)}, u32[]{:S(2)}) collective-permute-start(bf16[2,128,768]{2,1,0:T(8,128)(2,1)S(1)} %collective-permute-done.42.refs_3_), channel_id=1, source_target_pairs={{0,2},{1,3},{2,0},{3,1},{4,6},{5,7},{6,4},{7,5},{8,10},{9,11},{10,... | collective-permute-start | bytes 1179656 | tf_op jit(solution)/shard_map/ppermute | solution.py:108
  268.9 31.6 %collective-permute-start.38 = (bf16[1,1536,128]{2,1,0:T(8,128)(2,1)S(1)}, bf16[1,1536,128]{2,1,0:T(8,128)(2,1)S(1)}, u32[]{:S(2)}, u32[]{:S(2)}) collective-permute-start(bf16[1,1536,128]{2,1,0:T(8,128)(2,1)S(1)} %collective-permute-done.37.first), channel_id=1, source_target_pairs={{0,8},{8,0},{16,24},{24,16},{1,9},{9,1},{17,25},{25,17},{2,10},{10... | collective-permute-start | bytes 1179656 | tf_op jit(solution)/shard_map/ppermute | solution.py:108
  273.0 29.9 %collective-permute-start.6 = (bf16[32,768]{1,0:T(8,128)(2,1)S(1)}, bf16[32,768]{1,0:T(8,128)(2,1)S(1)}, u32[]{:S(2)}, u32[]{:S(2)}) collective-permute-start(bf16[32,768]{1,0:T(8,128)(2,1)S(1)} %get-tuple-element.47), channel_id=1, source_target_pairs={{0,2},{1,3},{2,0},{3,1},{4,6},{5,7},{6,4},{7,5},{8,10},{9,11},{10,... | collective-permute-start | bytes 147464 | tf_op jit(solution)/shard_map/ppermute | solution.py:108
  281.4 23.6 %collective-permute-start.7 = (bf16[32,768]{1,0:T(8,128)(2,1)S(1)}, bf16[32,768]{1,0:T(8,128)(2,1)S(1)}, u32[]{:S(2)}, u32[]{:S(2)}) collective-permute-start(bf16[32,768]{1,0:T(8,128)(2,1)S(1)} %get-tuple-element.48), channel_id=1, source_target_pairs={{0,4},{1,5},{2,6},{3,7},{4,0},{5,1},{6,2},{7,3},{8,12},{9,13},{10,... | collective-permute-start | bytes 147464 | tf_op jit(solution)/shard_map/ppermute | solution.py:108
  290.9 14.1 %collective-permute-start.8 = (bf16[32,768]{1,0:T(8,128)(2,1)S(1)}, bf16[32,768]{1,0:T(8,128)(2,1)S(1)}, u32[]{:S(2)}, u32[]{:S(2)}) collective-permute-start(bf16[32,768]{1,0:T(8,128)(2,1)S(1)} %get-tuple-element.49), channel_id=1, source_target_pairs={{0,6},{1,7},{2,4},{3,5},{4,2},{5,3},{6,0},{7,1},{8,14},{9,15},{10,... | collective-permute-start | bytes 147464 | tf_op jit(solution)/shard_map/ppermute | solution.py:108
  295.2 12.1 %collective-permute-start.14 = (bf16[32,768]{1,0:T(8,128)(2,1)S(1)}, bf16[32,768]{1,0:T(8,128)(2,1)S(1)}, u32[]{:S(2)}, u32[]{:S(2)}) collective-permute-start(bf16[32,768]{1,0:T(8,128)(2,1)S(1)} %get-tuple-element.56), channel_id=1, source_target_pairs={{0,2},{1,3},{2,0},{3,1},{4,6},{5,7},{6,4},{7,5},{8,10},{9,11},{10,... | collective-permute-start | bytes 147464 | tf_op jit(solution)/shard_map/ppermute | solution.py:108
  300.5 13.3 %collective-permute-start.15 = (bf16[32,768]{1,0:T(8,128)(2,1)S(1)}, bf16[32,768]{1,0:T(8,128)(2,1)S(1)}, u32[]{:S(2)}, u32[]{:S(2)}) collective-permute-start(bf16[32,768]{1,0:T(8,128)(2,1)S(1)} %get-tuple-element.57), channel_id=1, source_target_pairs={{0,4},{1,5},{2,6},{3,7},{4,0},{5,1},{6,2},{7,3},{8,12},{9,13},{10,... | collective-permute-start | bytes 147464 | tf_op jit(solution)/shard_map/ppermute | solution.py:108
  302.9 11.0 %collective-permute-start.16 = (bf16[32,768]{1,0:T(8,128)(2,1)S(1)}, bf16[32,768]{1,0:T(8,128)(2,1)S(1)}, u32[]{:S(2)}, u32[]{:S(2)}) collective-permute-start(bf16[32,768]{1,0:T(8,128)(2,1)S(1)} %get-tuple-element.58), channel_id=1, source_target_pairs={{0,6},{1,7},{2,4},{3,5},{4,2},{5,3},{6,0},{7,1},{8,14},{9,15},{10,... | collective-permute-start | bytes 147464 | tf_op jit(solution)/shard_map/ppermute | solution.py:108
  305.0 8.9 %collective-permute-start.22 = (bf16[32,768]{1,0:T(8,128)(2,1)S(1)}, bf16[32,768]{1,0:T(8,128)(2,1)S(1)}, u32[]{:S(2)}, u32[]{:S(2)}) collective-permute-start(bf16[32,768]{1,0:T(8,128)(2,1)S(1)} %get-tuple-element.65), channel_id=1, source_target_pairs={{0,2},{1,3},{2,0},{3,1},{4,6},{5,7},{6,4},{7,5},{8,10},{9,11},{10,... | collective-permute-start | bytes 147464 | tf_op jit(solution)/shard_map/ppermute | solution.py:108
  305.0 8.9 %collective-permute-start.23 = (bf16[32,768]{1,0:T(8,128)(2,1)S(1)}, bf16[32,768]{1,0:T(8,128)(2,1)S(1)}, u32[]{:S(2)}, u32[]{:S(2)}) collective-permute-start(bf16[32,768]{1,0:T(8,128)(2,1)S(1)} %get-tuple-element.66), channel_id=1, source_target_pairs={{0,4},{1,5},{2,6},{3,7},{4,0},{5,1},{6,2},{7,3},{8,12},{9,13},{10,... | collective-permute-start | bytes 147464 | tf_op jit(solution)/shard_map/ppermute | solution.py:108
  307.3 6.6 %collective-permute-start.24 = (bf16[32,768]{1,0:T(8,128)(2,1)S(1)}, bf16[32,768]{1,0:T(8,128)(2,1)S(1)}, u32[]{:S(2)}, u32[]{:S(2)}) collective-permute-start(bf16[32,768]{1,0:T(8,128)(2,1)S(1)} %get-tuple-element.67), channel_id=1, source_target_pairs={{0,6},{1,7},{2,4},{3,5},{4,2},{5,3},{6,0},{7,1},{8,14},{9,15},{10,... | collective-permute-start | bytes 147464 | tf_op jit(solution)/shard_map/ppermute | solution.py:108
  (6 other events, 14.1 us)
